TPU v7x, 32 devices: a whole 2x2x4 slice. The times are simulated.
32 devices in a mesh: region: 8 (over z, y), blk: 4 (over x, core).
Axes of the slice: x: 2, y: 2, z: 4, core: 2. Of those that a mesh axis runs over, the one named last changes fastest.
Arguments:
- jac_bus: float32 [256, 8, 128, 128], P('region', 'blk'), may hold values from -0.1875 to 0.1875
- pattern: int32 [256, 8], P(('region', 'blk')), may hold values from 0 to 23
- branch_weight: float32 [256, 128], P(('region', 'blk')), may hold values from 0.2 to 5
- bus_diag: float32 [256, 128], P(('region', 'blk')), may hold values from 0.3 to 3
- right_side: float32 [256, 128], P(('region', 'blk')), may hold values from -8 to 8
Outputs:
- solution: float32 [256, 128], P(('region', 'blk'))
- residual: float32 [256, 128], P(('region', 'blk'))
Inputs may be any that keep to these rules, and one draw needn't show every extreme that they name: pattern values below 8 name the region before the branch tile's region, those from 16 the region after it, with regions closed into a loop.
All inputs are finite; a program needn't handle non-finite values.
Results may differ from a plain program's by a relative error of at most 0.0003.
Values sent between devices are 32-bit elements; how exact they have to be, the bound alone decides.
No kernel may reach another device: no remote copies, remote signals or barrier semaphores. Data moves between devices by JAX's collectives and lax.ppermute only.
A program may use at most 64 MiB of HBM per device.

v0:
```python
import jax
import jax.numpy as jnp
from jax import lax
from jax.sharding import PartitionSpec as P

ITERS = 12


def extended(array, sides, width):
    for axis, dim in sides:
        size, length = (lax.axis_size(axis), array.shape[dim])
        up = [(i, (i + 1) % size) for i in range(size)]
        down = [(j, i) for i, j in up]
        last = lax.slice_in_dim(array, length - width, length, axis=dim)
        leading = lax.slice_in_dim(array, 0, width, axis=dim)
        before = lax.ppermute(last, axis, up)
        after = lax.ppermute(leading, axis, down)
        array = jnp.concatenate([before, array, after], axis=dim)
    return array


def from_behind(array, axis, by):
    length = lax.axis_size(axis)
    return lax.ppermute(array, axis, [(i, (i + by) % length) for i in range(length)])


def neighbours(values):
    return extended(values[None], (("region", 0),), 1)


def route(lower, middle, upper):
    from_upper = from_behind(lower, "region", -1)
    from_lower = from_behind(upper, "region", 1)
    return middle + from_upper + from_lower


def spread(tiles, weight, index, count):
    back = jnp.einsum("tjab,ta->tjb", tiles, weight, precision=lax.Precision.HIGHEST)
    width = back.shape[-1]
    return jnp.zeros((count, width), jnp.float32).at[index.reshape(-1)].add(back.reshape(-1, width))


def body(jac_bus, pattern, branch_weight, bus_diag, right_side):
    hp = lax.Precision.HIGHEST
    blocks = lax.axis_size("blk")
    per_dev = right_side.shape[0]
    width = right_side.shape[1]
    group_len = jac_bus.shape[1]
    tiles = lax.all_to_all(jac_bus, "blk", split_axis=0, concat_axis=1, tiled=True)
    group = jnp.arange(tiles.shape[1], dtype=jnp.int32) // group_len
    index = pattern // per_dev * (blocks * per_dev) + group[None, :] * per_dev + pattern % per_dev

    def collect(buffer):
        parts = buffer.reshape(3, blocks, per_dev, width)
        total = route(parts[0], parts[1], parts[2])
        return lax.psum_scatter(total, "blk", scatter_dimension=0, tiled=True)[0]

    def branch_rows(vector):
        region_vals = lax.all_gather(vector[None], "blk", axis=0, tiled=True)
        flat = neighbours(region_vals).reshape(-1, width)
        return jnp.einsum("tjab,tjb->ta", tiles, flat[index], precision=hp)

    count = 3 * blocks * per_dev

    def apply_operator(vector):
        rows = branch_rows(vector)
        return bus_diag * vector + collect(spread(tiles, branch_weight * rows, index, count))

    precond = bus_diag + collect(spread(tiles * tiles, branch_weight, index, count))
    solution = jnp.zeros_like(right_side)
    residual = right_side

    def paired(resid):
        scaled = resid / precond
        image = apply_operator(scaled)
        gamma, delta = lax.psum(
            (jnp.sum(resid * scaled), jnp.sum(image * scaled)), ("region", "blk")
        )
        return (scaled, image, gamma, delta)

    scaled, image, gamma, delta = paired(residual)
    alpha = gamma / delta
    direction, along = (scaled, image)
    solution = alpha * direction
    residual = residual - alpha * along

    def one_step(step, carry):
        solution, residual, direction, along, gamma, alpha = carry
        scaled, image, fresh, delta = paired(residual)
        beta = fresh / gamma
        alpha = fresh / (delta - beta * fresh / alpha)
        direction = scaled + beta * direction
        along = image + beta * along
        solution = solution + alpha * direction
        residual = residual - alpha * along
        return (solution, residual, direction, along, fresh, alpha)

    carry = lax.fori_loop(
        0, ITERS - 1, one_step, (solution, residual, direction, along, gamma, alpha)
    )
    solution, residual = (carry[0], carry[1])
    return (solution, residual)


def solution(mesh):
    return jax.shard_map(
        body,
        mesh=mesh,
        in_specs=(
            P("region", "blk", None, None),
            P(("region", "blk"), None),
            P(("region", "blk"), None),
            P(("region", "blk"), None),
            P(("region", "blk"), None),
        ),
        out_specs=(P(("region", "blk"), None), P(("region", "blk"), None)),
        check_vma=False,
    )
```

profile of v0, /device:TPU:0, one launch (start us, length us, event | category | flops | bytes accessed | tf_op | source)
XLA Modules:
  0.0 1099.3 jit_solution(10616008818148607382)
XLA Ops:
  5.6 48.7 %all-to-all-done = f32[32,2,128,128]{3,2,1,0:T(8,128)} async-done(((f32[32,2,128,128]{3,2,1,0:T(8,128)}), f32[32,2,128,128]{3,2,1,0:T(8,128)}, u32[]{:S(2)}, u32[]{:S(2)}) %all-to-all-start) | async-done | bytes 4194336 | tf_op jit(solution)/shard_map/all_to_all | solution.py:49
  62.0 5.4 collective-permute-start.4
  68.9 5.0 collective-permute-done.5
  73.9 10.1 all-reduce.1
  84.6 5.2 all-gather.1
  96.9 5.4 fusion.33
  111.4 5.0 collective-permute-done.9
  116.4 10.1 all-reduce.2
  127.8 37.2 %all-reduce.4 = (f32[]{:T(128)}, f32[]{:T(128)}) all-reduce(f32[]{:T(128)} %get-tuple-element.70, f32[]{:T(128)} %get-tuple-element.69), channel_id=1, replica_groups=mesh['region'=8,'blk'=4] {'region','blk'}, use_global_device_ids=true, to_apply=%region_3.4 | all-reduce | flops 2 | bytes 16 | tf_op jit(solution)/shard_map/psum | solution.py:76
  166.3 932.4 %while.21 = (s32[]{:T(128)}, f32[8,128]{1,0:T(8,128)S(1)}, f32[8,128]{1,0:T(8,128)S(1)}, f32[8,128]{1,0:T(8,128)S(1)}, f32[8,128]{1,0:T(8,128)S(1)}, /*index=5*/...) while((s32[]{:T(128)}, f32[8,128]{1,0:T(8,128)S(1)}, ...), condition=%wide.wide.region_15.16_spmd, body=%wide.wide.region_8.15_spmd.sunk | while | flops 25230720 | bytes 25991660 | solution.py:98
  166.3 5.5 all-gather.4
  177.2 5.0 collective-permute-done.1
  182.8 5.4 fusion.68
  197.6 10.2 all-reduce.9
  209.1 39.3 %all-reduce.10 = (f32[]{:T(128)}, f32[]{:T(128)}) all-reduce(f32[]{:T(128)} %get-tuple-element.267, f32[]{:T(128)} %get-tuple-element.268), channel_id=1, replica_groups=mesh['region'=8,'blk'=4] {'region','blk'}, use_global_device_ids=true, to_apply=%region_10.10 | all-reduce | flops 2 | bytes 16 | tf_op jit(solution)/shard_map/while/body/eval_jaxpr/psum | solution.py:76
  251.3 5.5 all-gather.4
  261.4 5.0 collective-permute-done.1
  267.0 5.4 fusion.68
  281.8 10.1 all-reduce.9
  293.2 40.4 %all-reduce.10 = (f32[]{:T(128)}, f32[]{:T(128)}) all-reduce(f32[]{:T(128)} %get-tuple-element.267, f32[]{:T(128)} %get-tuple-element.268), channel_id=1, replica_groups=mesh['region'=8,'blk'=4] {'region','blk'}, use_global_device_ids=true, to_apply=%region_10.10 | all-reduce | flops 2 | bytes 16 | tf_op jit(solution)/shard_map/while/body/eval_jaxpr/psum | solution.py:76
  336.6 5.5 all-gather.4
  346.6 5.0 collective-permute-done.1
  352.2 5.4 fusion.68
  367.1 10.2 all-reduce.9
  378.6 39.3 %all-reduce.10 = (f32[]{:T(128)}, f32[]{:T(128)}) all-reduce(f32[]{:T(128)} %get-tuple-element.267, f32[]{:T(128)} %get-tuple-element.268), channel_id=1, replica_groups=mesh['region'=8,'blk'=4] {'region','blk'}, use_global_device_ids=true, to_apply=%region_10.10 | all-reduce | flops 2 | bytes 16 | tf_op jit(solution)/shard_map/while/body/eval_jaxpr/psum | solution.py:76
  420.8 5.5 all-gather.4
  430.9 5.0 collective-permute-done.1
  436.5 5.4 fusion.68
  451.3 10.1 all-reduce.9
  462.7 40.4 %all-reduce.10 = (f32[]{:T(128)}, f32[]{:T(128)}) all-reduce(f32[]{:T(128)} %get-tuple-element.267, f32[]{:T(128)} %get-tuple-element.268), channel_id=1, replica_groups=mesh['region'=8,'blk'=4] {'region','blk'}, use_global_device_ids=true, to_apply=%region_10.10 | all-reduce | flops 2 | bytes 16 | tf_op jit(solution)/shard_map/while/body/eval_jaxpr/psum | solution.py:76
  506.0 5.5 all-gather.4
  516.1 5.0 collective-permute-done.1
  521.7 5.4 fusion.68
  536.6 10.2 all-reduce.9
  548.0 39.3 %all-reduce.10 = (f32[]{:T(128)}, f32[]{:T(128)}) all-reduce(f32[]{:T(128)} %get-tuple-element.267, f32[]{:T(128)} %get-tuple-element.268), channel_id=1, replica_groups=mesh['region'=8,'blk'=4] {'region','blk'}, use_global_device_ids=true, to_apply=%region_10.10 | all-reduce | flops 2 | bytes 16 | tf_op jit(solution)/shard_map/while/body/eval_jaxpr/psum | solution.py:76
  590.3 5.5 all-gather.4
  600.3 5.0 collective-permute-done.1
  605.9 5.4 fusion.68
  620.8 10.1 all-reduce.9
  632.2 40.4 %all-reduce.10 = (f32[]{:T(128)}, f32[]{:T(128)}) all-reduce(f32[]{:T(128)} %get-tuple-element.267, f32[]{:T(128)} %get-tuple-element.268), channel_id=1, replica_groups=mesh['region'=8,'blk'=4] {'region','blk'}, use_global_device_ids=true, to_apply=%region_10.10 | all-reduce | flops 2 | bytes 16 | tf_op jit(solution)/shard_map/while/body/eval_jaxpr/psum | solution.py:76
  675.5 5.5 all-gather.4
  685.6 5.0 collective-permute-done.1
  691.2 5.4 fusion.68
  706.0 10.2 all-reduce.9
  717.5 39.3 %all-reduce.10 = (f32[]{:T(128)}, f32[]{:T(128)}) all-reduce(f32[]{:T(128)} %get-tuple-element.267, f32[]{:T(128)} %get-tuple-element.268), channel_id=1, replica_groups=mesh['region'=8,'blk'=4] {'region','blk'}, use_global_device_ids=true, to_apply=%region_10.10 | all-reduce | flops 2 | bytes 16 | tf_op jit(solution)/shard_map/while/body/eval_jaxpr/psum | solution.py:76
  759.7 5.5 all-gather.4
  769.8 5.0 collective-permute-done.1
  775.4 5.4 fusion.68
  790.2 10.1 all-reduce.9
  801.7 40.4 %all-reduce.10 = (f32[]{:T(128)}, f32[]{:T(128)}) all-reduce(f32[]{:T(128)} %get-tuple-element.267, f32[]{:T(128)} %get-tuple-element.268), channel_id=1, replica_groups=mesh['region'=8,'blk'=4] {'region','blk'}, use_global_device_ids=true, to_apply=%region_10.10 | all-reduce | flops 2 | bytes 16 | tf_op jit(solution)/shard_map/while/body/eval_jaxpr/psum | solution.py:76
  845.0 5.5 all-gather.4
  855.1 5.0 collective-permute-done.1
  860.7 5.4 fusion.68
  875.5 10.2 all-reduce.9
  887.0 39.3 %all-reduce.10 = (f32[]{:T(128)}, f32[]{:T(128)}) all-reduce(f32[]{:T(128)} %get-tuple-element.267, f32[]{:T(128)} %get-tuple-element.268), channel_id=1, replica_groups=mesh['region'=8,'blk'=4] {'region','blk'}, use_global_device_ids=true, to_apply=%region_10.10 | all-reduce | flops 2 | bytes 16 | tf_op jit(solution)/shard_map/while/body/eval_jaxpr/psum | solution.py:76
  929.2 5.5 all-gather.4
  939.3 5.0 collective-permute-done.1
  944.9 5.4 fusion.68
  959.7 10.1 all-reduce.9
  971.1 40.4 %all-reduce.10 = (f32[]{:T(128)}, f32[]{:T(128)}) all-reduce(f32[]{:T(128)} %get-tuple-element.267, f32[]{:T(128)} %get-tuple-element.268), channel_id=1, replica_groups=mesh['region'=8,'blk'=4] {'region','blk'}, use_global_device_ids=true, to_apply=%region_10.10 | all-reduce | flops 2 | bytes 16 | tf_op jit(solution)/shard_map/while/body/eval_jaxpr/psum | solution.py:76
  1014.5 5.5 all-gather.4
  1030.2 5.4 fusion.68
  1045.0 10.2 all-reduce.9
  1056.5 39.3 %all-reduce.10 = (f32[]{:T(128)}, f32[]{:T(128)}) all-reduce(f32[]{:T(128)} %get-tuple-element.267, f32[]{:T(128)} %get-tuple-element.268), channel_id=1, replica_groups=mesh['region'=8,'blk'=4] {'region','blk'}, use_global_device_ids=true, to_apply=%region_10.10 | all-reduce | flops 2 | bytes 16 | tf_op jit(solution)/shard_map/while/body/eval_jaxpr/psum | solution.py:76
  (316 shorter events, 213.1 us)
Async XLA Ops:
  0.6 53.7 %all-to-all-start = ((f32[32,2,128,128]{3,2,1,0:T(8,128)}), f32[32,2,128,128]{3,2,1,0:T(8,128)}, u32[]{:S(2)}, u32[]{:S(2)}) async-start(f32[32,2,128,128]{3,2,1,0:T(8,128)} %param.7), calls=%async_computation | async-start | bytes 8388608 | tf_op jit(solution)/shard_map/all_to_all | solution.py:49
  56.9 10.6 copy-start.9
  56.9 27.1 %copy-start.4 = (f32[8,128]{1,0:T(8,128)S(1)}, f32[8,128]{1,0:T(8,128)}, u32[]{:S(2)}) copy-start(f32[8,128]{1,0:T(8,128)} %param.10) | copy-start | bytes 12292
  56.9 27.1 %copy-start.7 = (f32[8,128]{1,0:T(8,128)S(1)}, f32[8,128]{1,0:T(8,128)}, u32[]{:S(2)}) copy-start(f32[8,128]{1,0:T(8,128)} %param.11) | copy-start | bytes 12292
  62.0 6.9 collective-permute-start.4
  67.4 6.4 collective-permute-start.5
  89.8 6.4 collective-permute-start.6
  89.8 6.4 collective-permute-start.7
  96.9 5.4 copy-start.1
  105.2 6.2 collective-permute-start.8
  110.0 6.4 collective-permute-start.9
  171.9 5.3 collective-permute-start
  175.7 6.4 collective-permute-start.1
  182.8 5.4 copy-start.2
  191.1 6.5 collective-permute-start.2
  191.2 6.4 collective-permute-start.3
  256.8 4.5 collective-permute-start
  259.9 6.4 collective-permute-start.1
  267.0 5.4 copy-start.2
  275.3 6.5 collective-permute-start.2
  275.4 6.4 collective-permute-start.3
  342.1 4.5 collective-permute-start
  345.2 6.4 collective-permute-start.1
  352.2 5.4 copy-start.2
  360.6 6.5 collective-permute-start.2
  360.6 6.4 collective-permute-start.3
  426.3 4.5 collective-permute-start
  429.4 6.4 collective-permute-start.1
  436.4 5.4 copy-start.2
  444.8 6.5 collective-permute-start.2
  444.9 6.4 collective-permute-start.3
  511.6 4.5 collective-permute-start
  514.7 6.4 collective-permute-start.1
  521.7 5.4 copy-start.2
  530.1 6.5 collective-permute-start.2
  530.1 6.4 collective-permute-start.3
  595.8 4.5 collective-permute-start
  598.9 6.4 collective-permute-start.1
  605.9 5.4 copy-start.2
  614.3 6.5 collective-permute-start.2
  614.3 6.4 collective-permute-start.3
  681.1 4.5 collective-permute-start
  684.2 6.4 collective-permute-start.1
  691.2 5.4 copy-start.2
  699.5 6.5 collective-permute-start.2
  699.6 6.4 collective-permute-start.3
  765.3 4.5 collective-permute-start
  768.4 6.4 collective-permute-start.1
  775.4 5.4 copy-start.2
  783.7 6.5 collective-permute-start.2
  783.8 6.4 collective-permute-start.3
  850.6 4.5 collective-permute-start
  853.6 6.4 collective-permute-start.1
  869.0 6.5 collective-permute-start.2
  869.1 6.4 collective-permute-start.3
  934.8 4.5 collective-permute-start
  937.9 6.4 collective-permute-start.1
  953.2 6.5 collective-permute-start.2
  953.3 6.4 collective-permute-start.3
  1020.0 4.5 collective-permute-start
  1023.1 6.4 collective-permute-start.1
  1030.2 5.4 copy-start.2
  1038.5 6.5 collective-permute-start.2
  1038.6 6.4 collective-permute-start.3
  (7 other events, 23.3 us)
where the time goes:
time: 1100 us
  blocking collectives  673 us (61%)
  waiting for transfers between devices  138 us (13%)
  starting transfers between devices  107 us (10%)
  matrix products  92.2 us (8%)
  other arithmetic  34 us (3%)
  loops' own time  32.4 us (3%)
  local copies, waits for them, and re-layouts  20.5 us (2%)
    psum x12, blocking collectives, paired(): lax.psum((jnp.sum(resid * scaled), jnp.sum(image * scaled)), ('region', '...  475 us
    while x11, blocking collectives  112 us
    all_gather x12, blocking collectives, branch_rows(): region_vals = lax.all_gather(vector[None], 'blk', axis=0, tiled=True)  66.3 us
    dot_general x12, matrix products, branch_rows(): return jnp.einsum('tjab,tjb->ta', tiles, flat[index], precision=hp)  64.8 us
    ppermute x26, starting transfers between devices, from_behind(): lax.ppermute(array, axis, [(i, (i + by) % length) for i in range(length)])  62.7 us
    ppermute x12, waiting for transfers between devices, extended(): before = lax.ppermute(last, axis, up)  56.6 us
    all_to_all x1, waiting for transfers between devices, body(): lax.all_to_all(jac_bus, 'blk', split_axis=0, concat_axis=1, tiled=True)  48.7 us
    ppermute x12, starting transfers between devices, extended(): after = lax.ppermute(leading, axis, down)  39.4 us
  transfers between devices with their start and end apart: 51, of which 39 were waited for; matrix products, arithmetic and copies ran while one was open for 1% of the time, Pallas kernels for 0%

commit v1 on v0

v1 whole, which is shorter than its diff:
```python
import functools
import jax
import jax.numpy as jnp
from jax import lax
from jax.experimental import pallas as pl
from jax.experimental.pallas import tpu as pltpu
from jax.sharding import PartitionSpec as P

ITERS = 12
SUB = 8
VMEM_LIMIT = 16 * 1024 * 1024
BANKS = 4
UNROLL = 8

vmem = pl.BlockSpec(memory_space=pltpu.VMEM)
smem = pl.BlockSpec(memory_space=pltpu.SMEM)


def rows8(ref_value):
    return ref_value.reshape(-1, SUB, ref_value.shape[-1])


def diagonal(width):
    row = lax.broadcasted_iota(jnp.int32, (width, width), 0)
    lane = lax.broadcasted_iota(jnp.int32, (width, width), 1)
    return rows8(row == lane)


def as_column(row, eye):
    spread = jnp.where(eye, row[None], 0.0)
    return jnp.sum(spread, axis=-1, keepdims=True)


def lane_total(value):
    return jnp.sum(jnp.sum(value, axis=0, keepdims=True), axis=1, keepdims=True)


def forward(jac, index, spread, rows):
    tiles, slots, width, _ = jac.shape
    eye = diagonal(width)

    def tile(t, carry):
        total = None
        for j in range(slots):
            term = rows8(jac[t, j]) * spread[index[t * slots + j]][None]
            total = term if total is None else total + term
        total = jnp.sum(total, axis=-1, keepdims=True)
        rows[pl.ds(t, 1), :] = jnp.sum(
            jnp.sum(jnp.where(eye, total, 0.0), axis=0), axis=0, keepdims=True
        )
        return carry

    lax.fori_loop(0, tiles, tile, 0, unroll=UNROLL)


def backward(jac, index, weighted, banks, square):
    tiles, slots, width, _ = jac.shape
    eye = diagonal(width)
    banks[...] = jnp.zeros_like(banks)

    def tile(t, carry):
        column = as_column(weighted[pl.ds(t, 1), :], eye)
        for j in range(slots):
            block = rows8(jac[t, j])
            if square:
                block = block * block
            where = (lax.rem(t * slots + j, BANKS), index[t * slots + j])
            banks[where] += jnp.sum(block * column, axis=0)
        return carry

    lax.fori_loop(0, tiles, tile, 0, unroll=UNROLL)
    total = banks[0]
    for bank in range(1, BANKS):
        total = total + banks[bank]
    return jnp.sum(total, axis=1)


def publish(chunk, out):
    for member in range(out.shape[0]):
        out[member] = chunk


def diag_kernel(index, jac, weight, diag, rhs, out, banks):
    squares = backward(jac, index, weight, banks, True)
    publish(jnp.concatenate([squares, diag[...], rhs[...]], axis=0), out)


def back_kernel(index, jac, weight, own, *refs):
    others, (out, weighted, banks) = refs[:-3], refs[-3:]
    tiles = jac.shape[0]
    parts = [own] + list(others)
    even, odd = None, None
    for shift, part in enumerate(parts):
        if shift % 2 == 0:
            even = part[...] if even is None else even + part[...]
        else:
            odd = part[...] if odd is None else odd + part[...]
    total = even if odd is None else even + odd
    rows, sums = total[:tiles], total[tiles:]
    weighted[...] = weight[...] * rows
    delta = jnp.sum(weighted[...] * rows, axis=0, keepdims=True) + sums[1:2]
    scalars = jnp.concatenate([sums[:1], delta, sums[2:]], axis=0)
    columns = backward(jac, index, weighted, banks, False)
    publish(jnp.concatenate([columns, scalars], axis=0), out)


def send_rows(jac, index, resid, scaled, diag, spread, own, out):
    tiles = jac.shape[0]
    spread[...] = jnp.broadcast_to(scaled[:, None, :], spread.shape)
    forward(jac, index, spread, out)
    r, z, d = resid[own], scaled[own], diag[own]
    gamma = jnp.sum(r * z, axis=0, keepdims=True)
    delta = jnp.sum(d * z * z, axis=0, keepdims=True)
    pad = jnp.zeros((SUB - 2, z.shape[1]), jnp.float32)
    out[tiles:, :] = jnp.concatenate([gamma, delta, pad], axis=0)


def gathered(received, region, regions, per_dev):
    blocks = []
    for offset in (-1, 0, 1):
        total = None
        for e in (-1, 0, 1):
            source = lax.rem(region + (offset + e + regions), regions)
            start = (1 - e) * per_dev
            term = received[source, start : start + per_dev, :]
            total = term if total is None else total + term
        blocks.append(total)
    return jnp.concatenate(blocks, axis=0)


def halo(received, region, regions, start, per_dev):
    blocks = []
    for offset in (-1, 0, 1):
        source = lax.rem(region + (offset + regions), regions)
        blocks.append(received[source, start : start + per_dev, :])
    return jnp.concatenate(blocks, axis=0)


def first_kernel(place, index, jac, received, out, diag, precond, resid, spread):
    regions = received.shape[0]
    per_dev = diag.shape[0] // 3
    region = place[0]
    extent = 3 * per_dev
    d = halo(received, region, regions, extent, per_dev)
    r = halo(received, region, regions, extent + per_dev, per_dev)
    m = d + gathered(received, region, regions, per_dev)
    diag[...] = d
    precond[...] = m
    resid[...] = r
    own = slice(per_dev, 2 * per_dev)
    send_rows(jac, index, r, r / m, d, spread, own, out)


def update(place, received, diag, precond, resid, along, direct, answer, scal):
    regions = received.shape[0]
    per_dev = direct.shape[0]
    extent = 3 * per_dev
    r, d, m = resid[...], diag[...], precond[...]
    z = r / m
    image = d * z + gathered(received, place[0], regions, per_dev)
    sums = received[0, extent : extent + SUB, :]
    for member in range(1, regions):
        sums = sums + received[member, extent : extent + SUB, :]
    sums = jnp.sum(sums, axis=1, keepdims=True)
    gamma, delta = sums[:1], sums[1:2]
    before, alpha = scal[0:1, :1], scal[1:2, :1]
    started = alpha != 0.0
    beta = jnp.where(started, gamma / jnp.where(started, before, 1.0), 0.0)
    fall = jnp.where(started, beta * gamma / jnp.where(started, alpha, 1.0), 0.0)
    alpha = gamma / (delta - fall)
    s = image + beta * along[...]
    p = z[per_dev : 2 * per_dev] + beta * direct[...]
    x = answer[...] + alpha * p
    return x, r - alpha * s, s, p, gamma, alpha


def step_kernel(
    place, index, jac, received, diag, precond, resid, along, direct, answer, scal,
    out, resid_o, along_o, direct_o, answer_o, scal_o, spread,
):
    per_dev = direct.shape[0]
    x, r, s, p, gamma, alpha = update(
        place, received, diag, precond, resid, along, direct, answer, scal
    )
    resid_o[...] = r
    along_o[...] = s
    direct_o[...] = p
    answer_o[...] = x
    scal_o[0:1, :] = jnp.broadcast_to(gamma, (1, scal_o.shape[1]))
    scal_o[1:2, :] = jnp.broadcast_to(alpha, (1, scal_o.shape[1]))
    own = slice(per_dev, 2 * per_dev)
    send_rows(jac, index, r, r / precond[...], diag, spread, own, out)


def last_kernel(
    place, received, diag, precond, resid, along, direct, answer, scal, answer_o, resid_o
):
    per_dev = direct.shape[0]
    x, r, _, _, _, _ = update(
        place, received, diag, precond, resid, along, direct, answer, scal
    )
    answer_o[...] = x
    resid_o[...] = r[per_dev : 2 * per_dev]


def call(kernel, outs, scratch, specs, name, flops, moved):
    return pl.pallas_call(
        kernel,
        out_shape=[jax.ShapeDtypeStruct(shape, jnp.float32) for shape in outs],
        in_specs=specs,
        out_specs=[vmem] * len(outs),
        scratch_shapes=scratch,
        compiler_params=pltpu.CompilerParams(vmem_limit_bytes=VMEM_LIMIT),
        cost_estimate=pl.CostEstimate(
            flops=flops, bytes_accessed=moved, transcendentals=0
        ),
        name=name,
    )


def body(jac, pattern, branch_weight, bus_diag, right_side):
    blocks = lax.axis_size("blk")
    regions = lax.axis_size("region")
    per_dev, width = right_side.shape
    tiles, slots = jac.shape[:2]
    extent = 3 * per_dev
    f32 = jnp.float32

    def across_blk(value):
        return [
            lax.ppermute(value, "blk", [(i, (i + k) % blocks) for i in range(blocks)])
            for k in range(1, blocks)
        ]

    def across_region(chunks):
        return lax.all_to_all(chunks, "region", 0, 0, tiled=True)

    group = lax.axis_index("blk")
    place = lax.axis_index("region").astype(jnp.int32).reshape(1)
    fits = jnp.pad(pattern.astype(f32), ((0, 0), (0, width - pattern.shape[1])))
    mine = jnp.concatenate([branch_weight, fits], axis=0)
    shared = jnp.stack([mine] + across_blk(mine))
    order = lax.rem(group - jnp.arange(blocks, dtype=jnp.int32) + blocks, blocks)
    shared = shared[order]
    weight = shared[:, : branch_weight.shape[0]].reshape(tiles, width)
    chosen = shared[:, branch_weight.shape[0] :].reshape(tiles, width)
    index = lax.dynamic_slice_in_dim(chosen, group * slots, slots, axis=1)
    index = index.astype(jnp.int32).reshape(-1)

    flops = 4 * jac.size
    moved = 4 * jac.size
    row_count = tiles + SUB
    spread = pltpu.VMEM((extent, SUB, width), f32)
    banks = pltpu.VMEM((BANKS, extent, SUB, width), f32)
    chunk = (regions, extent + SUB, width)
    halo_shape, own_shape = (extent, width), (per_dev, width)

    (setup,) = call(
        diag_kernel, [(regions, extent + 2 * per_dev, width)], [banks],
        [smem, vmem, vmem, vmem, vmem], "diagonal", flops, moved,
    )(index, jac, weight, bus_diag, right_side)
    out, diag, precond, resid = call(
        first_kernel, [(row_count, width), halo_shape, halo_shape, halo_shape],
        [spread], [smem, smem, vmem, vmem], "first", flops, moved,
    )(place, index, jac, across_region(setup))

    def image_of(out):
        parts = across_blk(out)
        (chunks,) = call(
            back_kernel, [chunk], [pltpu.VMEM((tiles, width), f32), banks],
            [smem] + [vmem] * (3 + len(parts)), "back", flops, moved,
        )(index, jac, weight, out, *parts)
        return across_region(chunks)

    def step(i, carry):
        received, resid, along, direct, answer, scal = carry
        out, resid, along, direct, answer, scal = call(
            step_kernel,
            [(row_count, width), halo_shape, halo_shape, own_shape, own_shape, (SUB, width)],
            [spread], [smem, smem] + [vmem] * 9, "step", flops, moved,
        )(place, index, jac, received, diag, precond, resid, along, direct, answer, scal)
        return image_of(out), resid, along, direct, answer, scal

    carry = (
        image_of(out), resid, jnp.zeros(halo_shape, f32), jnp.zeros(own_shape, f32),
        jnp.zeros(own_shape, f32), jnp.zeros((SUB, width), f32),
    )
    carry = lax.fori_loop(0, ITERS - 1, step, carry)
    received, resid, along, direct, answer, scal = carry
    answer, resid = call(
        last_kernel, [own_shape, own_shape], [], [smem] + [vmem] * 8, "last", 1000, 1000
    )(place, received, diag, precond, resid, along, direct, answer, scal)
    return answer, resid


def solution(mesh):
    both = P(("region", "blk"), None)
    return jax.shard_map(
        body,
        mesh=mesh,
        in_specs=(P("region", "blk", None, None), both, both, both, both),
        out_specs=(both, both),
        check_vma=False,
    )
```

time: 1100 us -> 277 us (0.25)
  blocking collectives: 673 us -> 10.6 us
  matrix products: 92.2 us -> 0 us
  Pallas kernels: 0 us -> 70.3 us
  starting transfers between devices: 107 us -> 63 us
  other arithmetic: 34 us -> 1.48 us
  loops' own time: 32.4 us -> 0.61 us
  local copies, waits for them, and re-layouts: 20.5 us -> 2.21 us
  waiting for transfers between devices: 138 us -> 127 us
    psum x12 -> x0, blocking collectives: 475 us -> none  [paired(): lax.psum((jnp.sum(resid * scaled), jnp.sum(image * scaled)), ('region', '...]
    while x11 -> x0, blocking collectives: 112 us -> none
    dot_general x25 -> x0, matrix products: 92.2 us -> none  [the longest x12 64.8 us: branch_rows(): return jnp.einsum('tjab,tjb->ta', tiles, flat[index], precision=hp)]
    ppermute x50 -> x39, starting transfers between devices: 102 us -> 20.1 us  [across_blk(): lax.ppermute(value, 'blk', [(i, (i + k) % blocks) for i in range(blocks)])]
    pallas_call x0 -> x26, Pallas kernels: none -> 70.3 us  [the longest x11 37.7 us: step(): call(step_kernel, [(row_count, width), halo_shape, halo_shape, own_shape,...]
    all_gather x12 -> x0, blocking collectives: 66.3 us -> none  [branch_rows(): region_vals = lax.all_gather(vector[None], 'blk', axis=0, tiled=True)]
    ppermute x50 -> x39, waiting for transfers between devices: 89.6 us -> 38.4 us  [across_blk(): lax.ppermute(value, 'blk', [(i, (i + k) % blocks) for i in range(blocks)])]
    all_to_all x1 -> x12, waiting for transfers between devices: 48.7 us -> 88.3 us  [across_region(): return lax.all_to_all(chunks, 'region', 0, 0, tiled=True)]
  transfers between devices with their start and end apart: 51 -> 51, of which waited for: 39 -> 42; matrix products, arithmetic and copies ran while one was open for 1% -> 0% of each run, Pallas kernels for 0% -> 0%
where the time goes in v1:
time: 277 us; the launch traced here: 276 us
  waiting for transfers between devices  127 us (46%)
  Pallas kernels  70.3 us (25%)
  starting transfers between devices  63 us (23%)
  blocking collectives  10.6 us (4%)
    all_to_all x12, waiting for transfers between devices, across_region(): return lax.all_to_all(chunks, 'region', 0, 0, tiled=True)  88.3 us
    all_to_all x12, starting transfers between devices, across_region(): return lax.all_to_all(chunks, 'region', 0, 0, tiled=True)  42.9 us
    ppermute x39, waiting for transfers between devices, across_blk(): lax.ppermute(value, 'blk', [(i, (i + k) % blocks) for i in range(blocks)])  38.4 us
    pallas_call x11, Pallas kernels, step(): call(step_kernel, [(row_count, width), halo_shape, halo_shape, own_shape,...  37.7 us
    pallas_call x12, Pallas kernels, image_of(): call(back_kernel, [chunk], [pltpu.VMEM((tiles, width), f32), banks], [sme...  24.9 us
    ppermute x39, starting transfers between devices, across_blk(): lax.ppermute(value, 'blk', [(i, (i + k) % blocks) for i in range(blocks)])  20.1 us
    all_to_all x1, blocking collectives, across_region(): return lax.all_to_all(chunks, 'region', 0, 0, tiled=True)  10.6 us
  transfers between devices with their start and end apart: 51, of which 42 were waited for; matrix products, arithmetic and copies ran while one was open for 0% of the time, Pallas kernels for 0%

profile of v1, /device:TPU:0, one launch (start us, length us, event | category | flops | bytes accessed | tf_op | source)
XLA Modules:
  0.0 275.6 jit_solution(46597152124268598)
XLA Ops:
  2.0 3.0 %collective-permute-start.4 = (f32[16,128]{1,0:T(8,128)S(1)}, f32[16,128]{1,0:T(8,128)S(1)}, u32[]{:S(2)}, u32[]{:S(2)}) collective-permute-start(f32[16,128]{1,0:T(8,128)S(1)} %get-tuple-element.123), channel_id=1, source_target_pairs={{0,2},{1,3},{2,0},{3,1},{4,6},{5,7},{6,4},{7,5},{8,10},{9,11},{10,... | collective-permute-start | bytes 24584 | tf_op jit(solution)/shard_map/ppermute | solution.py:231
  5.0 1.7 collective-permute-start.5
  10.2 3.8 %diagonal.1 = f32[8,40,128]{2,1,0:T(8,128)} custom-call(s32[64]{0:T(128)S(1)} %reshape.55.index, f32[32,2,128,128]{3,2,1,0:T(8,128)} %jac.5, f32[32,128]{1,0:T(8,128)S(1)} %get-tuple-element.227.weight, f32[8,128]{1,0:T(8,128)S(1)} %copy-done, f32[8,128]{1,0:T(8,128)S(1)} %copy-done.1), custom_call_target="tpu_custom_call" | custom-call | flops 4194304 | bytes 4194304 | tf_op jit(solution)/shard_map/diagonal/pallas_call | solution.py:258
  14.0 5.8 %all-to-all-start.1 = ((f32[8,40,128]{2,1,0:T(8,128)}), f32[8,40,128]{2,1,0:T(8,128)S(1)}, u32[]{:S(2)}, u32[]{:S(2)}) async-start(f32[8,40,128]{2,1,0:T(8,128)} %diagonal.1), calls=%async_computation.1 | async-start | bytes 327680 | tf_op jit(solution)/shard_map/all_to_all | solution.py:236
  19.9 8.2 %all-to-all-done.1.received = f32[8,40,128]{2,1,0:T(8,128)S(1)} async-done(((f32[8,40,128]{2,1,0:T(8,128)}), f32[8,40,128]{2,1,0:T(8,128)S(1)}, u32[]{:S(2)}, u32[]{:S(2)}) %all-to-all-start.1) | async-done | bytes 163872 | tf_op jit(solution)/shard_map/all_to_all | solution.py:236
  28.1 3.3 %first.1 = (f32[40,128]{1,0:T(8,128)S(1)}, f32[24,128]{1,0:T(8,128)S(1)}, f32[24,128]{1,0:T(8,128)S(1)}, f32[24,128]{1,0:T(8,128)S(1)}) custom-call(s32[1]{0:T(128)} %bitcast.place, s32[64]{0:T(128)S(1)} %reshape.55.index, f32[32,2,128,128]{3,2,1,0:T(8,128)} %jac.5, f32[8,40,128]{2,1,0:T(8,128)S(1)} %all-to-all-done.1.received), custom_call_target="tpu_custom_call" | custom-call | flops 4194304 | bytes 4194304 | tf_op jit(solution)/shard_map/first/pallas_call | solution.py:262
  33.6 2.3 collective-permute-done.7.refs_1_
  37.4 10.6 %all_to_all.16 = f32[8,32,128]{2,1,0:T(8,128)S(1)} all-to-all(f32[8,32,128]{2,1,0:T(8,128)S(1)} %back.2), channel_id=1, replica_groups=mesh['region'=8,'blk'=4] {'region'}, dimensions={0} | all-to-all | bytes 262144 | tf_op jit(solution)/shard_map/all_to_all | solution.py:236
  47.9 226.9 %while.20 = (s32[]{:T(128)}, f32[8,32,128]{2,1,0:T(8,128)S(1)}, f32[24,128]{1,0:T(8,128)S(1)}, f32[24,128]{1,0:T(8,128)S(1)}, f32[8,128]{1,0:T(8,128)S(1)}, /*in...) while((s32[]{:T(128)}, f32[8,32,128]{2,1,0:T(8,128)S(1)}, ...), condition=%wide.region_1.2_spmd, body=%wide.region_0.1_spmd.sunk | while | flops 8388610 | bytes 25878840 | solution.py:288
  48.0 3.4 %step.1 = (f32[40,128]{1,0:T(8,128)S(1)}, f32[24,128]{1,0:T(8,128)S(1)}, f32[24,128]{1,0:T(8,128)S(1)}, f32[8,128]{1,0:T(8,128)S(1)}, f32[8,128]{1,0:T(8,128)S(1)}, /*index=5*/f32[8,128]{1,0:T(8,128)S(1)}) custom-call(s32[1]{0:T(128)} %get-tuple-element.250.place, s32[64]{0:T(128)S(1)} %get-tuple-element.251.index, ...), custom_call_target="tpu_custom_call" | custom-call | flops 4194304 | bytes 4194304 | tf_op jit(solution)/shard_map/while/body/eval_jaxpr/step/pallas_call | solution.py:277
  53.0 2.4 collective-permute-done.1.refs_1_
  56.0 2.1 back.3
  58.2 3.4 %all-to-all-start = ((f32[8,32,128]{2,1,0:T(8,128)}), f32[8,32,128]{2,1,0:T(8,128)S(1)}, u32[]{:S(2)}, u32[]{:S(2)}) async-start(f32[8,32,128]{2,1,0:T(8,128)} %back.3), calls=%async_computation | async-start | bytes 262144 | tf_op jit(solution)/shard_map/while/body/eval_jaxpr/all_to_all | solution.py:236
  61.5 7.3 %all-to-all-done = f32[8,32,128]{2,1,0:T(8,128)S(1)} async-done(((f32[8,32,128]{2,1,0:T(8,128)}), f32[8,32,128]{2,1,0:T(8,128)S(1)}, u32[]{:S(2)}, u32[]{:S(2)}) %all-to-all-start) | async-done | bytes 131104 | tf_op jit(solution)/shard_map/while/body/eval_jaxpr/all_to_all | solution.py:236
  68.8 3.4 %step.1 = (f32[40,128]{1,0:T(8,128)S(1)}, f32[24,128]{1,0:T(8,128)S(1)}, f32[24,128]{1,0:T(8,128)S(1)}, f32[8,128]{1,0:T(8,128)S(1)}, f32[8,128]{1,0:T(8,128)S(1)}, /*index=5*/f32[8,128]{1,0:T(8,128)S(1)}) custom-call(s32[1]{0:T(128)} %get-tuple-element.250.place, s32[64]{0:T(128)S(1)} %get-tuple-element.251.index, ...), custom_call_target="tpu_custom_call" | custom-call | flops 4194304 | bytes 4194304 | tf_op jit(solution)/shard_map/while/body/eval_jaxpr/step/pallas_call | solution.py:277
  73.8 2.4 collective-permute-done.1.refs_1_
  76.4 2.1 back.3
  78.5 3.4 %all-to-all-start = ((f32[8,32,128]{2,1,0:T(8,128)}), f32[8,32,128]{2,1,0:T(8,128)S(1)}, u32[]{:S(2)}, u32[]{:S(2)}) async-start(f32[8,32,128]{2,1,0:T(8,128)} %back.3), calls=%async_computation | async-start | bytes 262144 | tf_op jit(solution)/shard_map/while/body/eval_jaxpr/all_to_all | solution.py:236
  81.9 7.3 %all-to-all-done = f32[8,32,128]{2,1,0:T(8,128)S(1)} async-done(((f32[8,32,128]{2,1,0:T(8,128)}), f32[8,32,128]{2,1,0:T(8,128)S(1)}, u32[]{:S(2)}, u32[]{:S(2)}) %all-to-all-start) | async-done | bytes 131104 | tf_op jit(solution)/shard_map/while/body/eval_jaxpr/all_to_all | solution.py:236
  89.2 3.4 %step.1 = (f32[40,128]{1,0:T(8,128)S(1)}, f32[24,128]{1,0:T(8,128)S(1)}, f32[24,128]{1,0:T(8,128)S(1)}, f32[8,128]{1,0:T(8,128)S(1)}, f32[8,128]{1,0:T(8,128)S(1)}, /*index=5*/f32[8,128]{1,0:T(8,128)S(1)}) custom-call(s32[1]{0:T(128)} %get-tuple-element.250.place, s32[64]{0:T(128)S(1)} %get-tuple-element.251.index, ...), custom_call_target="tpu_custom_call" | custom-call | flops 4194304 | bytes 4194304 | tf_op jit(solution)/shard_map/while/body/eval_jaxpr/step/pallas_call | solution.py:277
  94.2 2.4 collective-permute-done.1.refs_1_
  97.2 2.1 back.3
  99.4 3.4 %all-to-all-start = ((f32[8,32,128]{2,1,0:T(8,128)}), f32[8,32,128]{2,1,0:T(8,128)S(1)}, u32[]{:S(2)}, u32[]{:S(2)}) async-start(f32[8,32,128]{2,1,0:T(8,128)} %back.3), calls=%async_computation | async-start | bytes 262144 | tf_op jit(solution)/shard_map/while/body/eval_jaxpr/all_to_all | solution.py:236
  102.7 7.3 %all-to-all-done = f32[8,32,128]{2,1,0:T(8,128)S(1)} async-done(((f32[8,32,128]{2,1,0:T(8,128)}), f32[8,32,128]{2,1,0:T(8,128)S(1)}, u32[]{:S(2)}, u32[]{:S(2)}) %all-to-all-start) | async-done | bytes 131104 | tf_op jit(solution)/shard_map/while/body/eval_jaxpr/all_to_all | solution.py:236
  110.1 3.4 %step.1 = (f32[40,128]{1,0:T(8,128)S(1)}, f32[24,128]{1,0:T(8,128)S(1)}, f32[24,128]{1,0:T(8,128)S(1)}, f32[8,128]{1,0:T(8,128)S(1)}, f32[8,128]{1,0:T(8,128)S(1)}, /*index=5*/f32[8,128]{1,0:T(8,128)S(1)}) custom-call(s32[1]{0:T(128)} %get-tuple-element.250.place, s32[64]{0:T(128)S(1)} %get-tuple-element.251.index, ...), custom_call_target="tpu_custom_call" | custom-call | flops 4194304 | bytes 4194304 | tf_op jit(solution)/shard_map/while/body/eval_jaxpr/step/pallas_call | solution.py:277
  115.0 2.4 collective-permute-done.1.refs_1_
  117.6 2.1 back.3
  119.8 3.4 %all-to-all-start = ((f32[8,32,128]{2,1,0:T(8,128)}), f32[8,32,128]{2,1,0:T(8,128)S(1)}, u32[]{:S(2)}, u32[]{:S(2)}) async-start(f32[8,32,128]{2,1,0:T(8,128)} %back.3), calls=%async_computation | async-start | bytes 262144 | tf_op jit(solution)/shard_map/while/body/eval_jaxpr/all_to_all | solution.py:236
  123.1 7.3 %all-to-all-done = f32[8,32,128]{2,1,0:T(8,128)S(1)} async-done(((f32[8,32,128]{2,1,0:T(8,128)}), f32[8,32,128]{2,1,0:T(8,128)S(1)}, u32[]{:S(2)}, u32[]{:S(2)}) %all-to-all-start) | async-done | bytes 131104 | tf_op jit(solution)/shard_map/while/body/eval_jaxpr/all_to_all | solution.py:236
  130.4 3.4 %step.1 = (f32[40,128]{1,0:T(8,128)S(1)}, f32[24,128]{1,0:T(8,128)S(1)}, f32[24,128]{1,0:T(8,128)S(1)}, f32[8,128]{1,0:T(8,128)S(1)}, f32[8,128]{1,0:T(8,128)S(1)}, /*index=5*/f32[8,128]{1,0:T(8,128)S(1)}) custom-call(s32[1]{0:T(128)} %get-tuple-element.250.place, s32[64]{0:T(128)S(1)} %get-tuple-element.251.index, ...), custom_call_target="tpu_custom_call" | custom-call | flops 4194304 | bytes 4194304 | tf_op jit(solution)/shard_map/while/body/eval_jaxpr/step/pallas_call | solution.py:277
  135.4 2.4 collective-permute-done.1.refs_1_
  138.5 2.1 back.3
  140.6 3.4 %all-to-all-start = ((f32[8,32,128]{2,1,0:T(8,128)}), f32[8,32,128]{2,1,0:T(8,128)S(1)}, u32[]{:S(2)}, u32[]{:S(2)}) async-start(f32[8,32,128]{2,1,0:T(8,128)} %back.3), calls=%async_computation | async-start | bytes 262144 | tf_op jit(solution)/shard_map/while/body/eval_jaxpr/all_to_all | solution.py:236
  144.0 7.3 %all-to-all-done = f32[8,32,128]{2,1,0:T(8,128)S(1)} async-done(((f32[8,32,128]{2,1,0:T(8,128)}), f32[8,32,128]{2,1,0:T(8,128)S(1)}, u32[]{:S(2)}, u32[]{:S(2)}) %all-to-all-start) | async-done | bytes 131104 | tf_op jit(solution)/shard_map/while/body/eval_jaxpr/all_to_all | solution.py:236
  151.3 3.4 %step.1 = (f32[40,128]{1,0:T(8,128)S(1)}, f32[24,128]{1,0:T(8,128)S(1)}, f32[24,128]{1,0:T(8,128)S(1)}, f32[8,128]{1,0:T(8,128)S(1)}, f32[8,128]{1,0:T(8,128)S(1)}, /*index=5*/f32[8,128]{1,0:T(8,128)S(1)}) custom-call(s32[1]{0:T(128)} %get-tuple-element.250.place, s32[64]{0:T(128)S(1)} %get-tuple-element.251.index, ...), custom_call_target="tpu_custom_call" | custom-call | flops 4194304 | bytes 4194304 | tf_op jit(solution)/shard_map/while/body/eval_jaxpr/step/pallas_call | solution.py:277
  156.2 2.4 collective-permute-done.1.refs_1_
  158.8 2.1 back.3
  161.0 3.4 %all-to-all-start = ((f32[8,32,128]{2,1,0:T(8,128)}), f32[8,32,128]{2,1,0:T(8,128)S(1)}, u32[]{:S(2)}, u32[]{:S(2)}) async-start(f32[8,32,128]{2,1,0:T(8,128)} %back.3), calls=%async_computation | async-start | bytes 262144 | tf_op jit(solution)/shard_map/while/body/eval_jaxpr/all_to_all | solution.py:236
  164.3 7.3 %all-to-all-done = f32[8,32,128]{2,1,0:T(8,128)S(1)} async-done(((f32[8,32,128]{2,1,0:T(8,128)}), f32[8,32,128]{2,1,0:T(8,128)S(1)}, u32[]{:S(2)}, u32[]{:S(2)}) %all-to-all-start) | async-done | bytes 131104 | tf_op jit(solution)/shard_map/while/body/eval_jaxpr/all_to_all | solution.py:236
  171.7 3.4 %step.1 = (f32[40,128]{1,0:T(8,128)S(1)}, f32[24,128]{1,0:T(8,128)S(1)}, f32[24,128]{1,0:T(8,128)S(1)}, f32[8,128]{1,0:T(8,128)S(1)}, f32[8,128]{1,0:T(8,128)S(1)}, /*index=5*/f32[8,128]{1,0:T(8,128)S(1)}) custom-call(s32[1]{0:T(128)} %get-tuple-element.250.place, s32[64]{0:T(128)S(1)} %get-tuple-element.251.index, ...), custom_call_target="tpu_custom_call" | custom-call | flops 4194304 | bytes 4194304 | tf_op jit(solution)/shard_map/while/body/eval_jaxpr/step/pallas_call | solution.py:277
  176.6 2.4 collective-permute-done.1.refs_1_
  179.7 2.1 back.3
  181.8 3.4 %all-to-all-start = ((f32[8,32,128]{2,1,0:T(8,128)}), f32[8,32,128]{2,1,0:T(8,128)S(1)}, u32[]{:S(2)}, u32[]{:S(2)}) async-start(f32[8,32,128]{2,1,0:T(8,128)} %back.3), calls=%async_computation | async-start | bytes 262144 | tf_op jit(solution)/shard_map/while/body/eval_jaxpr/all_to_all | solution.py:236
  185.2 7.3 %all-to-all-done = f32[8,32,128]{2,1,0:T(8,128)S(1)} async-done(((f32[8,32,128]{2,1,0:T(8,128)}), f32[8,32,128]{2,1,0:T(8,128)S(1)}, u32[]{:S(2)}, u32[]{:S(2)}) %all-to-all-start) | async-done | bytes 131104 | tf_op jit(solution)/shard_map/while/body/eval_jaxpr/all_to_all | solution.py:236
  192.5 3.4 %step.1 = (f32[40,128]{1,0:T(8,128)S(1)}, f32[24,128]{1,0:T(8,128)S(1)}, f32[24,128]{1,0:T(8,128)S(1)}, f32[8,128]{1,0:T(8,128)S(1)}, f32[8,128]{1,0:T(8,128)S(1)}, /*index=5*/f32[8,128]{1,0:T(8,128)S(1)}) custom-call(s32[1]{0:T(128)} %get-tuple-element.250.place, s32[64]{0:T(128)S(1)} %get-tuple-element.251.index, ...), custom_call_target="tpu_custom_call" | custom-call | flops 4194304 | bytes 4194304 | tf_op jit(solution)/shard_map/while/body/eval_jaxpr/step/pallas_call | solution.py:277
  197.5 2.4 collective-permute-done.1.refs_1_
  200.0 2.1 back.3
  202.2 3.4 %all-to-all-start = ((f32[8,32,128]{2,1,0:T(8,128)}), f32[8,32,128]{2,1,0:T(8,128)S(1)}, u32[]{:S(2)}, u32[]{:S(2)}) async-start(f32[8,32,128]{2,1,0:T(8,128)} %back.3), calls=%async_computation | async-start | bytes 262144 | tf_op jit(solution)/shard_map/while/body/eval_jaxpr/all_to_all | solution.py:236
  205.6 7.3 %all-to-all-done = f32[8,32,128]{2,1,0:T(8,128)S(1)} async-done(((f32[8,32,128]{2,1,0:T(8,128)}), f32[8,32,128]{2,1,0:T(8,128)S(1)}, u32[]{:S(2)}, u32[]{:S(2)}) %all-to-all-start) | async-done | bytes 131104 | tf_op jit(solution)/shard_map/while/body/eval_jaxpr/all_to_all | solution.py:236
  212.9 3.4 %step.1 = (f32[40,128]{1,0:T(8,128)S(1)}, f32[24,128]{1,0:T(8,128)S(1)}, f32[24,128]{1,0:T(8,128)S(1)}, f32[8,128]{1,0:T(8,128)S(1)}, f32[8,128]{1,0:T(8,128)S(1)}, /*index=5*/f32[8,128]{1,0:T(8,128)S(1)}) custom-call(s32[1]{0:T(128)} %get-tuple-element.250.place, s32[64]{0:T(128)S(1)} %get-tuple-element.251.index, ...), custom_call_target="tpu_custom_call" | custom-call | flops 4194304 | bytes 4194304 | tf_op jit(solution)/shard_map/while/body/eval_jaxpr/step/pallas_call | solution.py:277
  217.8 2.4 collective-permute-done.1.refs_1_
  220.9 2.1 back.3
  223.0 3.4 %all-to-all-start = ((f32[8,32,128]{2,1,0:T(8,128)}), f32[8,32,128]{2,1,0:T(8,128)S(1)}, u32[]{:S(2)}, u32[]{:S(2)}) async-start(f32[8,32,128]{2,1,0:T(8,128)} %back.3), calls=%async_computation | async-start | bytes 262144 | tf_op jit(solution)/shard_map/while/body/eval_jaxpr/all_to_all | solution.py:236
  226.4 7.3 %all-to-all-done = f32[8,32,128]{2,1,0:T(8,128)S(1)} async-done(((f32[8,32,128]{2,1,0:T(8,128)}), f32[8,32,128]{2,1,0:T(8,128)S(1)}, u32[]{:S(2)}, u32[]{:S(2)}) %all-to-all-start) | async-done | bytes 131104 | tf_op jit(solution)/shard_map/while/body/eval_jaxpr/all_to_all | solution.py:236
  233.7 3.4 %step.1 = (f32[40,128]{1,0:T(8,128)S(1)}, f32[24,128]{1,0:T(8,128)S(1)}, f32[24,128]{1,0:T(8,128)S(1)}, f32[8,128]{1,0:T(8,128)S(1)}, f32[8,128]{1,0:T(8,128)S(1)}, /*index=5*/f32[8,128]{1,0:T(8,128)S(1)}) custom-call(s32[1]{0:T(128)} %get-tuple-element.250.place, s32[64]{0:T(128)S(1)} %get-tuple-element.251.index, ...), custom_call_target="tpu_custom_call" | custom-call | flops 4194304 | bytes 4194304 | tf_op jit(solution)/shard_map/while/body/eval_jaxpr/step/pallas_call | solution.py:277
  238.7 2.4 collective-permute-done.1.refs_1_
  241.3 2.1 back.3
  243.4 3.4 %all-to-all-start = ((f32[8,32,128]{2,1,0:T(8,128)}), f32[8,32,128]{2,1,0:T(8,128)S(1)}, u32[]{:S(2)}, u32[]{:S(2)}) async-start(f32[8,32,128]{2,1,0:T(8,128)} %back.3), calls=%async_computation | async-start | bytes 262144 | tf_op jit(solution)/shard_map/while/body/eval_jaxpr/all_to_all | solution.py:236
  246.8 7.3 %all-to-all-done = f32[8,32,128]{2,1,0:T(8,128)S(1)} async-done(((f32[8,32,128]{2,1,0:T(8,128)}), f32[8,32,128]{2,1,0:T(8,128)S(1)}, u32[]{:S(2)}, u32[]{:S(2)}) %all-to-all-start) | async-done | bytes 131104 | tf_op jit(solution)/shard_map/while/body/eval_jaxpr/all_to_all | solution.py:236
  254.1 3.4 %step.1 = (f32[40,128]{1,0:T(8,128)S(1)}, f32[24,128]{1,0:T(8,128)S(1)}, f32[24,128]{1,0:T(8,128)S(1)}, f32[8,128]{1,0:T(8,128)S(1)}, f32[8,128]{1,0:T(8,128)S(1)}, /*index=5*/f32[8,128]{1,0:T(8,128)S(1)}) custom-call(s32[1]{0:T(128)} %get-tuple-element.250.place, s32[64]{0:T(128)S(1)} %get-tuple-element.251.index, ...), custom_call_target="tpu_custom_call" | custom-call | flops 4194304 | bytes 4194304 | tf_op jit(solution)/shard_map/while/body/eval_jaxpr/step/pallas_call | solution.py:277
  259.1 2.4 collective-permute-done.1.refs_1_
  262.1 2.1 back.3
  264.2 3.4 %all-to-all-start = ((f32[8,32,128]{2,1,0:T(8,128)}), f32[8,32,128]{2,1,0:T(8,128)S(1)}, u32[]{:S(2)}, u32[]{:S(2)}) async-start(f32[8,32,128]{2,1,0:T(8,128)} %back.3), calls=%async_computation | async-start | bytes 262144 | tf_op jit(solution)/shard_map/while/body/eval_jaxpr/all_to_all | solution.py:236
  267.6 7.3 %all-to-all-done = f32[8,32,128]{2,1,0:T(8,128)S(1)} async-done(((f32[8,32,128]{2,1,0:T(8,128)}), f32[8,32,128]{2,1,0:T(8,128)S(1)}, u32[]{:S(2)}, u32[]{:S(2)}) %all-to-all-start) | async-done | bytes 131104 | tf_op jit(solution)/shard_map/while/body/eval_jaxpr/all_to_all | solution.py:236
  (162 shorter events, 31.3 us)
Async XLA Ops:
  2.0 4.7 %collective-permute-start.4 = (f32[16,128]{1,0:T(8,128)S(1)}, f32[16,128]{1,0:T(8,128)S(1)}, u32[]{:S(2)}, u32[]{:S(2)}) collective-permute-start(f32[16,128]{1,0:T(8,128)S(1)} %get-tuple-element.123), channel_id=1, source_target_pairs={{0,2},{1,3},{2,0},{3,1},{4,6},{5,7},{6,4},{7,5},{8,10},{9,11},{10,... | collective-permute-start | bytes 24584 | tf_op jit(solution)/shard_map/ppermute | solution.py:231
  5.0 3.1 %collective-permute-start.3 = (f32[16,128]{1,0:T(8,128)S(1)}, f32[16,128]{1,0:T(8,128)S(1)}, u32[]{:S(2)}, u32[]{:S(2)}) collective-permute-start(f32[16,128]{1,0:T(8,128)S(1)} %get-tuple-element.123), channel_id=1, source_target_pairs={{0,1},{1,2},{2,3},{3,0},{4,5},{5,6},{6,7},{7,4},{8,9},{9,10},{10,1... | collective-permute-start | bytes 24584 | tf_op jit(solution)/shard_map/ppermute | solution.py:231
  5.0 3.1 %collective-permute-start.5 = (f32[16,128]{1,0:T(8,128)S(1)}, f32[16,128]{1,0:T(8,128)S(1)}, u32[]{:S(2)}, u32[]{:S(2)}) collective-permute-start(f32[16,128]{1,0:T(8,128)S(1)} %get-tuple-element.123), channel_id=1, source_target_pairs={{0,3},{1,0},{2,1},{3,2},{4,7},{5,4},{6,5},{7,6},{8,11},{9,8},{10,9... | collective-permute-start | bytes 24584 | tf_op jit(solution)/shard_map/ppermute | solution.py:231
  8.9 0.7 copy-start
  14.0 14.1 %all-to-all-start.1 = ((f32[8,40,128]{2,1,0:T(8,128)}), f32[8,40,128]{2,1,0:T(8,128)S(1)}, u32[]{:S(2)}, u32[]{:S(2)}) async-start(f32[8,40,128]{2,1,0:T(8,128)} %diagonal.1), calls=%async_computation.1 | async-start | bytes 327680 | tf_op jit(solution)/shard_map/all_to_all | solution.py:236
  28.1 7.8 %copy-start.2 = (f32[32,2,128,128]{3,2,1,0:T(8,128)S(1)}, f32[32,2,128,128]{3,2,1,0:T(8,128)}, u32[]{:S(2)}) copy-start(f32[32,2,128,128]{3,2,1,0:T(8,128)} %jac.5) | copy-start | bytes 12582916
  31.4 2.2 collective-permute-start.8
  32.1 3.8 %collective-permute-start.7 = (f32[40,128]{1,0:T(8,128)S(1)}, f32[40,128]{1,0:T(8,128)S(1)}, u32[]{:S(2)}, u32[]{:S(2)}) collective-permute-start(f32[40,128]{1,0:T(8,128)S(1)} %get-tuple-element.84.own), channel_id=1, source_target_pairs={{0,2},{1,3},{2,0},{3,1},{4,6},{5,7},{6,4},{7,5},{8,10},{9,11},{10,... | collective-permute-start | bytes 61448 | tf_op jit(solution)/shard_map/ppermute | solution.py:231
  32.3 3.6 %collective-permute-start.6 = (f32[40,128]{1,0:T(8,128)S(1)}, f32[40,128]{1,0:T(8,128)S(1)}, u32[]{:S(2)}, u32[]{:S(2)}) collective-permute-start(f32[40,128]{1,0:T(8,128)S(1)} %get-tuple-element.84.own), channel_id=1, source_target_pairs={{0,1},{1,2},{2,3},{3,0},{4,5},{5,6},{6,7},{7,4},{8,9},{9,10},{10,1... | collective-permute-start | bytes 61448 | tf_op jit(solution)/shard_map/ppermute | solution.py:231
  48.0 8.1 %copy-start.3 = (f32[32,2,128,128]{3,2,1,0:T(8,128)S(1)}, f32[32,2,128,128]{3,2,1,0:T(8,128)}, u32[]{:S(2)}) copy-start(f32[32,2,128,128]{3,2,1,0:T(8,128)} %get-tuple-element.252.jac) | copy-start | bytes 12582916 | tf_op jit(solution)/shard_map/while
  51.5 1.5 collective-permute-start.2
  51.5 3.8 %collective-permute-start.1 = (f32[40,128]{1,0:T(8,128)S(1)}, f32[40,128]{1,0:T(8,128)S(1)}, u32[]{:S(2)}, u32[]{:S(2)}) collective-permute-start(f32[40,128]{1,0:T(8,128)S(1)} %get-tuple-element.209.own), channel_id=1, source_target_pairs={{0,2},{1,3},{2,0},{3,1},{4,6},{5,7},{6,4},{7,5},{8,10},{9,11},{10,... | collective-permute-start | bytes 61448 | tf_op jit(solution)/shard_map/while/body/eval_jaxpr/ppermute | solution.py:231
  52.8 3.2 %collective-permute-start = (f32[40,128]{1,0:T(8,128)S(1)}, f32[40,128]{1,0:T(8,128)S(1)}, u32[]{:S(2)}, u32[]{:S(2)}) collective-permute-start(f32[40,128]{1,0:T(8,128)S(1)} %get-tuple-element.209.own), channel_id=1, source_target_pairs={{0,1},{1,2},{2,3},{3,0},{4,5},{5,6},{6,7},{7,4},{8,9},{9,10},{10,1... | collective-permute-start | bytes 61448 | tf_op jit(solution)/shard_map/while/body/eval_jaxpr/ppermute | solution.py:231
  58.2 10.7 %all-to-all-start = ((f32[8,32,128]{2,1,0:T(8,128)}), f32[8,32,128]{2,1,0:T(8,128)S(1)}, u32[]{:S(2)}, u32[]{:S(2)}) async-start(f32[8,32,128]{2,1,0:T(8,128)} %back.3), calls=%async_computation | async-start | bytes 262144 | tf_op jit(solution)/shard_map/while/body/eval_jaxpr/all_to_all | solution.py:236
  68.8 7.6 %copy-start.3 = (f32[32,2,128,128]{3,2,1,0:T(8,128)S(1)}, f32[32,2,128,128]{3,2,1,0:T(8,128)}, u32[]{:S(2)}) copy-start(f32[32,2,128,128]{3,2,1,0:T(8,128)} %get-tuple-element.252.jac) | copy-start | bytes 12582916 | tf_op jit(solution)/shard_map/while
  72.3 1.5 collective-permute-start.2
  72.3 3.8 %collective-permute-start.1 = (f32[40,128]{1,0:T(8,128)S(1)}, f32[40,128]{1,0:T(8,128)S(1)}, u32[]{:S(2)}, u32[]{:S(2)}) collective-permute-start(f32[40,128]{1,0:T(8,128)S(1)} %get-tuple-element.209.own), channel_id=1, source_target_pairs={{0,2},{1,3},{2,0},{3,1},{4,6},{5,7},{6,4},{7,5},{8,10},{9,11},{10,... | collective-permute-start | bytes 61448 | tf_op jit(solution)/shard_map/while/body/eval_jaxpr/ppermute | solution.py:231
  73.2 3.2 %collective-permute-start = (f32[40,128]{1,0:T(8,128)S(1)}, f32[40,128]{1,0:T(8,128)S(1)}, u32[]{:S(2)}, u32[]{:S(2)}) collective-permute-start(f32[40,128]{1,0:T(8,128)S(1)} %get-tuple-element.209.own), channel_id=1, source_target_pairs={{0,1},{1,2},{2,3},{3,0},{4,5},{5,6},{6,7},{7,4},{8,9},{9,10},{10,1... | collective-permute-start | bytes 61448 | tf_op jit(solution)/shard_map/while/body/eval_jaxpr/ppermute | solution.py:231
  78.5 10.7 %all-to-all-start = ((f32[8,32,128]{2,1,0:T(8,128)}), f32[8,32,128]{2,1,0:T(8,128)S(1)}, u32[]{:S(2)}, u32[]{:S(2)}) async-start(f32[8,32,128]{2,1,0:T(8,128)} %back.3), calls=%async_computation | async-start | bytes 262144 | tf_op jit(solution)/shard_map/while/body/eval_jaxpr/all_to_all | solution.py:236
  89.2 8.0 %copy-start.3 = (f32[32,2,128,128]{3,2,1,0:T(8,128)S(1)}, f32[32,2,128,128]{3,2,1,0:T(8,128)}, u32[]{:S(2)}) copy-start(f32[32,2,128,128]{3,2,1,0:T(8,128)} %get-tuple-element.252.jac) | copy-start | bytes 12582916 | tf_op jit(solution)/shard_map/while
  92.7 1.5 collective-permute-start.2
  92.7 3.8 %collective-permute-start.1 = (f32[40,128]{1,0:T(8,128)S(1)}, f32[40,128]{1,0:T(8,128)S(1)}, u32[]{:S(2)}, u32[]{:S(2)}) collective-permute-start(f32[40,128]{1,0:T(8,128)S(1)} %get-tuple-element.209.own), channel_id=1, source_target_pairs={{0,2},{1,3},{2,0},{3,1},{4,6},{5,7},{6,4},{7,5},{8,10},{9,11},{10,... | collective-permute-start | bytes 61448 | tf_op jit(solution)/shard_map/while/body/eval_jaxpr/ppermute | solution.py:231
  94.0 3.2 %collective-permute-start = (f32[40,128]{1,0:T(8,128)S(1)}, f32[40,128]{1,0:T(8,128)S(1)}, u32[]{:S(2)}, u32[]{:S(2)}) collective-permute-start(f32[40,128]{1,0:T(8,128)S(1)} %get-tuple-element.209.own), channel_id=1, source_target_pairs={{0,1},{1,2},{2,3},{3,0},{4,5},{5,6},{6,7},{7,4},{8,9},{9,10},{10,1... | collective-permute-start | bytes 61448 | tf_op jit(solution)/shard_map/while/body/eval_jaxpr/ppermute | solution.py:231
  99.4 10.7 %all-to-all-start = ((f32[8,32,128]{2,1,0:T(8,128)}), f32[8,32,128]{2,1,0:T(8,128)S(1)}, u32[]{:S(2)}, u32[]{:S(2)}) async-start(f32[8,32,128]{2,1,0:T(8,128)} %back.3), calls=%async_computation | async-start | bytes 262144 | tf_op jit(solution)/shard_map/while/body/eval_jaxpr/all_to_all | solution.py:236
  110.0 7.6 %copy-start.3 = (f32[32,2,128,128]{3,2,1,0:T(8,128)S(1)}, f32[32,2,128,128]{3,2,1,0:T(8,128)}, u32[]{:S(2)}) copy-start(f32[32,2,128,128]{3,2,1,0:T(8,128)} %get-tuple-element.252.jac) | copy-start | bytes 12582916 | tf_op jit(solution)/shard_map/while
  113.5 1.5 collective-permute-start.2
  113.6 3.8 %collective-permute-start.1 = (f32[40,128]{1,0:T(8,128)S(1)}, f32[40,128]{1,0:T(8,128)S(1)}, u32[]{:S(2)}, u32[]{:S(2)}) collective-permute-start(f32[40,128]{1,0:T(8,128)S(1)} %get-tuple-element.209.own), channel_id=1, source_target_pairs={{0,2},{1,3},{2,0},{3,1},{4,6},{5,7},{6,4},{7,5},{8,10},{9,11},{10,... | collective-permute-start | bytes 61448 | tf_op jit(solution)/shard_map/while/body/eval_jaxpr/ppermute | solution.py:231
  114.4 3.2 %collective-permute-start = (f32[40,128]{1,0:T(8,128)S(1)}, f32[40,128]{1,0:T(8,128)S(1)}, u32[]{:S(2)}, u32[]{:S(2)}) collective-permute-start(f32[40,128]{1,0:T(8,128)S(1)} %get-tuple-element.209.own), channel_id=1, source_target_pairs={{0,1},{1,2},{2,3},{3,0},{4,5},{5,6},{6,7},{7,4},{8,9},{9,10},{10,1... | collective-permute-start | bytes 61448 | tf_op jit(solution)/shard_map/while/body/eval_jaxpr/ppermute | solution.py:231
  119.8 10.7 %all-to-all-start = ((f32[8,32,128]{2,1,0:T(8,128)}), f32[8,32,128]{2,1,0:T(8,128)S(1)}, u32[]{:S(2)}, u32[]{:S(2)}) async-start(f32[8,32,128]{2,1,0:T(8,128)} %back.3), calls=%async_computation | async-start | bytes 262144 | tf_op jit(solution)/shard_map/while/body/eval_jaxpr/all_to_all | solution.py:236
  130.4 8.0 %copy-start.3 = (f32[32,2,128,128]{3,2,1,0:T(8,128)S(1)}, f32[32,2,128,128]{3,2,1,0:T(8,128)}, u32[]{:S(2)}) copy-start(f32[32,2,128,128]{3,2,1,0:T(8,128)} %get-tuple-element.252.jac) | copy-start | bytes 12582916 | tf_op jit(solution)/shard_map/while
  133.9 1.5 collective-permute-start.2
  133.9 3.8 %collective-permute-start.1 = (f32[40,128]{1,0:T(8,128)S(1)}, f32[40,128]{1,0:T(8,128)S(1)}, u32[]{:S(2)}, u32[]{:S(2)}) collective-permute-start(f32[40,128]{1,0:T(8,128)S(1)} %get-tuple-element.209.own), channel_id=1, source_target_pairs={{0,2},{1,3},{2,0},{3,1},{4,6},{5,7},{6,4},{7,5},{8,10},{9,11},{10,... | collective-permute-start | bytes 61448 | tf_op jit(solution)/shard_map/while/body/eval_jaxpr/ppermute | solution.py:231
  135.2 3.2 %collective-permute-start = (f32[40,128]{1,0:T(8,128)S(1)}, f32[40,128]{1,0:T(8,128)S(1)}, u32[]{:S(2)}, u32[]{:S(2)}) collective-permute-start(f32[40,128]{1,0:T(8,128)S(1)} %get-tuple-element.209.own), channel_id=1, source_target_pairs={{0,1},{1,2},{2,3},{3,0},{4,5},{5,6},{6,7},{7,4},{8,9},{9,10},{10,1... | collective-permute-start | bytes 61448 | tf_op jit(solution)/shard_map/while/body/eval_jaxpr/ppermute | solution.py:231
  140.6 10.7 %all-to-all-start = ((f32[8,32,128]{2,1,0:T(8,128)}), f32[8,32,128]{2,1,0:T(8,128)S(1)}, u32[]{:S(2)}, u32[]{:S(2)}) async-start(f32[8,32,128]{2,1,0:T(8,128)} %back.3), calls=%async_computation | async-start | bytes 262144 | tf_op jit(solution)/shard_map/while/body/eval_jaxpr/all_to_all | solution.py:236
  151.2 7.6 %copy-start.3 = (f32[32,2,128,128]{3,2,1,0:T(8,128)S(1)}, f32[32,2,128,128]{3,2,1,0:T(8,128)}, u32[]{:S(2)}) copy-start(f32[32,2,128,128]{3,2,1,0:T(8,128)} %get-tuple-element.252.jac) | copy-start | bytes 12582916 | tf_op jit(solution)/shard_map/while
  154.7 1.5 collective-permute-start.2
  154.8 3.8 %collective-permute-start.1 = (f32[40,128]{1,0:T(8,128)S(1)}, f32[40,128]{1,0:T(8,128)S(1)}, u32[]{:S(2)}, u32[]{:S(2)}) collective-permute-start(f32[40,128]{1,0:T(8,128)S(1)} %get-tuple-element.209.own), channel_id=1, source_target_pairs={{0,2},{1,3},{2,0},{3,1},{4,6},{5,7},{6,4},{7,5},{8,10},{9,11},{10,... | collective-permute-start | bytes 61448 | tf_op jit(solution)/shard_map/while/body/eval_jaxpr/ppermute | solution.py:231
  155.6 3.2 %collective-permute-start = (f32[40,128]{1,0:T(8,128)S(1)}, f32[40,128]{1,0:T(8,128)S(1)}, u32[]{:S(2)}, u32[]{:S(2)}) collective-permute-start(f32[40,128]{1,0:T(8,128)S(1)} %get-tuple-element.209.own), channel_id=1, source_target_pairs={{0,1},{1,2},{2,3},{3,0},{4,5},{5,6},{6,7},{7,4},{8,9},{9,10},{10,1... | collective-permute-start | bytes 61448 | tf_op jit(solution)/shard_map/while/body/eval_jaxpr/ppermute | solution.py:231
  161.0 10.7 %all-to-all-start = ((f32[8,32,128]{2,1,0:T(8,128)}), f32[8,32,128]{2,1,0:T(8,128)S(1)}, u32[]{:S(2)}, u32[]{:S(2)}) async-start(f32[8,32,128]{2,1,0:T(8,128)} %back.3), calls=%async_computation | async-start | bytes 262144 | tf_op jit(solution)/shard_map/while/body/eval_jaxpr/all_to_all | solution.py:236
  171.6 8.0 %copy-start.3 = (f32[32,2,128,128]{3,2,1,0:T(8,128)S(1)}, f32[32,2,128,128]{3,2,1,0:T(8,128)}, u32[]{:S(2)}) copy-start(f32[32,2,128,128]{3,2,1,0:T(8,128)} %get-tuple-element.252.jac) | copy-start | bytes 12582916 | tf_op jit(solution)/shard_map/while
  175.1 1.5 collective-permute-start.2
  175.2 3.8 %collective-permute-start.1 = (f32[40,128]{1,0:T(8,128)S(1)}, f32[40,128]{1,0:T(8,128)S(1)}, u32[]{:S(2)}, u32[]{:S(2)}) collective-permute-start(f32[40,128]{1,0:T(8,128)S(1)} %get-tuple-element.209.own), channel_id=1, source_target_pairs={{0,2},{1,3},{2,0},{3,1},{4,6},{5,7},{6,4},{7,5},{8,10},{9,11},{10,... | collective-permute-start | bytes 61448 | tf_op jit(solution)/shard_map/while/body/eval_jaxpr/ppermute | solution.py:231
  176.5 3.2 %collective-permute-start = (f32[40,128]{1,0:T(8,128)S(1)}, f32[40,128]{1,0:T(8,128)S(1)}, u32[]{:S(2)}, u32[]{:S(2)}) collective-permute-start(f32[40,128]{1,0:T(8,128)S(1)} %get-tuple-element.209.own), channel_id=1, source_target_pairs={{0,1},{1,2},{2,3},{3,0},{4,5},{5,6},{6,7},{7,4},{8,9},{9,10},{10,1... | collective-permute-start | bytes 61448 | tf_op jit(solution)/shard_map/while/body/eval_jaxpr/ppermute | solution.py:231
  181.8 10.7 %all-to-all-start = ((f32[8,32,128]{2,1,0:T(8,128)}), f32[8,32,128]{2,1,0:T(8,128)S(1)}, u32[]{:S(2)}, u32[]{:S(2)}) async-start(f32[8,32,128]{2,1,0:T(8,128)} %back.3), calls=%async_computation | async-start | bytes 262144 | tf_op jit(solution)/shard_map/while/body/eval_jaxpr/all_to_all | solution.py:236
  192.4 7.6 %copy-start.3 = (f32[32,2,128,128]{3,2,1,0:T(8,128)S(1)}, f32[32,2,128,128]{3,2,1,0:T(8,128)}, u32[]{:S(2)}) copy-start(f32[32,2,128,128]{3,2,1,0:T(8,128)} %get-tuple-element.252.jac) | copy-start | bytes 12582916 | tf_op jit(solution)/shard_map/while
  195.9 1.5 collective-permute-start.2
  196.0 3.8 %collective-permute-start.1 = (f32[40,128]{1,0:T(8,128)S(1)}, f32[40,128]{1,0:T(8,128)S(1)}, u32[]{:S(2)}, u32[]{:S(2)}) collective-permute-start(f32[40,128]{1,0:T(8,128)S(1)} %get-tuple-element.209.own), channel_id=1, source_target_pairs={{0,2},{1,3},{2,0},{3,1},{4,6},{5,7},{6,4},{7,5},{8,10},{9,11},{10,... | collective-permute-start | bytes 61448 | tf_op jit(solution)/shard_map/while/body/eval_jaxpr/ppermute | solution.py:231
  196.8 3.2 %collective-permute-start = (f32[40,128]{1,0:T(8,128)S(1)}, f32[40,128]{1,0:T(8,128)S(1)}, u32[]{:S(2)}, u32[]{:S(2)}) collective-permute-start(f32[40,128]{1,0:T(8,128)S(1)} %get-tuple-element.209.own), channel_id=1, source_target_pairs={{0,1},{1,2},{2,3},{3,0},{4,5},{5,6},{6,7},{7,4},{8,9},{9,10},{10,1... | collective-permute-start | bytes 61448 | tf_op jit(solution)/shard_map/while/body/eval_jaxpr/ppermute | solution.py:231
  202.2 10.7 %all-to-all-start = ((f32[8,32,128]{2,1,0:T(8,128)}), f32[8,32,128]{2,1,0:T(8,128)S(1)}, u32[]{:S(2)}, u32[]{:S(2)}) async-start(f32[8,32,128]{2,1,0:T(8,128)} %back.3), calls=%async_computation | async-start | bytes 262144 | tf_op jit(solution)/shard_map/while/body/eval_jaxpr/all_to_all | solution.py:236
  212.8 8.0 %copy-start.3 = (f32[32,2,128,128]{3,2,1,0:T(8,128)S(1)}, f32[32,2,128,128]{3,2,1,0:T(8,128)}, u32[]{:S(2)}) copy-start(f32[32,2,128,128]{3,2,1,0:T(8,128)} %get-tuple-element.252.jac) | copy-start | bytes 12582916 | tf_op jit(solution)/shard_map/while
  216.3 1.5 collective-permute-start.2
  216.4 3.8 %collective-permute-start.1 = (f32[40,128]{1,0:T(8,128)S(1)}, f32[40,128]{1,0:T(8,128)S(1)}, u32[]{:S(2)}, u32[]{:S(2)}) collective-permute-start(f32[40,128]{1,0:T(8,128)S(1)} %get-tuple-element.209.own), channel_id=1, source_target_pairs={{0,2},{1,3},{2,0},{3,1},{4,6},{5,7},{6,4},{7,5},{8,10},{9,11},{10,... | collective-permute-start | bytes 61448 | tf_op jit(solution)/shard_map/while/body/eval_jaxpr/ppermute | solution.py:231
  217.7 3.2 %collective-permute-start = (f32[40,128]{1,0:T(8,128)S(1)}, f32[40,128]{1,0:T(8,128)S(1)}, u32[]{:S(2)}, u32[]{:S(2)}) collective-permute-start(f32[40,128]{1,0:T(8,128)S(1)} %get-tuple-element.209.own), channel_id=1, source_target_pairs={{0,1},{1,2},{2,3},{3,0},{4,5},{5,6},{6,7},{7,4},{8,9},{9,10},{10,1... | collective-permute-start | bytes 61448 | tf_op jit(solution)/shard_map/while/body/eval_jaxpr/ppermute | solution.py:231
  223.0 10.7 %all-to-all-start = ((f32[8,32,128]{2,1,0:T(8,128)}), f32[8,32,128]{2,1,0:T(8,128)S(1)}, u32[]{:S(2)}, u32[]{:S(2)}) async-start(f32[8,32,128]{2,1,0:T(8,128)} %back.3), calls=%async_computation | async-start | bytes 262144 | tf_op jit(solution)/shard_map/while/body/eval_jaxpr/all_to_all | solution.py:236
  233.7 7.6 %copy-start.3 = (f32[32,2,128,128]{3,2,1,0:T(8,128)S(1)}, f32[32,2,128,128]{3,2,1,0:T(8,128)}, u32[]{:S(2)}) copy-start(f32[32,2,128,128]{3,2,1,0:T(8,128)} %get-tuple-element.252.jac) | copy-start | bytes 12582916 | tf_op jit(solution)/shard_map/while
  237.1 1.5 collective-permute-start.2
  237.2 3.8 %collective-permute-start.1 = (f32[40,128]{1,0:T(8,128)S(1)}, f32[40,128]{1,0:T(8,128)S(1)}, u32[]{:S(2)}, u32[]{:S(2)}) collective-permute-start(f32[40,128]{1,0:T(8,128)S(1)} %get-tuple-element.209.own), channel_id=1, source_target_pairs={{0,2},{1,3},{2,0},{3,1},{4,6},{5,7},{6,4},{7,5},{8,10},{9,11},{10,... | collective-permute-start | bytes 61448 | tf_op jit(solution)/shard_map/while/body/eval_jaxpr/ppermute | solution.py:231
  238.0 3.2 %collective-permute-start = (f32[40,128]{1,0:T(8,128)S(1)}, f32[40,128]{1,0:T(8,128)S(1)}, u32[]{:S(2)}, u32[]{:S(2)}) collective-permute-start(f32[40,128]{1,0:T(8,128)S(1)} %get-tuple-element.209.own), channel_id=1, source_target_pairs={{0,1},{1,2},{2,3},{3,0},{4,5},{5,6},{6,7},{7,4},{8,9},{9,10},{10,1... | collective-permute-start | bytes 61448 | tf_op jit(solution)/shard_map/while/body/eval_jaxpr/ppermute | solution.py:231
  243.4 10.7 %all-to-all-start = ((f32[8,32,128]{2,1,0:T(8,128)}), f32[8,32,128]{2,1,0:T(8,128)S(1)}, u32[]{:S(2)}, u32[]{:S(2)}) async-start(f32[8,32,128]{2,1,0:T(8,128)} %back.3), calls=%async_computation | async-start | bytes 262144 | tf_op jit(solution)/shard_map/while/body/eval_jaxpr/all_to_all | solution.py:236
  254.0 8.0 %copy-start.3 = (f32[32,2,128,128]{3,2,1,0:T(8,128)S(1)}, f32[32,2,128,128]{3,2,1,0:T(8,128)}, u32[]{:S(2)}) copy-start(f32[32,2,128,128]{3,2,1,0:T(8,128)} %get-tuple-element.252.jac) | copy-start | bytes 12582916 | tf_op jit(solution)/shard_map/while
  257.5 1.5 collective-permute-start.2
  257.6 3.8 %collective-permute-start.1 = (f32[40,128]{1,0:T(8,128)S(1)}, f32[40,128]{1,0:T(8,128)S(1)}, u32[]{:S(2)}, u32[]{:S(2)}) collective-permute-start(f32[40,128]{1,0:T(8,128)S(1)} %get-tuple-element.209.own), channel_id=1, source_target_pairs={{0,2},{1,3},{2,0},{3,1},{4,6},{5,7},{6,4},{7,5},{8,10},{9,11},{10,... | collective-permute-start | bytes 61448 | tf_op jit(solution)/shard_map/while/body/eval_jaxpr/ppermute | solution.py:231
  258.9 3.2 %collective-permute-start = (f32[40,128]{1,0:T(8,128)S(1)}, f32[40,128]{1,0:T(8,128)S(1)}, u32[]{:S(2)}, u32[]{:S(2)}) collective-permute-start(f32[40,128]{1,0:T(8,128)S(1)} %get-tuple-element.209.own), channel_id=1, source_target_pairs={{0,1},{1,2},{2,3},{3,0},{4,5},{5,6},{6,7},{7,4},{8,9},{9,10},{10,1... | collective-permute-start | bytes 61448 | tf_op jit(solution)/shard_map/while/body/eval_jaxpr/ppermute | solution.py:231
  264.2 10.7 %all-to-all-start = ((f32[8,32,128]{2,1,0:T(8,128)}), f32[8,32,128]{2,1,0:T(8,128)S(1)}, u32[]{:S(2)}, u32[]{:S(2)}) async-start(f32[8,32,128]{2,1,0:T(8,128)} %back.3), calls=%async_computation | async-start | bytes 262144 | tf_op jit(solution)/shard_map/while/body/eval_jaxpr/all_to_all | solution.py:236
  (1 other events, 0.7 us)

commit v2 on v1

v2 whole, which is shorter than its diff:
```python
import functools
import jax
import jax.numpy as jnp
from jax import lax
from jax.experimental import pallas as pl
from jax.experimental.pallas import tpu as pltpu
from jax.sharding import PartitionSpec as P

ITERS = 12
SUB = 8
SPOTS = {(2, 1): 0, (1, 0): 0, (1, 1): 1, (-1, -1): 0, (-1, 0): 1, (-2, -1): 1}
VMEM_LIMIT = 16 * 1024 * 1024
BANKS = 4
PIECES = 8

vmem = pl.BlockSpec(memory_space=pltpu.VMEM)
anywhere = pl.BlockSpec(memory_space=pl.ANY)
hbm = pl.BlockSpec(memory_space=pltpu.HBM)


def rows8(ref_value):
    return ref_value.reshape(-1, SUB, ref_value.shape[-1])


def diagonal(width):
    row = lax.broadcasted_iota(jnp.int32, (width, width), 0)
    lane = lax.broadcasted_iota(jnp.int32, (width, width), 1)
    return rows8(row == lane)


def as_column(row, eye):
    spread = jnp.where(eye, row[None], 0.0)
    return jnp.sum(spread, axis=-1, keepdims=True)


def lane_total(value):
    return jnp.sum(jnp.sum(value, axis=0, keepdims=True), axis=1, keepdims=True)


def copy_in(source, target, sem):
    return pltpu.make_async_copy(source, target, sem)


def forward(jac, index, spread, rows):
    tiles, slots, width, _ = jac.shape
    eye = diagonal(width)
    for t in range(tiles):
        total = None
        for j in range(slots):
            term = rows8(jac[t, j]) * spread[index[t * slots + j]][None]
            total = term if total is None else total + term
        total = jnp.sum(total, axis=-1, keepdims=True)
        rows[t : t + 1, :] = jnp.sum(
            jnp.sum(jnp.where(eye, total, 0.0), axis=0), axis=0, keepdims=True
        )


def backward(jac, chosen, weighted, banks, back, ready, square, arrived=lambda t: None):
    tiles, slots, width, _ = jac.shape
    eye = diagonal(width)
    banks[...] = jnp.zeros_like(banks)

    def add(t):
        for j in range(slots):
            where = ((t * slots + j) % BANKS, chosen(t, j))
            banks[where] += back[t * slots + j]

    half = tiles // 2
    for t in range(tiles):
        arrived(t)
        if t == half:
            ready()
            for early in range(half):
                add(early)
        column = as_column(weighted[t : t + 1, :], eye)
        for j in range(slots):
            block = rows8(jac[t, j])
            if square:
                block = block * block
            back[t * slots + j] = jnp.sum(block * column, axis=0)
        if t >= half:
            add(t)
    total = banks[0]
    for bank in range(1, BANKS):
        total = total + banks[bank]
    return jnp.sum(total, axis=1)


def publish(chunk, out):
    for member in range(out.shape[0]):
        out[member] = chunk


def place_blocks(out, keep, columns, scalars):
    regions, per_dev = out.shape[0], columns.shape[0] // 3
    region = lax.axis_index("region")
    first, middle, last = (
        columns[n * per_dev : (n + 1) * per_dev] for n in range(3)
    )
    keep[...] = jnp.concatenate([columns, scalars], axis=0)
    blank = jnp.concatenate([jnp.zeros_like(first)] * 2 + [scalars], axis=0)
    for away in range(3, regions - 2):
        out[lax.rem(region + away, regions)] = blank
    zero = jnp.zeros_like(first)
    for away, pair in (
        (-2, (first, zero)), (-1, (first, middle)), (1, (middle, last)), (2, (zero, last)),
    ):
        target = lax.rem(region + (away + regions), regions)
        out[target] = jnp.concatenate([*pair, scalars], axis=0)
    out[region] = blank


def diag_kernel(jac, vectors, *refs):
    ins, refs = refs[:-10], refs[-10:]
    out, weight, place, held, fits, index, small, banks, back, sems = refs
    tiles, slots = jac.shape[:2]
    blocks = len(ins)
    per_dev = tiles // blocks
    step = tiles // PIECES
    pieces = [
        copy_in(
            jac.at[pl.ds(n * step, step)], held.at[pl.ds(n * step, step)], sems.at[n]
        )
        for n in range(PIECES)
    ]
    for copy in pieces:
        copy.start()
    group = lax.axis_index("blk")
    for shift, part in enumerate(ins):
        source = lax.rem(group + (blocks - shift), blocks)
        spot = pl.ds(pl.multiple_of(source * per_dev, per_dev), per_dev)
        weight[spot, :] = part[:per_dev, :]
        fits[spot, :] = part[per_dev:, :].astype(jnp.int32)
    table = copy_in(fits, index, sems.at[PIECES])
    table.start()
    listed = copy_in(small, place, sems.at[PIECES + 1])

    def ready():
        table.wait()
        for t in range(tiles):
            for j in range(slots):
                small[t * slots + j] = index[t, group * slots + j]
        listed.start()

    def arrived(t):
        if t % step == 0:
            pieces[t // step].wait()

    squares = backward(
        held, lambda t, j: small[t * slots + j], weight, banks, back, ready, True, arrived
    )
    publish(jnp.concatenate([squares, vectors[...]], axis=0), out)
    listed.wait()


def back_kernel(place, jac, weight, own, *refs):
    others, refs = refs[:-7], refs[-7:]
    out, keep, weighted, banks, back, index, sem = refs
    copy = copy_in(place, index, sem)
    copy.start()
    tiles, slots = jac.shape[:2]
    parts = [own] + list(others)
    even, odd = None, None
    for shift, part in enumerate(parts):
        if shift % 2 == 0:
            even = part[...] if even is None else even + part[...]
        else:
            odd = part[...] if odd is None else odd + part[...]
    total = even if odd is None else even + odd
    rows, sums = total[:tiles], total[tiles:]
    weighted[...] = weight[...] * rows
    delta = jnp.sum(weighted[...] * rows, axis=0, keepdims=True) + sums[1:2]
    scalars = jnp.concatenate([sums[:1], delta, sums[2:]], axis=0)
    columns = backward(
        jac, lambda t, j: index[t * slots + j], weighted, banks, back, copy.wait, False
    )
    place_blocks(out, keep, columns, scalars)


def send_rows(jac, index, resid, scaled, diag, spread, own, out):
    tiles = jac.shape[0]
    spread[...] = jnp.broadcast_to(scaled[:, None, :], spread.shape)
    forward(jac, index, spread, out)
    r, z, d = resid[own], scaled[own], diag[own]
    gamma = jnp.sum(r * z, axis=0, keepdims=True)
    delta = jnp.sum(d * z * z, axis=0, keepdims=True)
    pad = jnp.zeros((SUB - 2, z.shape[1]), jnp.float32)
    out[tiles:, :] = jnp.concatenate([gamma, delta, pad], axis=0)


def gathered(received, region, regions, per_dev):
    blocks = []
    for offset in (-1, 0, 1):
        total = None
        for e in (-1, 0, 1):
            source = lax.rem(region + (offset + e + regions), regions)
            start = (1 - e) * per_dev
            term = received[source, start : start + per_dev, :]
            total = term if total is None else total + term
        blocks.append(total)
    return jnp.concatenate(blocks, axis=0)


def halo(received, region, regions, start, per_dev):
    blocks = []
    for offset in (-1, 0, 1):
        source = lax.rem(region + (offset + regions), regions)
        blocks.append(received[source, start : start + per_dev, :])
    return jnp.concatenate(blocks, axis=0)


def first_kernel(
    place, jac, received, out, diag, precond, resid, spread, index, sem
):
    copy = copy_in(place, index, sem)
    copy.start()
    regions = received.shape[0]
    per_dev = diag.shape[0] // 3
    region = lax.axis_index("region")
    extent = 3 * per_dev
    d = halo(received, region, regions, extent, per_dev)
    r = halo(received, region, regions, extent + per_dev, per_dev)
    m = d + gathered(received, region, regions, per_dev)
    diag[...] = d
    precond[...] = m
    resid[...] = r
    own = slice(per_dev, 2 * per_dev)
    copy.wait()
    send_rows(jac, index, r, r / m, d, spread, own, out)


def collected(received, kept, per_dev):
    regions = received.shape[0]
    region = lax.axis_index("region")
    blocks = []
    for offset in (-1, 0, 1):
        total = None
        for e in (-1, 0, 1):
            away = offset + e
            if away == 0:
                start = (1 - e) * per_dev
                term = kept[start : start + per_dev, :]
            else:
                source = lax.rem(region + (away + regions), regions)
                start = SPOTS[away, offset] * per_dev
                term = received[source, start : start + per_dev, :]
            total = term if total is None else total + term
        blocks.append(total)
    return jnp.concatenate(blocks, axis=0)


def update(received, kept, diag, precond, resid, along, direct, answer, scal):
    regions = received.shape[0]
    per_dev = direct.shape[0]
    r, d, m = resid[...], diag[...], precond[...]
    z = r / m
    image = d * z + collected(received, kept, per_dev)
    region = lax.axis_index("region")
    sums = None
    for member in range(regions):
        term = jnp.where(
            region == member, kept[3 * per_dev :, :], received[member, 2 * per_dev :, :]
        )
        sums = term if sums is None else sums + term
    sums = jnp.sum(sums, axis=1, keepdims=True)
    gamma, delta = sums[:1], sums[1:2]
    before, alpha = scal[0:1, :1], scal[1:2, :1]
    started = alpha != 0.0
    beta = jnp.where(started, gamma / jnp.where(started, before, 1.0), 0.0)
    fall = jnp.where(started, beta * gamma / jnp.where(started, alpha, 1.0), 0.0)
    alpha = gamma / (delta - fall)
    s = image + beta * along[...]
    p = z[per_dev : 2 * per_dev] + beta * direct[...]
    x = answer[...] + alpha * p
    return x, r - alpha * s, s, p, gamma, alpha


def step_kernel(
    place, jac, received, kept, diag, precond, resid, along, direct, answer, scal,
    out, resid_o, along_o, direct_o, answer_o, scal_o, spread, index, sem,
):
    copy = copy_in(place, index, sem)
    copy.start()
    per_dev = direct.shape[0]
    x, r, s, p, gamma, alpha = update(
        received, kept, diag, precond, resid, along, direct, answer, scal
    )
    resid_o[...] = r
    along_o[...] = s
    direct_o[...] = p
    answer_o[...] = x
    scal_o[0:1, :] = jnp.broadcast_to(gamma, (1, scal_o.shape[1]))
    scal_o[1:2, :] = jnp.broadcast_to(alpha, (1, scal_o.shape[1]))
    own = slice(per_dev, 2 * per_dev)
    copy.wait()
    send_rows(jac, index, r, r / precond[...], diag, spread, own, out)


def last_kernel(
    received, kept, diag, precond, resid, along, direct, answer, scal, answer_o,
    resid_o,
):
    per_dev = direct.shape[0]
    x, r, _, _, _, _ = update(
        received, kept, diag, precond, resid, along, direct, answer, scal
    )
    answer_o[...] = x
    resid_o[...] = r[per_dev : 2 * per_dev]


def call(kernel, outs, scratch, specs, name, flops, moved, limit=VMEM_LIMIT):
    outs = [
        shape
        if isinstance(shape, jax.ShapeDtypeStruct)
        else jax.ShapeDtypeStruct(shape, jnp.float32)
        for shape in outs
    ]
    return pl.pallas_call(
        kernel,
        out_shape=outs,
        in_specs=specs,
        out_specs=[vmem] * len(outs),
        scratch_shapes=scratch,
        compiler_params=pltpu.CompilerParams(vmem_limit_bytes=limit),
        cost_estimate=pl.CostEstimate(
            flops=flops, bytes_accessed=moved, transcendentals=0
        ),
        name=name,
    )


def body(jac, pattern, branch_weight, bus_diag, right_side):
    blocks = lax.axis_size("blk")
    regions = lax.axis_size("region")
    per_dev, width = right_side.shape
    tiles, slots = jac.shape[:2]
    extent = 3 * per_dev
    f32 = jnp.float32

    def across_blk(value):
        return [
            lax.ppermute(value, "blk", [(i, (i + k) % blocks) for i in range(blocks)])
            for k in range(1, blocks)
        ]

    def across_region(chunks):
        return lax.all_to_all(chunks, "region", 0, 0, tiled=True)

    flops = 4 * jac.size
    moved = 4 * jac.size
    row_count = tiles + SUB
    spread = pltpu.VMEM((extent, SUB, width), f32)
    banks = pltpu.VMEM((BANKS, extent, SUB, width), f32)
    back = pltpu.VMEM((tiles * slots, SUB, width), f32)
    table = [pltpu.SMEM((tiles * slots,), jnp.int32), pltpu.SemaphoreType.DMA]
    chunk = (regions, 2 * per_dev + SUB, width)
    kept_shape = (extent + SUB, width)
    halo_shape, own_shape = (extent, width), (per_dev, width)

    fits = jnp.pad(pattern, ((0, 0), (0, width - pattern.shape[1]))).astype(f32)
    vectors = jnp.concatenate([bus_diag, right_side], axis=0)
    mine = jnp.concatenate([branch_weight, fits], axis=0)
    setup, weight, place, jac = call(
        diag_kernel,
        [
            (regions, extent + 2 * per_dev, width), (tiles, width),
            jax.ShapeDtypeStruct((tiles * slots,), jnp.int32), jac.shape,
        ],
        [
            pltpu.VMEM((tiles, width), jnp.int32), pltpu.SMEM((tiles, width), jnp.int32),
            pltpu.SMEM((tiles * slots,), jnp.int32), banks, back,
            pltpu.SemaphoreType.DMA((PIECES + 2,)),
        ],
        [hbm] + [vmem] * (1 + blocks), "diagonal", flops, moved, 47 * 1024 * 1024,
    )(jac, vectors, mine, *across_blk(mine))
    setup = across_region(setup)
    out, diag, precond, resid = call(
        first_kernel, [(row_count, width), halo_shape, halo_shape, halo_shape],
        [spread] + table, [anywhere, vmem, vmem],
        "first", flops, moved,
    )(place, jac, setup)

    def image_of(out):
        parts = across_blk(out)
        chunks, kept = call(
            back_kernel, [chunk, kept_shape], [pltpu.VMEM((tiles, width), f32), banks, back] + table,
            [anywhere] + [vmem] * (3 + len(parts)),
            "back", flops, moved,
        )(place, jac, weight, out, *parts)
        return across_region(chunks), kept

    def step(carry):
        received, kept, resid, along, direct, answer, scal = carry
        out, resid, along, direct, answer, scal = call(
            step_kernel,
            [(row_count, width), halo_shape, halo_shape, own_shape, own_shape, (SUB, width)],
            [spread] + table, [anywhere] + [vmem] * 10,
            "step", flops, moved,
        )(place, jac, received, kept, diag, precond, resid, along, direct, answer, scal)
        return *image_of(out), resid, along, direct, answer, scal

    carry = (
        *image_of(out), resid, jnp.zeros(halo_shape, f32), jnp.zeros(own_shape, f32),
        jnp.zeros(own_shape, f32), jnp.zeros((SUB, width), f32),
    )
    for _ in range(ITERS - 1):
        carry = step(carry)
    received, kept, resid, along, direct, answer, scal = carry
    answer, resid = call(
        last_kernel, [own_shape, own_shape], [], [vmem] * 9, "last", 1000, 1000
    )(received, kept, diag, precond, resid, along, direct, answer, scal)
    return answer, resid


def solution(mesh):
    both = P(("region", "blk"), None)
    return jax.shard_map(
        body,
        mesh=mesh,
        in_specs=(P("region", "blk", None, None), both, both, both, both),
        out_specs=(both, both),
        check_vma=False,
    )
```

time: 277 us -> 224 us (0.81)
  blocking collectives: 10.6 us -> 136 us
  waiting for transfers between devices: 127 us -> 20 us
  Pallas kernels: 70.3 us -> 29.3 us
  starting transfers between devices: 63 us -> 34.6 us
    all_to_all x1 -> x13, blocking collectives: 10.6 us -> 136 us  [across_region(): return lax.all_to_all(chunks, 'region', 0, 0, tiled=True)]
    all_to_all x12 -> x0, waiting for transfers between devices: 88.3 us -> none  [across_region(): return lax.all_to_all(chunks, 'region', 0, 0, tiled=True)]
    all_to_all x12 -> x0, starting transfers between devices: 42.9 us -> none  [across_region(): return lax.all_to_all(chunks, 'region', 0, 0, tiled=True)]
    pallas_call x11, Pallas kernels: 37.7 us -> 13.4 us  [step(): call(step_kernel, [(row_count, width), halo_shape, halo_shape, own_shape,...]
    ppermute x39, waiting for transfers between devices: 38.4 us -> 20 us  [across_blk(): lax.ppermute(value, 'blk', [(i, (i + k) % blocks) for i in range(blocks)])]
    pallas_call x14, Pallas kernels: 29.4 us -> 14.6 us  [the longest x12 11.4 us: image_of(): call(back_kernel, [chunk, kept_shape], [pltpu.VMEM((tiles, width), f32),...]
    ppermute x39, starting transfers between devices: 20.1 us -> 34.6 us  [across_blk(): lax.ppermute(value, 'blk', [(i, (i + k) % blocks) for i in range(blocks)])]
  transfers between devices with their start and end apart: 51 -> 39, of which waited for: 42 -> 28; matrix products, arithmetic and copies ran while one was open for 0% -> 0% of each run, Pallas kernels for 0% -> 0%
where the time goes in v2:
time: 224 us; the launch traced here: 223 us
  blocking collectives  136 us (61%)
  starting transfers between devices  34.6 us (15%)
  Pallas kernels  29.3 us (13%)
  waiting for transfers between devices  20 us (9%)
    all_to_all x13, blocking collectives, across_region(): return lax.all_to_all(chunks, 'region', 0, 0, tiled=True)  136 us
    ppermute x39, starting transfers between devices, across_blk(): lax.ppermute(value, 'blk', [(i, (i + k) % blocks) for i in range(blocks)])  34.6 us
    ppermute x39, waiting for transfers between devices, across_blk(): lax.ppermute(value, 'blk', [(i, (i + k) % blocks) for i in range(blocks)])  20 us
    pallas_call x11, Pallas kernels, step(): call(step_kernel, [(row_count, width), halo_shape, halo_shape, own_shape,...  13.4 us
    pallas_call x12, Pallas kernels, image_of(): call(back_kernel, [chunk, kept_shape], [pltpu.VMEM((tiles, width), f32),...  11.4 us
  transfers between devices with their start and end apart: 39, of which 28 were waited for; matrix products, arithmetic and copies ran while one was open for 0% of the time, Pallas kernels for 0%

profile of v2, /device:TPU:0, one launch (start us, length us, event | category | flops | bytes accessed | tf_op | source)
XLA Modules:
  0.0 223.1 jit_solution(16316673645817027767)
XLA Ops:
  2.5 2.5 %collective-permute-start.1 = (f32[16,128]{1,0:T(8,128)S(1)}, f32[16,128]{1,0:T(8,128)S(1)}, u32[]{:S(2)}, u32[]{:S(2)}) collective-permute-start(f32[16,128]{1,0:T(8,128)S(1)} %pad_maximum_fusion.1.refs_0_), channel_id=1, source_target_pairs={{0,2},{1,3},{2,0},{3,1},{4,6},{5,7},{6,4},{7,5},{8,10},{9,11},{10,... | collective-permute-start | bytes 24584 | tf_op jit(solution)/shard_map/ppermute | solution.py:342
  5.0 1.5 collective-permute-start.2
  7.8 2.5 %diagonal.1 = (f32[8,40,128]{2,1,0:T(8,128)S(1)}, f32[32,128]{1,0:T(8,128)S(1)}, s32[64]{0:T(128)S(1)}, f32[32,2,128,128]{3,2,1,0:T(8,128)S(1)}) custom-call(f32[32,2,128,128]{3,2,1,0:T(8,128)} %jac.1, f32[16,128]{1,0:T(8,128)S(1)} %pad_maximum_fusion.vectors, f32[16,128]{1,0:T(8,128)S(1)} %pad_maximum_fusion.1.refs_0_, ...), custom_call_target="tpu_custom_call" | custom-call | flops 4194304 | bytes 4194304 | tf_op jit(solution)/shard_map/diagonal/pallas_call | solution.py:363
  10.3 13.9 %all_to_all.65.received = f32[8,40,128]{2,1,0:T(8,128)S(1)} all-to-all(f32[8,40,128]{2,1,0:T(8,128)S(1)} %get-tuple-element.103), channel_id=1, replica_groups=mesh['region'=8,'blk'=4] {'region'}, dimensions={0} | all-to-all | bytes 327680 | tf_op jit(solution)/shard_map/all_to_all | solution.py:347
  24.2 1.2 first.1
  25.5 1.3 collective-permute-start.4
  26.8 1.4 collective-permute-start.5
  29.6 0.9 back.12
  30.6 10.3 %all_to_all.66.received = f32[8,24,128]{2,1,0:T(8,128)S(1)} all-to-all(f32[8,24,128]{2,1,0:T(8,128)S(1)} %get-tuple-element.105), channel_id=1, replica_groups=mesh['region'=8,'blk'=4] {'region'}, dimensions={0} | all-to-all | bytes 196608 | tf_op jit(solution)/shard_map/all_to_all | solution.py:347
  40.9 1.2 step.11
  42.2 1.5 collective-permute-start.7
  43.7 1.4 collective-permute-start.8
  46.6 0.9 back.13
  47.5 10.0 %all_to_all.67.received = f32[8,24,128]{2,1,0:T(8,128)S(1)} all-to-all(f32[8,24,128]{2,1,0:T(8,128)S(1)} %get-tuple-element.111), channel_id=1, replica_groups=mesh['region'=8,'blk'=4] {'region'}, dimensions={0} | all-to-all | bytes 196608 | tf_op jit(solution)/shard_map/all_to_all | solution.py:347
  57.6 1.2 step.12
  58.9 1.0 collective-permute-start.10
  59.8 1.3 collective-permute-start.11
  61.1 0.9 collective-permute-done.9.refs_0_
  62.8 0.9 back.14
  63.8 10.1 %all_to_all.68.received = f32[8,24,128]{2,1,0:T(8,128)S(1)} all-to-all(f32[8,24,128]{2,1,0:T(8,128)S(1)} %get-tuple-element.119), channel_id=1, replica_groups=mesh['region'=8,'blk'=4] {'region'}, dimensions={0} | all-to-all | bytes 196608 | tf_op jit(solution)/shard_map/all_to_all | solution.py:347
  73.9 1.2 step.13
  75.3 1.1 collective-permute-start.13
  76.4 1.4 collective-permute-start.14
  79.2 0.9 back.15
  80.2 10.3 %all_to_all.69.received = f32[8,24,128]{2,1,0:T(8,128)S(1)} all-to-all(f32[8,24,128]{2,1,0:T(8,128)S(1)} %get-tuple-element.127), channel_id=1, replica_groups=mesh['region'=8,'blk'=4] {'region'}, dimensions={0} | all-to-all | bytes 196608 | tf_op jit(solution)/shard_map/all_to_all | solution.py:347
  90.5 1.2 step.14
  91.8 1.0 collective-permute-start.16
  92.8 1.4 collective-permute-start.17
  95.8 0.9 back.16
  96.8 10.1 %all_to_all.70.received = f32[8,24,128]{2,1,0:T(8,128)S(1)} all-to-all(f32[8,24,128]{2,1,0:T(8,128)S(1)} %get-tuple-element.135), channel_id=1, replica_groups=mesh['region'=8,'blk'=4] {'region'}, dimensions={0} | all-to-all | bytes 196608 | tf_op jit(solution)/shard_map/all_to_all | solution.py:347
  106.9 1.2 step.15
  108.3 1.0 collective-permute-start.19
  109.3 1.4 collective-permute-start.20
  112.2 0.9 back.17
  113.2 10.3 %all_to_all.71.received = f32[8,24,128]{2,1,0:T(8,128)S(1)} all-to-all(f32[8,24,128]{2,1,0:T(8,128)S(1)} %get-tuple-element.143), channel_id=1, replica_groups=mesh['region'=8,'blk'=4] {'region'}, dimensions={0} | all-to-all | bytes 196608 | tf_op jit(solution)/shard_map/all_to_all | solution.py:347
  123.5 1.2 step.16
  124.8 1.0 collective-permute-start.22
  125.8 1.4 collective-permute-start.23
  128.8 0.9 back.18
  129.8 10.1 %all_to_all.72.received = f32[8,24,128]{2,1,0:T(8,128)S(1)} all-to-all(f32[8,24,128]{2,1,0:T(8,128)S(1)} %get-tuple-element.151), channel_id=1, replica_groups=mesh['region'=8,'blk'=4] {'region'}, dimensions={0} | all-to-all | bytes 196608 | tf_op jit(solution)/shard_map/all_to_all | solution.py:347
  139.9 1.2 step.17
  141.3 1.0 collective-permute-start.25
  142.3 1.4 collective-permute-start.26
  145.3 0.9 back.19
  146.2 10.3 %all_to_all.73.received = f32[8,24,128]{2,1,0:T(8,128)S(1)} all-to-all(f32[8,24,128]{2,1,0:T(8,128)S(1)} %get-tuple-element.159), channel_id=1, replica_groups=mesh['region'=8,'blk'=4] {'region'}, dimensions={0} | all-to-all | bytes 196608 | tf_op jit(solution)/shard_map/all_to_all | solution.py:347
  156.5 1.2 step.18
  158.7 1.4 collective-permute-start.29
  160.0 0.9 collective-permute-done.27.refs_0_
  161.7 0.9 back.20
  162.7 10.2 %all_to_all.74.received = f32[8,24,128]{2,1,0:T(8,128)S(1)} all-to-all(f32[8,24,128]{2,1,0:T(8,128)S(1)} %get-tuple-element.167), channel_id=1, replica_groups=mesh['region'=8,'blk'=4] {'region'}, dimensions={0} | all-to-all | bytes 196608 | tf_op jit(solution)/shard_map/all_to_all | solution.py:347
  172.9 1.2 step.19
  175.2 1.4 collective-permute-start.32
  178.3 0.9 back.21
  179.2 10.2 %all_to_all.75.received = f32[8,24,128]{2,1,0:T(8,128)S(1)} all-to-all(f32[8,24,128]{2,1,0:T(8,128)S(1)} %get-tuple-element.175), channel_id=1, replica_groups=mesh['region'=8,'blk'=4] {'region'}, dimensions={0} | all-to-all | bytes 196608 | tf_op jit(solution)/shard_map/all_to_all | solution.py:347
  189.4 1.2 step.20
  190.8 0.9 collective-permute-start.34
  191.8 1.4 collective-permute-start.35
  194.8 0.9 back.22
  195.7 10.2 %all_to_all.76.received = f32[8,24,128]{2,1,0:T(8,128)S(1)} all-to-all(f32[8,24,128]{2,1,0:T(8,128)S(1)} %get-tuple-element.183), channel_id=1, replica_groups=mesh['region'=8,'blk'=4] {'region'}, dimensions={0} | all-to-all | bytes 196608 | tf_op jit(solution)/shard_map/all_to_all | solution.py:347
  205.9 1.2 step.21
  208.2 1.4 collective-permute-start.38
  209.5 0.9 collective-permute-done.36.refs_0_
  211.2 0.9 back.23
  212.2 10.2 %all_to_all.77.received = f32[8,24,128]{2,1,0:T(8,128)S(1)} all-to-all(f32[8,24,128]{2,1,0:T(8,128)S(1)} %get-tuple-element.191), channel_id=1, replica_groups=mesh['region'=8,'blk'=4] {'region'}, dimensions={0} | all-to-all | bytes 196608 | tf_op jit(solution)/shard_map/all_to_all | solution.py:347
  (58 shorter events, 24.5 us)
Async XLA Ops:
  2.0 5.1 %collective-permute-start = (f32[16,128]{1,0:T(8,128)S(1)}, f32[16,128]{1,0:T(8,128)S(1)}, u32[]{:S(2)}, u32[]{:S(2)}) collective-permute-start(f32[16,128]{1,0:T(8,128)S(1)} %pad_maximum_fusion.1.refs_0_), channel_id=1, source_target_pairs={{0,1},{1,2},{2,3},{3,0},{4,5},{5,6},{6,7},{7,4},{8,9},{9,10},{10,1... | collective-permute-start | bytes 24584 | tf_op jit(solution)/shard_map/ppermute | solution.py:342
  2.5 4.7 %collective-permute-start.1 = (f32[16,128]{1,0:T(8,128)S(1)}, f32[16,128]{1,0:T(8,128)S(1)}, u32[]{:S(2)}, u32[]{:S(2)}) collective-permute-start(f32[16,128]{1,0:T(8,128)S(1)} %pad_maximum_fusion.1.refs_0_), channel_id=1, source_target_pairs={{0,2},{1,3},{2,0},{3,1},{4,6},{5,7},{6,4},{7,5},{8,10},{9,11},{10,... | collective-permute-start | bytes 24584 | tf_op jit(solution)/shard_map/ppermute | solution.py:342
  5.0 2.8 %collective-permute-start.2 = (f32[16,128]{1,0:T(8,128)S(1)}, f32[16,128]{1,0:T(8,128)S(1)}, u32[]{:S(2)}, u32[]{:S(2)}) collective-permute-start(f32[16,128]{1,0:T(8,128)S(1)} %pad_maximum_fusion.1.refs_0_), channel_id=1, source_target_pairs={{0,3},{1,0},{2,1},{3,2},{4,7},{5,4},{6,5},{7,6},{8,11},{9,8},{10,9... | collective-permute-start | bytes 24584 | tf_op jit(solution)/shard_map/ppermute | solution.py:342
  25.4 3.3 %collective-permute-start.3 = (f32[40,128]{1,0:T(8,128)S(1)}, f32[40,128]{1,0:T(8,128)S(1)}, u32[]{:S(2)}, u32[]{:S(2)}) collective-permute-start(f32[40,128]{1,0:T(8,128)S(1)} %get-tuple-element.104.own), channel_id=1, source_target_pairs={{0,1},{1,2},{2,3},{3,0},{4,5},{5,6},{6,7},{7,4},{8,9},{9,10},{10,1... | collective-permute-start | bytes 61448 | tf_op jit(solution)/shard_map/ppermute | solution.py:342
  25.5 3.8 %collective-permute-start.4 = (f32[40,128]{1,0:T(8,128)S(1)}, f32[40,128]{1,0:T(8,128)S(1)}, u32[]{:S(2)}, u32[]{:S(2)}) collective-permute-start(f32[40,128]{1,0:T(8,128)S(1)} %get-tuple-element.104.own), channel_id=1, source_target_pairs={{0,2},{1,3},{2,0},{3,1},{4,6},{5,7},{6,4},{7,5},{8,10},{9,11},{10,... | collective-permute-start | bytes 61448 | tf_op jit(solution)/shard_map/ppermute | solution.py:342
  26.8 2.8 %collective-permute-start.5 = (f32[40,128]{1,0:T(8,128)S(1)}, f32[40,128]{1,0:T(8,128)S(1)}, u32[]{:S(2)}, u32[]{:S(2)}) collective-permute-start(f32[40,128]{1,0:T(8,128)S(1)} %get-tuple-element.104.own), channel_id=1, source_target_pairs={{0,3},{1,0},{2,1},{3,2},{4,7},{5,4},{6,5},{7,6},{8,11},{9,8},{10,9... | collective-permute-start | bytes 61448 | tf_op jit(solution)/shard_map/ppermute | solution.py:342
  42.1 3.3 %collective-permute-start.6 = (f32[40,128]{1,0:T(8,128)S(1)}, f32[40,128]{1,0:T(8,128)S(1)}, u32[]{:S(2)}, u32[]{:S(2)}) collective-permute-start(f32[40,128]{1,0:T(8,128)S(1)} %get-tuple-element.110.own), channel_id=1, source_target_pairs={{0,1},{1,2},{2,3},{3,0},{4,5},{5,6},{6,7},{7,4},{8,9},{9,10},{10,1... | collective-permute-start | bytes 61448 | tf_op jit(solution)/shard_map/ppermute | solution.py:342
  42.2 3.8 %collective-permute-start.7 = (f32[40,128]{1,0:T(8,128)S(1)}, f32[40,128]{1,0:T(8,128)S(1)}, u32[]{:S(2)}, u32[]{:S(2)}) collective-permute-start(f32[40,128]{1,0:T(8,128)S(1)} %get-tuple-element.110.own), channel_id=1, source_target_pairs={{0,2},{1,3},{2,0},{3,1},{4,6},{5,7},{6,4},{7,5},{8,10},{9,11},{10,... | collective-permute-start | bytes 61448 | tf_op jit(solution)/shard_map/ppermute | solution.py:342
  43.7 2.9 %collective-permute-start.8 = (f32[40,128]{1,0:T(8,128)S(1)}, f32[40,128]{1,0:T(8,128)S(1)}, u32[]{:S(2)}, u32[]{:S(2)}) collective-permute-start(f32[40,128]{1,0:T(8,128)S(1)} %get-tuple-element.110.own), channel_id=1, source_target_pairs={{0,3},{1,0},{2,1},{3,2},{4,7},{5,4},{6,5},{7,6},{8,11},{9,8},{10,9... | collective-permute-start | bytes 61448 | tf_op jit(solution)/shard_map/ppermute | solution.py:342
  58.8 3.3 %collective-permute-start.9 = (f32[40,128]{1,0:T(8,128)S(1)}, f32[40,128]{1,0:T(8,128)S(1)}, u32[]{:S(2)}, u32[]{:S(2)}) collective-permute-start(f32[40,128]{1,0:T(8,128)S(1)} %get-tuple-element.118.own), channel_id=1, source_target_pairs={{0,1},{1,2},{2,3},{3,0},{4,5},{5,6},{6,7},{7,4},{8,9},{9,10},{10,1... | collective-permute-start | bytes 61448 | tf_op jit(solution)/shard_map/ppermute | solution.py:342
  58.9 3.9 %collective-permute-start.10 = (f32[40,128]{1,0:T(8,128)S(1)}, f32[40,128]{1,0:T(8,128)S(1)}, u32[]{:S(2)}, u32[]{:S(2)}) collective-permute-start(f32[40,128]{1,0:T(8,128)S(1)} %get-tuple-element.118.own), channel_id=1, source_target_pairs={{0,2},{1,3},{2,0},{3,1},{4,6},{5,7},{6,4},{7,5},{8,10},{9,11},{10,... | collective-permute-start | bytes 61448 | tf_op jit(solution)/shard_map/ppermute | solution.py:342
  59.8 3.0 %collective-permute-start.11 = (f32[40,128]{1,0:T(8,128)S(1)}, f32[40,128]{1,0:T(8,128)S(1)}, u32[]{:S(2)}, u32[]{:S(2)}) collective-permute-start(f32[40,128]{1,0:T(8,128)S(1)} %get-tuple-element.118.own), channel_id=1, source_target_pairs={{0,3},{1,0},{2,1},{3,2},{4,7},{5,4},{6,5},{7,6},{8,11},{9,8},{10,9... | collective-permute-start | bytes 61448 | tf_op jit(solution)/shard_map/ppermute | solution.py:342
  75.1 3.3 %collective-permute-start.12 = (f32[40,128]{1,0:T(8,128)S(1)}, f32[40,128]{1,0:T(8,128)S(1)}, u32[]{:S(2)}, u32[]{:S(2)}) collective-permute-start(f32[40,128]{1,0:T(8,128)S(1)} %get-tuple-element.126.own), channel_id=1, source_target_pairs={{0,1},{1,2},{2,3},{3,0},{4,5},{5,6},{6,7},{7,4},{8,9},{9,10},{10,1... | collective-permute-start | bytes 61448 | tf_op jit(solution)/shard_map/ppermute | solution.py:342
  75.3 3.8 %collective-permute-start.13 = (f32[40,128]{1,0:T(8,128)S(1)}, f32[40,128]{1,0:T(8,128)S(1)}, u32[]{:S(2)}, u32[]{:S(2)}) collective-permute-start(f32[40,128]{1,0:T(8,128)S(1)} %get-tuple-element.126.own), channel_id=1, source_target_pairs={{0,2},{1,3},{2,0},{3,1},{4,6},{5,7},{6,4},{7,5},{8,10},{9,11},{10,... | collective-permute-start | bytes 61448 | tf_op jit(solution)/shard_map/ppermute | solution.py:342
  76.4 2.9 %collective-permute-start.14 = (f32[40,128]{1,0:T(8,128)S(1)}, f32[40,128]{1,0:T(8,128)S(1)}, u32[]{:S(2)}, u32[]{:S(2)}) collective-permute-start(f32[40,128]{1,0:T(8,128)S(1)} %get-tuple-element.126.own), channel_id=1, source_target_pairs={{0,3},{1,0},{2,1},{3,2},{4,7},{5,4},{6,5},{7,6},{8,11},{9,8},{10,9... | collective-permute-start | bytes 61448 | tf_op jit(solution)/shard_map/ppermute | solution.py:342
  91.7 3.3 %collective-permute-start.15 = (f32[40,128]{1,0:T(8,128)S(1)}, f32[40,128]{1,0:T(8,128)S(1)}, u32[]{:S(2)}, u32[]{:S(2)}) collective-permute-start(f32[40,128]{1,0:T(8,128)S(1)} %get-tuple-element.134.own), channel_id=1, source_target_pairs={{0,1},{1,2},{2,3},{3,0},{4,5},{5,6},{6,7},{7,4},{8,9},{9,10},{10,1... | collective-permute-start | bytes 61448 | tf_op jit(solution)/shard_map/ppermute | solution.py:342
  91.8 4.1 %collective-permute-start.16 = (f32[40,128]{1,0:T(8,128)S(1)}, f32[40,128]{1,0:T(8,128)S(1)}, u32[]{:S(2)}, u32[]{:S(2)}) collective-permute-start(f32[40,128]{1,0:T(8,128)S(1)} %get-tuple-element.134.own), channel_id=1, source_target_pairs={{0,2},{1,3},{2,0},{3,1},{4,6},{5,7},{6,4},{7,5},{8,10},{9,11},{10,... | collective-permute-start | bytes 61448 | tf_op jit(solution)/shard_map/ppermute | solution.py:342
  92.8 3.0 %collective-permute-start.17 = (f32[40,128]{1,0:T(8,128)S(1)}, f32[40,128]{1,0:T(8,128)S(1)}, u32[]{:S(2)}, u32[]{:S(2)}) collective-permute-start(f32[40,128]{1,0:T(8,128)S(1)} %get-tuple-element.134.own), channel_id=1, source_target_pairs={{0,3},{1,0},{2,1},{3,2},{4,7},{5,4},{6,5},{7,6},{8,11},{9,8},{10,9... | collective-permute-start | bytes 61448 | tf_op jit(solution)/shard_map/ppermute | solution.py:342
  108.1 3.3 %collective-permute-start.18 = (f32[40,128]{1,0:T(8,128)S(1)}, f32[40,128]{1,0:T(8,128)S(1)}, u32[]{:S(2)}, u32[]{:S(2)}) collective-permute-start(f32[40,128]{1,0:T(8,128)S(1)} %get-tuple-element.142.own), channel_id=1, source_target_pairs={{0,1},{1,2},{2,3},{3,0},{4,5},{5,6},{6,7},{7,4},{8,9},{9,10},{10,1... | collective-permute-start | bytes 61448 | tf_op jit(solution)/shard_map/ppermute | solution.py:342
  108.3 3.9 %collective-permute-start.19 = (f32[40,128]{1,0:T(8,128)S(1)}, f32[40,128]{1,0:T(8,128)S(1)}, u32[]{:S(2)}, u32[]{:S(2)}) collective-permute-start(f32[40,128]{1,0:T(8,128)S(1)} %get-tuple-element.142.own), channel_id=1, source_target_pairs={{0,2},{1,3},{2,0},{3,1},{4,6},{5,7},{6,4},{7,5},{8,10},{9,11},{10,... | collective-permute-start | bytes 61448 | tf_op jit(solution)/shard_map/ppermute | solution.py:342
  109.3 2.9 %collective-permute-start.20 = (f32[40,128]{1,0:T(8,128)S(1)}, f32[40,128]{1,0:T(8,128)S(1)}, u32[]{:S(2)}, u32[]{:S(2)}) collective-permute-start(f32[40,128]{1,0:T(8,128)S(1)} %get-tuple-element.142.own), channel_id=1, source_target_pairs={{0,3},{1,0},{2,1},{3,2},{4,7},{5,4},{6,5},{7,6},{8,11},{9,8},{10,9... | collective-permute-start | bytes 61448 | tf_op jit(solution)/shard_map/ppermute | solution.py:342
  124.7 3.3 %collective-permute-start.21 = (f32[40,128]{1,0:T(8,128)S(1)}, f32[40,128]{1,0:T(8,128)S(1)}, u32[]{:S(2)}, u32[]{:S(2)}) collective-permute-start(f32[40,128]{1,0:T(8,128)S(1)} %get-tuple-element.150.own), channel_id=1, source_target_pairs={{0,1},{1,2},{2,3},{3,0},{4,5},{5,6},{6,7},{7,4},{8,9},{9,10},{10,1... | collective-permute-start | bytes 61448 | tf_op jit(solution)/shard_map/ppermute | solution.py:342
  124.8 4.1 %collective-permute-start.22 = (f32[40,128]{1,0:T(8,128)S(1)}, f32[40,128]{1,0:T(8,128)S(1)}, u32[]{:S(2)}, u32[]{:S(2)}) collective-permute-start(f32[40,128]{1,0:T(8,128)S(1)} %get-tuple-element.150.own), channel_id=1, source_target_pairs={{0,2},{1,3},{2,0},{3,1},{4,6},{5,7},{6,4},{7,5},{8,10},{9,11},{10,... | collective-permute-start | bytes 61448 | tf_op jit(solution)/shard_map/ppermute | solution.py:342
  125.8 3.0 %collective-permute-start.23 = (f32[40,128]{1,0:T(8,128)S(1)}, f32[40,128]{1,0:T(8,128)S(1)}, u32[]{:S(2)}, u32[]{:S(2)}) collective-permute-start(f32[40,128]{1,0:T(8,128)S(1)} %get-tuple-element.150.own), channel_id=1, source_target_pairs={{0,3},{1,0},{2,1},{3,2},{4,7},{5,4},{6,5},{7,6},{8,11},{9,8},{10,9... | collective-permute-start | bytes 61448 | tf_op jit(solution)/shard_map/ppermute | solution.py:342
  141.1 3.3 %collective-permute-start.24 = (f32[40,128]{1,0:T(8,128)S(1)}, f32[40,128]{1,0:T(8,128)S(1)}, u32[]{:S(2)}, u32[]{:S(2)}) collective-permute-start(f32[40,128]{1,0:T(8,128)S(1)} %get-tuple-element.158.own), channel_id=1, source_target_pairs={{0,1},{1,2},{2,3},{3,0},{4,5},{5,6},{6,7},{7,4},{8,9},{9,10},{10,1... | collective-permute-start | bytes 61448 | tf_op jit(solution)/shard_map/ppermute | solution.py:342
  141.3 3.9 %collective-permute-start.25 = (f32[40,128]{1,0:T(8,128)S(1)}, f32[40,128]{1,0:T(8,128)S(1)}, u32[]{:S(2)}, u32[]{:S(2)}) collective-permute-start(f32[40,128]{1,0:T(8,128)S(1)} %get-tuple-element.158.own), channel_id=1, source_target_pairs={{0,2},{1,3},{2,0},{3,1},{4,6},{5,7},{6,4},{7,5},{8,10},{9,11},{10,... | collective-permute-start | bytes 61448 | tf_op jit(solution)/shard_map/ppermute | solution.py:342
  142.3 3.0 %collective-permute-start.26 = (f32[40,128]{1,0:T(8,128)S(1)}, f32[40,128]{1,0:T(8,128)S(1)}, u32[]{:S(2)}, u32[]{:S(2)}) collective-permute-start(f32[40,128]{1,0:T(8,128)S(1)} %get-tuple-element.158.own), channel_id=1, source_target_pairs={{0,3},{1,0},{2,1},{3,2},{4,7},{5,4},{6,5},{7,6},{8,11},{9,8},{10,9... | collective-permute-start | bytes 61448 | tf_op jit(solution)/shard_map/ppermute | solution.py:342
  157.7 3.3 %collective-permute-start.27 = (f32[40,128]{1,0:T(8,128)S(1)}, f32[40,128]{1,0:T(8,128)S(1)}, u32[]{:S(2)}, u32[]{:S(2)}) collective-permute-start(f32[40,128]{1,0:T(8,128)S(1)} %get-tuple-element.166.own), channel_id=1, source_target_pairs={{0,1},{1,2},{2,3},{3,0},{4,5},{5,6},{6,7},{7,4},{8,9},{9,10},{10,1... | collective-permute-start | bytes 61448 | tf_op jit(solution)/shard_map/ppermute | solution.py:342
  157.8 3.9 %collective-permute-start.28 = (f32[40,128]{1,0:T(8,128)S(1)}, f32[40,128]{1,0:T(8,128)S(1)}, u32[]{:S(2)}, u32[]{:S(2)}) collective-permute-start(f32[40,128]{1,0:T(8,128)S(1)} %get-tuple-element.166.own), channel_id=1, source_target_pairs={{0,2},{1,3},{2,0},{3,1},{4,6},{5,7},{6,4},{7,5},{8,10},{9,11},{10,... | collective-permute-start | bytes 61448 | tf_op jit(solution)/shard_map/ppermute | solution.py:342
  158.7 3.0 %collective-permute-start.29 = (f32[40,128]{1,0:T(8,128)S(1)}, f32[40,128]{1,0:T(8,128)S(1)}, u32[]{:S(2)}, u32[]{:S(2)}) collective-permute-start(f32[40,128]{1,0:T(8,128)S(1)} %get-tuple-element.166.own), channel_id=1, source_target_pairs={{0,3},{1,0},{2,1},{3,2},{4,7},{5,4},{6,5},{7,6},{8,11},{9,8},{10,9... | collective-permute-start | bytes 61448 | tf_op jit(solution)/shard_map/ppermute | solution.py:342
  174.1 3.3 %collective-permute-start.30 = (f32[40,128]{1,0:T(8,128)S(1)}, f32[40,128]{1,0:T(8,128)S(1)}, u32[]{:S(2)}, u32[]{:S(2)}) collective-permute-start(f32[40,128]{1,0:T(8,128)S(1)} %get-tuple-element.174.own), channel_id=1, source_target_pairs={{0,1},{1,2},{2,3},{3,0},{4,5},{5,6},{6,7},{7,4},{8,9},{9,10},{10,1... | collective-permute-start | bytes 61448 | tf_op jit(solution)/shard_map/ppermute | solution.py:342
  174.3 4.0 %collective-permute-start.31 = (f32[40,128]{1,0:T(8,128)S(1)}, f32[40,128]{1,0:T(8,128)S(1)}, u32[]{:S(2)}, u32[]{:S(2)}) collective-permute-start(f32[40,128]{1,0:T(8,128)S(1)} %get-tuple-element.174.own), channel_id=1, source_target_pairs={{0,2},{1,3},{2,0},{3,1},{4,6},{5,7},{6,4},{7,5},{8,10},{9,11},{10,... | collective-permute-start | bytes 61448 | tf_op jit(solution)/shard_map/ppermute | solution.py:342
  175.2 3.1 %collective-permute-start.32 = (f32[40,128]{1,0:T(8,128)S(1)}, f32[40,128]{1,0:T(8,128)S(1)}, u32[]{:S(2)}, u32[]{:S(2)}) collective-permute-start(f32[40,128]{1,0:T(8,128)S(1)} %get-tuple-element.174.own), channel_id=1, source_target_pairs={{0,3},{1,0},{2,1},{3,2},{4,7},{5,4},{6,5},{7,6},{8,11},{9,8},{10,9... | collective-permute-start | bytes 61448 | tf_op jit(solution)/shard_map/ppermute | solution.py:342
  190.6 3.3 %collective-permute-start.33 = (f32[40,128]{1,0:T(8,128)S(1)}, f32[40,128]{1,0:T(8,128)S(1)}, u32[]{:S(2)}, u32[]{:S(2)}) collective-permute-start(f32[40,128]{1,0:T(8,128)S(1)} %get-tuple-element.182.own), channel_id=1, source_target_pairs={{0,1},{1,2},{2,3},{3,0},{4,5},{5,6},{6,7},{7,4},{8,9},{9,10},{10,1... | collective-permute-start | bytes 61448 | tf_op jit(solution)/shard_map/ppermute | solution.py:342
  190.8 4.0 %collective-permute-start.34 = (f32[40,128]{1,0:T(8,128)S(1)}, f32[40,128]{1,0:T(8,128)S(1)}, u32[]{:S(2)}, u32[]{:S(2)}) collective-permute-start(f32[40,128]{1,0:T(8,128)S(1)} %get-tuple-element.182.own), channel_id=1, source_target_pairs={{0,2},{1,3},{2,0},{3,1},{4,6},{5,7},{6,4},{7,5},{8,10},{9,11},{10,... | collective-permute-start | bytes 61448 | tf_op jit(solution)/shard_map/ppermute | solution.py:342
  191.8 3.0 %collective-permute-start.35 = (f32[40,128]{1,0:T(8,128)S(1)}, f32[40,128]{1,0:T(8,128)S(1)}, u32[]{:S(2)}, u32[]{:S(2)}) collective-permute-start(f32[40,128]{1,0:T(8,128)S(1)} %get-tuple-element.182.own), channel_id=1, source_target_pairs={{0,3},{1,0},{2,1},{3,2},{4,7},{5,4},{6,5},{7,6},{8,11},{9,8},{10,9... | collective-permute-start | bytes 61448 | tf_op jit(solution)/shard_map/ppermute | solution.py:342
  207.2 3.3 %collective-permute-start.36 = (f32[40,128]{1,0:T(8,128)S(1)}, f32[40,128]{1,0:T(8,128)S(1)}, u32[]{:S(2)}, u32[]{:S(2)}) collective-permute-start(f32[40,128]{1,0:T(8,128)S(1)} %get-tuple-element.190.own), channel_id=1, source_target_pairs={{0,1},{1,2},{2,3},{3,0},{4,5},{5,6},{6,7},{7,4},{8,9},{9,10},{10,1... | collective-permute-start | bytes 61448 | tf_op jit(solution)/shard_map/ppermute | solution.py:342
  207.3 3.9 %collective-permute-start.37 = (f32[40,128]{1,0:T(8,128)S(1)}, f32[40,128]{1,0:T(8,128)S(1)}, u32[]{:S(2)}, u32[]{:S(2)}) collective-permute-start(f32[40,128]{1,0:T(8,128)S(1)} %get-tuple-element.190.own), channel_id=1, source_target_pairs={{0,2},{1,3},{2,0},{3,1},{4,6},{5,7},{6,4},{7,5},{8,10},{9,11},{10,... | collective-permute-start | bytes 61448 | tf_op jit(solution)/shard_map/ppermute | solution.py:342
  208.2 3.0 %collective-permute-start.38 = (f32[40,128]{1,0:T(8,128)S(1)}, f32[40,128]{1,0:T(8,128)S(1)}, u32[]{:S(2)}, u32[]{:S(2)}) collective-permute-start(f32[40,128]{1,0:T(8,128)S(1)} %get-tuple-element.190.own), channel_id=1, source_target_pairs={{0,3},{1,0},{2,1},{3,2},{4,7},{5,4},{6,5},{7,6},{8,11},{9,8},{10,9... | collective-permute-start | bytes 61448 | tf_op jit(solution)/shard_map/ppermute | solution.py:342

commit v3 on v2

--- a/solution.py
+++ b/solution.py
@@ -10,11 +10,9 @@
 SUB = 8
 SPOTS = {(2, 1): 0, (1, 0): 0, (1, 1): 1, (-1, -1): 0, (-1, 0): 1, (-2, -1): 1}
 VMEM_LIMIT = 16 * 1024 * 1024
-BANKS = 4
 PIECES = 8
 
 vmem = pl.BlockSpec(memory_space=pltpu.VMEM)
-anywhere = pl.BlockSpec(memory_space=pl.ANY)
 hbm = pl.BlockSpec(memory_space=pltpu.HBM)
 
 
@@ -28,26 +26,47 @@
     return rows8(row == lane)
 
 
-def as_column(row, eye):
-    spread = jnp.where(eye, row[None], 0.0)
-    return jnp.sum(spread, axis=-1, keepdims=True)
-
-
-def lane_total(value):
-    return jnp.sum(jnp.sum(value, axis=0, keepdims=True), axis=1, keepdims=True)
+def three_terms(value):
+    high = value.astype(jnp.bfloat16).astype(jnp.float32)
+    middle = (value - high).astype(jnp.bfloat16).astype(jnp.float32)
+    return high, middle, (value - high) - middle
+
+
+def selectors(tiles, width):
+    shape = (tiles // 2, width, 2 * width)
+    pair, row, lane = (lax.broadcasted_iota(jnp.int32, shape, n) for n in range(3))
+    wanted = 2 * pair + lane // width
+    return ((row % tiles == wanted) & (row < 3 * tiles)).astype(jnp.bfloat16)
 
 
 def copy_in(source, target, sem):
     return pltpu.make_async_copy(source, target, sem)
 
 
-def forward(jac, index, spread, rows):
+def gather_rows(scaled, lookup, picked):
+    slots, tiles, width = lookup.shape
+    groups = [scaled[n : n + SUB] for n in range(0, scaled.shape[0], SUB)]
+    for j in range(slots):
+        for start in range(0, tiles, SUB):
+            wanted = lookup[j, start : start + SUB, :]
+            within = lax.rem(wanted, SUB)
+            total = None
+            for n, group in enumerate(groups):
+                found = jnp.take_along_axis(
+                    group, within, axis=0, mode="promise_in_bounds"
+                )
+                found = jnp.where(wanted // SUB == n, found, 0.0)
+                total = found if total is None else total + found
+            picked[j, start : start + SUB, :] = total
+
+
+def forward(jac, picked, rows):
     tiles, slots, width, _ = jac.shape
     eye = diagonal(width)
     for t in range(tiles):
         total = None
         for j in range(slots):
-            term = rows8(jac[t, j]) * spread[index[t * slots + j]][None]
+            term = rows8(jac[t, j]) * picked[j, t : t + 1, :][None]
             total = term if total is None else total + term
         total = jnp.sum(total, axis=-1, keepdims=True)
         rows[t : t + 1, :] = jnp.sum(
@@ -55,35 +74,30 @@
         )
 
 
-def backward(jac, chosen, weighted, banks, back, ready, square, arrived=lambda t: None):
+def backward(jac, weighted, picks, spots, back, square, arrived=lambda t: None):
     tiles, slots, width, _ = jac.shape
-    eye = diagonal(width)
-    banks[...] = jnp.zeros_like(banks)
-
-    def add(t):
-        for j in range(slots):
-            where = ((t * slots + j) % BANKS, chosen(t, j))
-            banks[where] += back[t * slots + j]
-
-    half = tiles // 2
+    value = weighted[...]
+    terms = three_terms(value)
+    rest = jnp.zeros((width - 3 * tiles, width), jnp.float32)
+    turned = jnp.transpose(jnp.concatenate([*terms, rest], axis=0))
+    turned = turned.astype(jnp.bfloat16)
     for t in range(tiles):
         arrived(t)
-        if t == half:
-            ready()
-            for early in range(half):
-                add(early)
-        column = as_column(weighted[t : t + 1, :], eye)
+        if t % 2 == 0:
+            both = jnp.dot(turned, picks[t // 2], preferred_element_type=jnp.float32)
+        column = rows8(both[:, t % 2 * width : (t % 2 + 1) * width])
         for j in range(slots):
             block = rows8(jac[t, j])
             if square:
                 block = block * block
-            back[t * slots + j] = jnp.sum(block * column, axis=0)
-        if t >= half:
-            add(t)
-    total = banks[0]
-    for bank in range(1, BANKS):
-        total = total + banks[bank]
-    return jnp.sum(total, axis=1)
+            back[j * tiles + t : j * tiles + t + 1, :] = jnp.sum(
+                jnp.sum(block * column, axis=0), axis=0, keepdims=True
+            )
+    terms = three_terms(back[...])
+    stacked = jnp.concatenate([*terms, jnp.zeros_like(terms[0])], axis=0)
+    return jnp.dot(
+        spots[...], stacked.astype(jnp.bfloat16), preferred_element_type=jnp.float32
+    )
 
 
 def publish(chunk, out):
@@ -110,10 +124,10 @@
     out[region] = blank
 
 
-def diag_kernel(jac, vectors, *refs):
-    ins, refs = refs[:-10], refs[-10:]
-    out, weight, place, held, fits, index, small, banks, back, sems = refs
-    tiles, slots = jac.shape[:2]
+def diag_kernel(jac, vectors, picks, *refs):
+    ins, refs = refs[:-8], refs[-8:]
+    out, weight, spots, held, lookup, fits, back, sems = refs
+    tiles, slots, width, _ = jac.shape
     blocks = len(ins)
     per_dev = tiles // blocks
     step = tiles // PIECES
@@ -130,34 +144,30 @@
         source = lax.rem(group + (blocks - shift), blocks)
         spot = pl.ds(pl.multiple_of(source * per_dev, per_dev), per_dev)
         weight[spot, :] = part[:per_dev, :]
-        fits[spot, :] = part[per_dev:, :].astype(jnp.int32)
-    table = copy_in(fits, index, sems.at[PIECES])
-    table.start()
-    listed = copy_in(small, place, sems.at[PIECES + 1])
-
-    def ready():
-        table.wait()
-        for t in range(tiles):
-            for j in range(slots):
-                small[t * slots + j] = index[t, group * slots + j]
-        listed.start()
+        fits[spot, :] = part[per_dev:, :]
+    lane = lax.broadcasted_iota(jnp.int32, fits.shape, 1)
+    chosen = []
+    for j in range(slots):
+        own = jnp.where(lane == group * slots + j, fits[...], 0.0)
+        own = jnp.sum(own, axis=1, keepdims=True)
+        chosen.append(jnp.broadcast_to(own, fits.shape))
+        lookup[j] = chosen[j].astype(jnp.int32)
+    unused = jnp.full((slots * tiles, width), -1.0, jnp.float32)
+    names = jnp.transpose(jnp.concatenate(chosen * 3 + [unused], axis=0))
+    names = names[: spots.shape[0]].astype(jnp.int32)
+    column = lax.broadcasted_iota(jnp.int32, names.shape, 0)
+    spots[...] = jnp.where(column == names, 1.0, 0.0).astype(jnp.bfloat16)
 
     def arrived(t):
         if t % step == 0:
             pieces[t // step].wait()
 
-    squares = backward(
-        held, lambda t, j: small[t * slots + j], weight, banks, back, ready, True, arrived
-    )
+    squares = backward(held, weight, picks, spots, back, True, arrived)
     publish(jnp.concatenate([squares, vectors[...]], axis=0), out)
-    listed.wait()
-
-
-def back_kernel(place, jac, weight, own, *refs):
-    others, refs = refs[:-7], refs[-7:]
-    out, keep, weighted, banks, back, index, sem = refs
-    copy = copy_in(place, index, sem)
-    copy.start()
+
+
+def back_kernel(jac, weight, picks, spots, own, *refs):
+    others, (out, keep, weighted, back) = refs[:-4], refs[-4:]
     tiles, slots = jac.shape[:2]
     parts = [own] + list(others)
     even, odd = None, None
@@ -171,16 +181,14 @@
     weighted[...] = weight[...] * rows
     delta = jnp.sum(weighted[...] * rows, axis=0, keepdims=True) + sums[1:2]
     scalars = jnp.concatenate([sums[:1], delta, sums[2:]], axis=0)
-    columns = backward(
-        jac, lambda t, j: index[t * slots + j], weighted, banks, back, copy.wait, False
-    )
+    columns = backward(jac, weighted, picks, spots, back, False)
     place_blocks(out, keep, columns, scalars)
 
 
-def send_rows(jac, index, resid, scaled, diag, spread, own, out):
+def send_rows(jac, lookup, resid, scaled, diag, picked, own, out):
     tiles = jac.shape[0]
-    spread[...] = jnp.broadcast_to(scaled[:, None, :], spread.shape)
-    forward(jac, index, spread, out)
+    gather_rows(scaled, lookup, picked)
+    forward(jac, picked, out)
     r, z, d = resid[own], scaled[own], diag[own]
     gamma = jnp.sum(r * z, axis=0, keepdims=True)
     delta = jnp.sum(d * z * z, axis=0, keepdims=True)
@@ -209,11 +217,7 @@
     return jnp.concatenate(blocks, axis=0)
 
 
-def first_kernel(
-    place, jac, received, out, diag, precond, resid, spread, index, sem
-):
-    copy = copy_in(place, index, sem)
-    copy.start()
+def first_kernel(jac, lookup, received, out, diag, precond, resid, picked):
     regions = received.shape[0]
     per_dev = diag.shape[0] // 3
     region = lax.axis_index("region")
@@ -225,8 +229,7 @@
     precond[...] = m
     resid[...] = r
     own = slice(per_dev, 2 * per_dev)
-    copy.wait()
-    send_rows(jac, index, r, r / m, d, spread, own, out)
+    send_rows(jac, lookup, r, r / m, d, picked, own, out)
 
 
 def collected(received, kept, per_dev):
@@ -276,11 +279,9 @@
 
 
 def step_kernel(
-    place, jac, received, kept, diag, precond, resid, along, direct, answer, scal,
-    out, resid_o, along_o, direct_o, answer_o, scal_o, spread, index, sem,
+    jac, lookup, received, kept, diag, precond, resid, along, direct, answer, scal,
+    out, resid_o, along_o, direct_o, answer_o, scal_o, picked,
 ):
-    copy = copy_in(place, index, sem)
-    copy.start()
     per_dev = direct.shape[0]
     x, r, s, p, gamma, alpha = update(
         received, kept, diag, precond, resid, along, direct, answer, scal
@@ -292,8 +293,7 @@
     scal_o[0:1, :] = jnp.broadcast_to(gamma, (1, scal_o.shape[1]))
     scal_o[1:2, :] = jnp.broadcast_to(alpha, (1, scal_o.shape[1]))
     own = slice(per_dev, 2 * per_dev)
-    copy.wait()
-    send_rows(jac, index, r, r / precond[...], diag, spread, own, out)
+    send_rows(jac, lookup, r, r / precond[...], diag, picked, own, out)
 
 
 def last_kernel(
@@ -349,10 +349,8 @@
     flops = 4 * jac.size
     moved = 4 * jac.size
     row_count = tiles + SUB
-    spread = pltpu.VMEM((extent, SUB, width), f32)
-    banks = pltpu.VMEM((BANKS, extent, SUB, width), f32)
-    back = pltpu.VMEM((tiles * slots, SUB, width), f32)
-    table = [pltpu.SMEM((tiles * slots,), jnp.int32), pltpu.SemaphoreType.DMA]
+    picked = pltpu.VMEM((slots, tiles, width), f32)
+    back = pltpu.VMEM((tiles * slots, width), f32)
     chunk = (regions, 2 * per_dev + SUB, width)
     kept_shape = (extent + SUB, width)
     halo_shape, own_shape = (extent, width), (per_dev, width)
@@ -360,33 +358,31 @@
     fits = jnp.pad(pattern, ((0, 0), (0, width - pattern.shape[1]))).astype(f32)
     vectors = jnp.concatenate([bus_diag, right_side], axis=0)
     mine = jnp.concatenate([branch_weight, fits], axis=0)
-    setup, weight, place, jac = call(
+    picks = selectors(tiles, width)
+    setup, weight, spots, jac, lookup = call(
         diag_kernel,
         [
             (regions, extent + 2 * per_dev, width), (tiles, width),
-            jax.ShapeDtypeStruct((tiles * slots,), jnp.int32), jac.shape,
+            jax.ShapeDtypeStruct((extent, 4 * tiles * slots), jnp.bfloat16), jac.shape,
+            jax.ShapeDtypeStruct((slots, tiles, width), jnp.int32),
         ],
         [
-            pltpu.VMEM((tiles, width), jnp.int32), pltpu.SMEM((tiles, width), jnp.int32),
-            pltpu.SMEM((tiles * slots,), jnp.int32), banks, back,
-            pltpu.SemaphoreType.DMA((PIECES + 2,)),
+            pltpu.VMEM((tiles, width), f32), back, pltpu.SemaphoreType.DMA((PIECES,)),
         ],
-        [hbm] + [vmem] * (1 + blocks), "diagonal", flops, moved, 47 * 1024 * 1024,
-    )(jac, vectors, mine, *across_blk(mine))
+        [hbm] + [vmem] * (2 + blocks), "diagonal", flops, moved, 47 * 1024 * 1024,
+    )(jac, vectors, picks, mine, *across_blk(mine))
     setup = across_region(setup)
     out, diag, precond, resid = call(
         first_kernel, [(row_count, width), halo_shape, halo_shape, halo_shape],
-        [spread] + table, [anywhere, vmem, vmem],
-        "first", flops, moved,
-    )(place, jac, setup)
+        [picked], [vmem] * 3, "first", flops, moved,
+    )(jac, lookup, setup)
 
     def image_of(out):
         parts = across_blk(out)
         chunks, kept = call(
-            back_kernel, [chunk, kept_shape], [pltpu.VMEM((tiles, width), f32), banks, back] + table,
-            [anywhere] + [vmem] * (3 + len(parts)),
-            "back", flops, moved,
-        )(place, jac, weight, out, *parts)
+            back_kernel, [chunk, kept_shape], [pltpu.VMEM((tiles, width), f32), back],
+            [vmem] * (5 + len(parts)), "back", flops, moved,
+        )(jac, weight, picks, spots, out, *parts)
         return across_region(chunks), kept
 
     def step(carry):
@@ -394,9 +390,8 @@
         out, resid, along, direct, answer, scal = call(
             step_kernel,
             [(row_count, width), halo_shape, halo_shape, own_shape, own_shape, (SUB, width)],
-            [spread] + table, [anywhere] + [vmem] * 10,
-            "step", flops, moved,
-        )(place, jac, received, kept, diag, precond, resid, along, direct, answer, scal)
+            [picked], [vmem] * 11, "step", flops, moved,
+        )(jac, lookup, received, kept, diag, precond, resid, along, direct, answer, scal)
         return *image_of(out), resid, along, direct, answer, scal
 
     carry = (

time: 224 us -> 217 us (0.969)
  Pallas kernels: 29.3 us -> 22.3 us
    pallas_call x11, Pallas kernels: 13.4 us -> 9.39 us  [step(): call(step_kernel, [(row_count, width), halo_shape, halo_shape, own_shape,...]
    pallas_call x12, Pallas kernels: 11.4 us -> 8.79 us  [image_of(): call(back_kernel, [chunk, kept_shape], [pltpu.VMEM((tiles, width), f32),...]
  transfers between devices with their start and end apart: 39 -> 39, of which waited for: 28 -> 34; matrix products, arithmetic and copies ran while one was open for 0% -> 1% of each run, Pallas kernels for 0% -> 0%
where the time goes in v3:
time: 217 us; the launch traced here: 216 us
  blocking collectives  136 us (63%)
  starting transfers between devices  35.9 us (17%)
  Pallas kernels  22.3 us (10%)
  waiting for transfers between devices  18.4 us (8%)
  other arithmetic  2.53 us (1%)
    all_to_all x13, blocking collectives, across_region(): return lax.all_to_all(chunks, 'region', 0, 0, tiled=True)  136 us
    ppermute x39, starting transfers between devices, across_blk(): lax.ppermute(value, 'blk', [(i, (i + k) % blocks) for i in range(blocks)])  35.9 us
    ppermute x39, waiting for transfers between devices, across_blk(): lax.ppermute(value, 'blk', [(i, (i + k) % blocks) for i in range(blocks)])  18.4 us
    pallas_call x11, Pallas kernels, step(): call(step_kernel, [(row_count, width), halo_shape, halo_shape, own_shape,...  9.39 us
    pallas_call x12, Pallas kernels, image_of(): call(back_kernel, [chunk, kept_shape], [pltpu.VMEM((tiles, width), f32),...  8.79 us
  transfers between devices with their start and end apart: 39, of which 34 were waited for; matrix products, arithmetic and copies ran while one was open for 1% of the time, Pallas kernels for 0%

profile of v3, /device:TPU:0, one launch (start us, length us, event | category | flops | bytes accessed | tf_op | source)
XLA Modules:
  0.0 215.9 jit_solution(2223802475423358117)
XLA Ops:
  2.5 2.5 %collective-permute-start.1 = (f32[16,128]{1,0:T(8,128)S(1)}, f32[16,128]{1,0:T(8,128)S(1)}, u32[]{:S(2)}, u32[]{:S(2)}) collective-permute-start(f32[16,128]{1,0:T(8,128)S(1)} %pad_maximum_fusion.1.refs_0_), channel_id=1, source_target_pairs={{0,2},{1,3},{2,0},{3,1},{4,6},{5,7},{6,4},{7,5},{8,10},{9,11},{10,... | collective-permute-start | bytes 24584 | tf_op jit(solution)/shard_map/ppermute | solution.py:342
  5.0 1.5 collective-permute-start.2
  7.8 2.7 %diagonal.1 = (f32[8,40,128]{2,1,0:T(8,128)S(1)}, f32[32,128]{1,0:T(8,128)S(1)}, bf16[24,256]{1,0:T(8,128)(2,1)S(1)}, f32[32,2,128,128]{3,2,1,0:T(8,128)S(1)}, s32[2,32,128]{2,1,0:T(8,128)S(1)}) custom-call(f32[32,2,128,128]{3,2,1,0:T(8,128)} %jac.1, f32[16,128]{1,0:T(8,128)S(1)} %pad_maximum_fusion.vectors, bf16[16,128,256]{2,1,0:T(8,128)(2,1)S(1)} %fusion.1.picks, ...), custom_call_target="tpu_custom_call" | custom-call | flops 4194304 | bytes 4194304 | tf_op jit(solution)/shard_map/diagonal/pallas_call | solution.py:362
  10.6 13.9 %all_to_all.65.received = f32[8,40,128]{2,1,0:T(8,128)S(1)} all-to-all(f32[8,40,128]{2,1,0:T(8,128)S(1)} %get-tuple-element.105), channel_id=1, replica_groups=mesh['region'=8,'blk'=4] {'region'}, dimensions={0} | all-to-all | bytes 327680 | tf_op jit(solution)/shard_map/all_to_all | solution.py:347
  25.2 1.3 collective-permute-start.4
  26.5 1.4 collective-permute-start.5
  30.1 10.3 %all_to_all.66.received = f32[8,24,128]{2,1,0:T(8,128)S(1)} all-to-all(f32[8,24,128]{2,1,0:T(8,128)S(1)} %get-tuple-element.107), channel_id=1, replica_groups=mesh['region'=8,'blk'=4] {'region'}, dimensions={0} | all-to-all | bytes 196608 | tf_op jit(solution)/shard_map/all_to_all | solution.py:347
  40.4 0.9 step.11
  41.3 1.5 collective-permute-start.7
  42.8 1.4 collective-permute-start.8
  46.4 10.0 %all_to_all.67.received = f32[8,24,128]{2,1,0:T(8,128)S(1)} all-to-all(f32[8,24,128]{2,1,0:T(8,128)S(1)} %get-tuple-element.113), channel_id=1, replica_groups=mesh['region'=8,'blk'=4] {'region'}, dimensions={0} | all-to-all | bytes 196608 | tf_op jit(solution)/shard_map/all_to_all | solution.py:347
  56.4 0.9 step.12
  57.3 1.0 collective-permute-start.10
  58.3 1.3 collective-permute-start.11
  59.6 0.9 collective-permute-done.9.refs_0_
  60.5 0.7 collective-permute-done.10.refs_1_
  62.0 10.1 %all_to_all.68.received = f32[8,24,128]{2,1,0:T(8,128)S(1)} all-to-all(f32[8,24,128]{2,1,0:T(8,128)S(1)} %get-tuple-element.121), channel_id=1, replica_groups=mesh['region'=8,'blk'=4] {'region'}, dimensions={0} | all-to-all | bytes 196608 | tf_op jit(solution)/shard_map/all_to_all | solution.py:347
  72.1 0.9 step.13
  73.2 1.1 collective-permute-start.13
  74.2 1.4 collective-permute-start.14
  76.3 0.8 collective-permute-done.13.refs_1_
  77.8 10.3 %all_to_all.69.received = f32[8,24,128]{2,1,0:T(8,128)S(1)} all-to-all(f32[8,24,128]{2,1,0:T(8,128)S(1)} %get-tuple-element.129), channel_id=1, replica_groups=mesh['region'=8,'blk'=4] {'region'}, dimensions={0} | all-to-all | bytes 196608 | tf_op jit(solution)/shard_map/all_to_all | solution.py:347
  88.1 0.9 step.14
  89.0 1.1 collective-permute-start.16
  90.1 1.4 collective-permute-start.17
  91.5 0.8 collective-permute-done.15.refs_0_
  92.2 0.8 collective-permute-done.16.refs_1_
  93.8 10.1 %all_to_all.70.received = f32[8,24,128]{2,1,0:T(8,128)S(1)} all-to-all(f32[8,24,128]{2,1,0:T(8,128)S(1)} %get-tuple-element.137), channel_id=1, replica_groups=mesh['region'=8,'blk'=4] {'region'}, dimensions={0} | all-to-all | bytes 196608 | tf_op jit(solution)/shard_map/all_to_all | solution.py:347
  103.9 0.9 step.15
  105.0 1.1 collective-permute-start.19
  106.0 1.4 collective-permute-start.20
  108.1 0.8 collective-permute-done.19.refs_1_
  108.9 0.7 back.17
  109.7 10.2 %all_to_all.71.received = f32[8,24,128]{2,1,0:T(8,128)S(1)} all-to-all(f32[8,24,128]{2,1,0:T(8,128)S(1)} %get-tuple-element.145), channel_id=1, replica_groups=mesh['region'=8,'blk'=4] {'region'}, dimensions={0} | all-to-all | bytes 196608 | tf_op jit(solution)/shard_map/all_to_all | solution.py:347
  119.9 0.9 step.16
  120.8 1.1 collective-permute-start.22
  121.9 1.4 collective-permute-start.23
  124.0 0.8 collective-permute-done.22.refs_1_
  125.5 10.1 %all_to_all.72.received = f32[8,24,128]{2,1,0:T(8,128)S(1)} all-to-all(f32[8,24,128]{2,1,0:T(8,128)S(1)} %get-tuple-element.153), channel_id=1, replica_groups=mesh['region'=8,'blk'=4] {'region'}, dimensions={0} | all-to-all | bytes 196608 | tf_op jit(solution)/shard_map/all_to_all | solution.py:347
  135.6 0.9 step.17
  136.6 1.2 collective-permute-start.25
  137.8 1.4 collective-permute-start.26
  141.5 10.2 %all_to_all.73.received = f32[8,24,128]{2,1,0:T(8,128)S(1)} all-to-all(f32[8,24,128]{2,1,0:T(8,128)S(1)} %get-tuple-element.161), channel_id=1, replica_groups=mesh['region'=8,'blk'=4] {'region'}, dimensions={0} | all-to-all | bytes 196608 | tf_op jit(solution)/shard_map/all_to_all | solution.py:347
  151.6 0.9 step.18
  152.5 1.2 collective-permute-start.28
  153.7 1.4 collective-permute-start.29
  155.7 0.7 collective-permute-done.28.refs_1_
  157.3 10.2 %all_to_all.74.received = f32[8,24,128]{2,1,0:T(8,128)S(1)} all-to-all(f32[8,24,128]{2,1,0:T(8,128)S(1)} %get-tuple-element.169), channel_id=1, replica_groups=mesh['region'=8,'blk'=4] {'region'}, dimensions={0} | all-to-all | bytes 196608 | tf_op jit(solution)/shard_map/all_to_all | solution.py:347
  167.5 0.9 step.19
  168.5 1.1 collective-permute-start.31
  169.6 1.4 collective-permute-start.32
  171.6 0.8 collective-permute-done.31.refs_1_
  173.2 10.2 %all_to_all.75.received = f32[8,24,128]{2,1,0:T(8,128)S(1)} all-to-all(f32[8,24,128]{2,1,0:T(8,128)S(1)} %get-tuple-element.177), channel_id=1, replica_groups=mesh['region'=8,'blk'=4] {'region'}, dimensions={0} | all-to-all | bytes 196608 | tf_op jit(solution)/shard_map/all_to_all | solution.py:347
  183.4 0.9 step.20
  184.4 1.1 collective-permute-start.34
  185.5 1.4 collective-permute-start.35
  187.5 0.7 collective-permute-done.34.refs_1_
  189.1 10.2 %all_to_all.76.received = f32[8,24,128]{2,1,0:T(8,128)S(1)} all-to-all(f32[8,24,128]{2,1,0:T(8,128)S(1)} %get-tuple-element.185), channel_id=1, replica_groups=mesh['region'=8,'blk'=4] {'region'}, dimensions={0} | all-to-all | bytes 196608 | tf_op jit(solution)/shard_map/all_to_all | solution.py:347
  199.3 0.9 step.21
  200.3 1.1 collective-permute-start.37
  201.4 1.4 collective-permute-start.38
  203.4 0.8 collective-permute-done.37.refs_1_
  205.0 10.2 %all_to_all.77.received = f32[8,24,128]{2,1,0:T(8,128)S(1)} all-to-all(f32[8,24,128]{2,1,0:T(8,128)S(1)} %get-tuple-element.193), channel_id=1, replica_groups=mesh['region'=8,'blk'=4] {'region'}, dimensions={0} | all-to-all | bytes 196608 | tf_op jit(solution)/shard_map/all_to_all | solution.py:347
  215.2 0.7 last.1
  (64 shorter events, 22.8 us)
Async XLA Ops:
  2.0 5.6 %collective-permute-start = (f32[16,128]{1,0:T(8,128)S(1)}, f32[16,128]{1,0:T(8,128)S(1)}, u32[]{:S(2)}, u32[]{:S(2)}) collective-permute-start(f32[16,128]{1,0:T(8,128)S(1)} %pad_maximum_fusion.1.refs_0_), channel_id=1, source_target_pairs={{0,1},{1,2},{2,3},{3,0},{4,5},{5,6},{6,7},{7,4},{8,9},{9,10},{10,1... | collective-permute-start | bytes 24584 | tf_op jit(solution)/shard_map/ppermute | solution.py:342
  2.5 5.1 %collective-permute-start.1 = (f32[16,128]{1,0:T(8,128)S(1)}, f32[16,128]{1,0:T(8,128)S(1)}, u32[]{:S(2)}, u32[]{:S(2)}) collective-permute-start(f32[16,128]{1,0:T(8,128)S(1)} %pad_maximum_fusion.1.refs_0_), channel_id=1, source_target_pairs={{0,2},{1,3},{2,0},{3,1},{4,6},{5,7},{6,4},{7,5},{8,10},{9,11},{10,... | collective-permute-start | bytes 24584 | tf_op jit(solution)/shard_map/ppermute | solution.py:342
  5.0 2.8 %collective-permute-start.2 = (f32[16,128]{1,0:T(8,128)S(1)}, f32[16,128]{1,0:T(8,128)S(1)}, u32[]{:S(2)}, u32[]{:S(2)}) collective-permute-start(f32[16,128]{1,0:T(8,128)S(1)} %pad_maximum_fusion.1.refs_0_), channel_id=1, source_target_pairs={{0,3},{1,0},{2,1},{3,2},{4,7},{5,4},{6,5},{7,6},{8,11},{9,8},{10,9... | collective-permute-start | bytes 24584 | tf_op jit(solution)/shard_map/ppermute | solution.py:342
  25.1 3.3 %collective-permute-start.3 = (f32[40,128]{1,0:T(8,128)S(1)}, f32[40,128]{1,0:T(8,128)S(1)}, u32[]{:S(2)}, u32[]{:S(2)}) collective-permute-start(f32[40,128]{1,0:T(8,128)S(1)} %get-tuple-element.106.own), channel_id=1, source_target_pairs={{0,1},{1,2},{2,3},{3,0},{4,5},{5,6},{6,7},{7,4},{8,9},{9,10},{10,1... | collective-permute-start | bytes 61448 | tf_op jit(solution)/shard_map/ppermute | solution.py:342
  25.2 3.8 %collective-permute-start.4 = (f32[40,128]{1,0:T(8,128)S(1)}, f32[40,128]{1,0:T(8,128)S(1)}, u32[]{:S(2)}, u32[]{:S(2)}) collective-permute-start(f32[40,128]{1,0:T(8,128)S(1)} %get-tuple-element.106.own), channel_id=1, source_target_pairs={{0,2},{1,3},{2,0},{3,1},{4,6},{5,7},{6,4},{7,5},{8,10},{9,11},{10,... | collective-permute-start | bytes 61448 | tf_op jit(solution)/shard_map/ppermute | solution.py:342
  26.5 2.8 %collective-permute-start.5 = (f32[40,128]{1,0:T(8,128)S(1)}, f32[40,128]{1,0:T(8,128)S(1)}, u32[]{:S(2)}, u32[]{:S(2)}) collective-permute-start(f32[40,128]{1,0:T(8,128)S(1)} %get-tuple-element.106.own), channel_id=1, source_target_pairs={{0,3},{1,0},{2,1},{3,2},{4,7},{5,4},{6,5},{7,6},{8,11},{9,8},{10,9... | collective-permute-start | bytes 61448 | tf_op jit(solution)/shard_map/ppermute | solution.py:342
  41.2 3.3 %collective-permute-start.6 = (f32[40,128]{1,0:T(8,128)S(1)}, f32[40,128]{1,0:T(8,128)S(1)}, u32[]{:S(2)}, u32[]{:S(2)}) collective-permute-start(f32[40,128]{1,0:T(8,128)S(1)} %get-tuple-element.112.own), channel_id=1, source_target_pairs={{0,1},{1,2},{2,3},{3,0},{4,5},{5,6},{6,7},{7,4},{8,9},{9,10},{10,1... | collective-permute-start | bytes 61448 | tf_op jit(solution)/shard_map/ppermute | solution.py:342
  41.3 3.8 %collective-permute-start.7 = (f32[40,128]{1,0:T(8,128)S(1)}, f32[40,128]{1,0:T(8,128)S(1)}, u32[]{:S(2)}, u32[]{:S(2)}) collective-permute-start(f32[40,128]{1,0:T(8,128)S(1)} %get-tuple-element.112.own), channel_id=1, source_target_pairs={{0,2},{1,3},{2,0},{3,1},{4,6},{5,7},{6,4},{7,5},{8,10},{9,11},{10,... | collective-permute-start | bytes 61448 | tf_op jit(solution)/shard_map/ppermute | solution.py:342
  42.8 2.9 %collective-permute-start.8 = (f32[40,128]{1,0:T(8,128)S(1)}, f32[40,128]{1,0:T(8,128)S(1)}, u32[]{:S(2)}, u32[]{:S(2)}) collective-permute-start(f32[40,128]{1,0:T(8,128)S(1)} %get-tuple-element.112.own), channel_id=1, source_target_pairs={{0,3},{1,0},{2,1},{3,2},{4,7},{5,4},{6,5},{7,6},{8,11},{9,8},{10,9... | collective-permute-start | bytes 61448 | tf_op jit(solution)/shard_map/ppermute | solution.py:342
  57.3 3.3 %collective-permute-start.9 = (f32[40,128]{1,0:T(8,128)S(1)}, f32[40,128]{1,0:T(8,128)S(1)}, u32[]{:S(2)}, u32[]{:S(2)}) collective-permute-start(f32[40,128]{1,0:T(8,128)S(1)} %get-tuple-element.120.own), channel_id=1, source_target_pairs={{0,1},{1,2},{2,3},{3,0},{4,5},{5,6},{6,7},{7,4},{8,9},{9,10},{10,1... | collective-permute-start | bytes 61448 | tf_op jit(solution)/shard_map/ppermute | solution.py:342
  57.3 3.9 %collective-permute-start.10 = (f32[40,128]{1,0:T(8,128)S(1)}, f32[40,128]{1,0:T(8,128)S(1)}, u32[]{:S(2)}, u32[]{:S(2)}) collective-permute-start(f32[40,128]{1,0:T(8,128)S(1)} %get-tuple-element.120.own), channel_id=1, source_target_pairs={{0,2},{1,3},{2,0},{3,1},{4,6},{5,7},{6,4},{7,5},{8,10},{9,11},{10,... | collective-permute-start | bytes 61448 | tf_op jit(solution)/shard_map/ppermute | solution.py:342
  58.3 3.0 %collective-permute-start.11 = (f32[40,128]{1,0:T(8,128)S(1)}, f32[40,128]{1,0:T(8,128)S(1)}, u32[]{:S(2)}, u32[]{:S(2)}) collective-permute-start(f32[40,128]{1,0:T(8,128)S(1)} %get-tuple-element.120.own), channel_id=1, source_target_pairs={{0,3},{1,0},{2,1},{3,2},{4,7},{5,4},{6,5},{7,6},{8,11},{9,8},{10,9... | collective-permute-start | bytes 61448 | tf_op jit(solution)/shard_map/ppermute | solution.py:342
  73.0 3.3 %collective-permute-start.12 = (f32[40,128]{1,0:T(8,128)S(1)}, f32[40,128]{1,0:T(8,128)S(1)}, u32[]{:S(2)}, u32[]{:S(2)}) collective-permute-start(f32[40,128]{1,0:T(8,128)S(1)} %get-tuple-element.128.own), channel_id=1, source_target_pairs={{0,1},{1,2},{2,3},{3,0},{4,5},{5,6},{6,7},{7,4},{8,9},{9,10},{10,1... | collective-permute-start | bytes 61448 | tf_op jit(solution)/shard_map/ppermute | solution.py:342
  73.2 3.8 %collective-permute-start.13 = (f32[40,128]{1,0:T(8,128)S(1)}, f32[40,128]{1,0:T(8,128)S(1)}, u32[]{:S(2)}, u32[]{:S(2)}) collective-permute-start(f32[40,128]{1,0:T(8,128)S(1)} %get-tuple-element.128.own), channel_id=1, source_target_pairs={{0,2},{1,3},{2,0},{3,1},{4,6},{5,7},{6,4},{7,5},{8,10},{9,11},{10,... | collective-permute-start | bytes 61448 | tf_op jit(solution)/shard_map/ppermute | solution.py:342
  74.2 2.9 %collective-permute-start.14 = (f32[40,128]{1,0:T(8,128)S(1)}, f32[40,128]{1,0:T(8,128)S(1)}, u32[]{:S(2)}, u32[]{:S(2)}) collective-permute-start(f32[40,128]{1,0:T(8,128)S(1)} %get-tuple-element.128.own), channel_id=1, source_target_pairs={{0,3},{1,0},{2,1},{3,2},{4,7},{5,4},{6,5},{7,6},{8,11},{9,8},{10,9... | collective-permute-start | bytes 61448 | tf_op jit(solution)/shard_map/ppermute | solution.py:342
  89.0 3.3 %collective-permute-start.15 = (f32[40,128]{1,0:T(8,128)S(1)}, f32[40,128]{1,0:T(8,128)S(1)}, u32[]{:S(2)}, u32[]{:S(2)}) collective-permute-start(f32[40,128]{1,0:T(8,128)S(1)} %get-tuple-element.136.own), channel_id=1, source_target_pairs={{0,1},{1,2},{2,3},{3,0},{4,5},{5,6},{6,7},{7,4},{8,9},{9,10},{10,1... | collective-permute-start | bytes 61448 | tf_op jit(solution)/shard_map/ppermute | solution.py:342
  89.0 4.0 %collective-permute-start.16 = (f32[40,128]{1,0:T(8,128)S(1)}, f32[40,128]{1,0:T(8,128)S(1)}, u32[]{:S(2)}, u32[]{:S(2)}) collective-permute-start(f32[40,128]{1,0:T(8,128)S(1)} %get-tuple-element.136.own), channel_id=1, source_target_pairs={{0,2},{1,3},{2,0},{3,1},{4,6},{5,7},{6,4},{7,5},{8,10},{9,11},{10,... | collective-permute-start | bytes 61448 | tf_op jit(solution)/shard_map/ppermute | solution.py:342
  90.1 3.0 %collective-permute-start.17 = (f32[40,128]{1,0:T(8,128)S(1)}, f32[40,128]{1,0:T(8,128)S(1)}, u32[]{:S(2)}, u32[]{:S(2)}) collective-permute-start(f32[40,128]{1,0:T(8,128)S(1)} %get-tuple-element.136.own), channel_id=1, source_target_pairs={{0,3},{1,0},{2,1},{3,2},{4,7},{5,4},{6,5},{7,6},{8,11},{9,8},{10,9... | collective-permute-start | bytes 61448 | tf_op jit(solution)/shard_map/ppermute | solution.py:342
  104.8 3.3 %collective-permute-start.18 = (f32[40,128]{1,0:T(8,128)S(1)}, f32[40,128]{1,0:T(8,128)S(1)}, u32[]{:S(2)}, u32[]{:S(2)}) collective-permute-start(f32[40,128]{1,0:T(8,128)S(1)} %get-tuple-element.144.own), channel_id=1, source_target_pairs={{0,1},{1,2},{2,3},{3,0},{4,5},{5,6},{6,7},{7,4},{8,9},{9,10},{10,1... | collective-permute-start | bytes 61448 | tf_op jit(solution)/shard_map/ppermute | solution.py:342
  105.0 3.9 %collective-permute-start.19 = (f32[40,128]{1,0:T(8,128)S(1)}, f32[40,128]{1,0:T(8,128)S(1)}, u32[]{:S(2)}, u32[]{:S(2)}) collective-permute-start(f32[40,128]{1,0:T(8,128)S(1)} %get-tuple-element.144.own), channel_id=1, source_target_pairs={{0,2},{1,3},{2,0},{3,1},{4,6},{5,7},{6,4},{7,5},{8,10},{9,11},{10,... | collective-permute-start | bytes 61448 | tf_op jit(solution)/shard_map/ppermute | solution.py:342
  106.0 2.9 %collective-permute-start.20 = (f32[40,128]{1,0:T(8,128)S(1)}, f32[40,128]{1,0:T(8,128)S(1)}, u32[]{:S(2)}, u32[]{:S(2)}) collective-permute-start(f32[40,128]{1,0:T(8,128)S(1)} %get-tuple-element.144.own), channel_id=1, source_target_pairs={{0,3},{1,0},{2,1},{3,2},{4,7},{5,4},{6,5},{7,6},{8,11},{9,8},{10,9... | collective-permute-start | bytes 61448 | tf_op jit(solution)/shard_map/ppermute | solution.py:342
  120.8 3.3 %collective-permute-start.21 = (f32[40,128]{1,0:T(8,128)S(1)}, f32[40,128]{1,0:T(8,128)S(1)}, u32[]{:S(2)}, u32[]{:S(2)}) collective-permute-start(f32[40,128]{1,0:T(8,128)S(1)} %get-tuple-element.152.own), channel_id=1, source_target_pairs={{0,1},{1,2},{2,3},{3,0},{4,5},{5,6},{6,7},{7,4},{8,9},{9,10},{10,1... | collective-permute-start | bytes 61448 | tf_op jit(solution)/shard_map/ppermute | solution.py:342
  120.8 4.0 %collective-permute-start.22 = (f32[40,128]{1,0:T(8,128)S(1)}, f32[40,128]{1,0:T(8,128)S(1)}, u32[]{:S(2)}, u32[]{:S(2)}) collective-permute-start(f32[40,128]{1,0:T(8,128)S(1)} %get-tuple-element.152.own), channel_id=1, source_target_pairs={{0,2},{1,3},{2,0},{3,1},{4,6},{5,7},{6,4},{7,5},{8,10},{9,11},{10,... | collective-permute-start | bytes 61448 | tf_op jit(solution)/shard_map/ppermute | solution.py:342
  121.9 2.9 %collective-permute-start.23 = (f32[40,128]{1,0:T(8,128)S(1)}, f32[40,128]{1,0:T(8,128)S(1)}, u32[]{:S(2)}, u32[]{:S(2)}) collective-permute-start(f32[40,128]{1,0:T(8,128)S(1)} %get-tuple-element.152.own), channel_id=1, source_target_pairs={{0,3},{1,0},{2,1},{3,2},{4,7},{5,4},{6,5},{7,6},{8,11},{9,8},{10,9... | collective-permute-start | bytes 61448 | tf_op jit(solution)/shard_map/ppermute | solution.py:342
  136.5 3.3 %collective-permute-start.24 = (f32[40,128]{1,0:T(8,128)S(1)}, f32[40,128]{1,0:T(8,128)S(1)}, u32[]{:S(2)}, u32[]{:S(2)}) collective-permute-start(f32[40,128]{1,0:T(8,128)S(1)} %get-tuple-element.160.own), channel_id=1, source_target_pairs={{0,1},{1,2},{2,3},{3,0},{4,5},{5,6},{6,7},{7,4},{8,9},{9,10},{10,1... | collective-permute-start | bytes 61448 | tf_op jit(solution)/shard_map/ppermute | solution.py:342
  136.6 3.8 %collective-permute-start.25 = (f32[40,128]{1,0:T(8,128)S(1)}, f32[40,128]{1,0:T(8,128)S(1)}, u32[]{:S(2)}, u32[]{:S(2)}) collective-permute-start(f32[40,128]{1,0:T(8,128)S(1)} %get-tuple-element.160.own), channel_id=1, source_target_pairs={{0,2},{1,3},{2,0},{3,1},{4,6},{5,7},{6,4},{7,5},{8,10},{9,11},{10,... | collective-permute-start | bytes 61448 | tf_op jit(solution)/shard_map/ppermute | solution.py:342
  137.8 2.9 %collective-permute-start.26 = (f32[40,128]{1,0:T(8,128)S(1)}, f32[40,128]{1,0:T(8,128)S(1)}, u32[]{:S(2)}, u32[]{:S(2)}) collective-permute-start(f32[40,128]{1,0:T(8,128)S(1)} %get-tuple-element.160.own), channel_id=1, source_target_pairs={{0,3},{1,0},{2,1},{3,2},{4,7},{5,4},{6,5},{7,6},{8,11},{9,8},{10,9... | collective-permute-start | bytes 61448 | tf_op jit(solution)/shard_map/ppermute | solution.py:342
  152.5 3.3 %collective-permute-start.27 = (f32[40,128]{1,0:T(8,128)S(1)}, f32[40,128]{1,0:T(8,128)S(1)}, u32[]{:S(2)}, u32[]{:S(2)}) collective-permute-start(f32[40,128]{1,0:T(8,128)S(1)} %get-tuple-element.168.own), channel_id=1, source_target_pairs={{0,1},{1,2},{2,3},{3,0},{4,5},{5,6},{6,7},{7,4},{8,9},{9,10},{10,1... | collective-permute-start | bytes 61448 | tf_op jit(solution)/shard_map/ppermute | solution.py:342
  152.5 3.9 %collective-permute-start.28 = (f32[40,128]{1,0:T(8,128)S(1)}, f32[40,128]{1,0:T(8,128)S(1)}, u32[]{:S(2)}, u32[]{:S(2)}) collective-permute-start(f32[40,128]{1,0:T(8,128)S(1)} %get-tuple-element.168.own), channel_id=1, source_target_pairs={{0,2},{1,3},{2,0},{3,1},{4,6},{5,7},{6,4},{7,5},{8,10},{9,11},{10,... | collective-permute-start | bytes 61448 | tf_op jit(solution)/shard_map/ppermute | solution.py:342
  153.7 2.8 %collective-permute-start.29 = (f32[40,128]{1,0:T(8,128)S(1)}, f32[40,128]{1,0:T(8,128)S(1)}, u32[]{:S(2)}, u32[]{:S(2)}) collective-permute-start(f32[40,128]{1,0:T(8,128)S(1)} %get-tuple-element.168.own), channel_id=1, source_target_pairs={{0,3},{1,0},{2,1},{3,2},{4,7},{5,4},{6,5},{7,6},{8,11},{9,8},{10,9... | collective-permute-start | bytes 61448 | tf_op jit(solution)/shard_map/ppermute | solution.py:342
  168.4 3.3 %collective-permute-start.30 = (f32[40,128]{1,0:T(8,128)S(1)}, f32[40,128]{1,0:T(8,128)S(1)}, u32[]{:S(2)}, u32[]{:S(2)}) collective-permute-start(f32[40,128]{1,0:T(8,128)S(1)} %get-tuple-element.176.own), channel_id=1, source_target_pairs={{0,1},{1,2},{2,3},{3,0},{4,5},{5,6},{6,7},{7,4},{8,9},{9,10},{10,1... | collective-permute-start | bytes 61448 | tf_op jit(solution)/shard_map/ppermute | solution.py:342
  168.5 3.9 %collective-permute-start.31 = (f32[40,128]{1,0:T(8,128)S(1)}, f32[40,128]{1,0:T(8,128)S(1)}, u32[]{:S(2)}, u32[]{:S(2)}) collective-permute-start(f32[40,128]{1,0:T(8,128)S(1)} %get-tuple-element.176.own), channel_id=1, source_target_pairs={{0,2},{1,3},{2,0},{3,1},{4,6},{5,7},{6,4},{7,5},{8,10},{9,11},{10,... | collective-permute-start | bytes 61448 | tf_op jit(solution)/shard_map/ppermute | solution.py:342
  169.6 2.9 %collective-permute-start.32 = (f32[40,128]{1,0:T(8,128)S(1)}, f32[40,128]{1,0:T(8,128)S(1)}, u32[]{:S(2)}, u32[]{:S(2)}) collective-permute-start(f32[40,128]{1,0:T(8,128)S(1)} %get-tuple-element.176.own), channel_id=1, source_target_pairs={{0,3},{1,0},{2,1},{3,2},{4,7},{5,4},{6,5},{7,6},{8,11},{9,8},{10,9... | collective-permute-start | bytes 61448 | tf_op jit(solution)/shard_map/ppermute | solution.py:342
  184.2 3.3 %collective-permute-start.33 = (f32[40,128]{1,0:T(8,128)S(1)}, f32[40,128]{1,0:T(8,128)S(1)}, u32[]{:S(2)}, u32[]{:S(2)}) collective-permute-start(f32[40,128]{1,0:T(8,128)S(1)} %get-tuple-element.184.own), channel_id=1, source_target_pairs={{0,1},{1,2},{2,3},{3,0},{4,5},{5,6},{6,7},{7,4},{8,9},{9,10},{10,1... | collective-permute-start | bytes 61448 | tf_op jit(solution)/shard_map/ppermute | solution.py:342
  184.4 3.8 %collective-permute-start.34 = (f32[40,128]{1,0:T(8,128)S(1)}, f32[40,128]{1,0:T(8,128)S(1)}, u32[]{:S(2)}, u32[]{:S(2)}) collective-permute-start(f32[40,128]{1,0:T(8,128)S(1)} %get-tuple-element.184.own), channel_id=1, source_target_pairs={{0,2},{1,3},{2,0},{3,1},{4,6},{5,7},{6,4},{7,5},{8,10},{9,11},{10,... | collective-permute-start | bytes 61448 | tf_op jit(solution)/shard_map/ppermute | solution.py:342
  185.5 2.8 %collective-permute-start.35 = (f32[40,128]{1,0:T(8,128)S(1)}, f32[40,128]{1,0:T(8,128)S(1)}, u32[]{:S(2)}, u32[]{:S(2)}) collective-permute-start(f32[40,128]{1,0:T(8,128)S(1)} %get-tuple-element.184.own), channel_id=1, source_target_pairs={{0,3},{1,0},{2,1},{3,2},{4,7},{5,4},{6,5},{7,6},{8,11},{9,8},{10,9... | collective-permute-start | bytes 61448 | tf_op jit(solution)/shard_map/ppermute | solution.py:342
  200.1 3.3 %collective-permute-start.36 = (f32[40,128]{1,0:T(8,128)S(1)}, f32[40,128]{1,0:T(8,128)S(1)}, u32[]{:S(2)}, u32[]{:S(2)}) collective-permute-start(f32[40,128]{1,0:T(8,128)S(1)} %get-tuple-element.192.own), channel_id=1, source_target_pairs={{0,1},{1,2},{2,3},{3,0},{4,5},{5,6},{6,7},{7,4},{8,9},{9,10},{10,1... | collective-permute-start | bytes 61448 | tf_op jit(solution)/shard_map/ppermute | solution.py:342
  200.3 3.9 %collective-permute-start.37 = (f32[40,128]{1,0:T(8,128)S(1)}, f32[40,128]{1,0:T(8,128)S(1)}, u32[]{:S(2)}, u32[]{:S(2)}) collective-permute-start(f32[40,128]{1,0:T(8,128)S(1)} %get-tuple-element.192.own), channel_id=1, source_target_pairs={{0,2},{1,3},{2,0},{3,1},{4,6},{5,7},{6,4},{7,5},{8,10},{9,11},{10,... | collective-permute-start | bytes 61448 | tf_op jit(solution)/shard_map/ppermute | solution.py:342
  201.4 2.8 %collective-permute-start.38 = (f32[40,128]{1,0:T(8,128)S(1)}, f32[40,128]{1,0:T(8,128)S(1)}, u32[]{:S(2)}, u32[]{:S(2)}) collective-permute-start(f32[40,128]{1,0:T(8,128)S(1)} %get-tuple-element.192.own), channel_id=1, source_target_pairs={{0,3},{1,0},{2,1},{3,2},{4,7},{5,4},{6,5},{7,6},{8,11},{9,8},{10,9... | collective-permute-start | bytes 61448 | tf_op jit(solution)/shard_map/ppermute | solution.py:342

commit v4 on v3

--- a/solution.py
+++ b/solution.py
@@ -11,6 +11,7 @@
 SPOTS = {(2, 1): 0, (1, 0): 0, (1, 1): 1, (-1, -1): 0, (-1, 0): 1, (-2, -1): 1}
 VMEM_LIMIT = 16 * 1024 * 1024
 PIECES = 8
+LOAD_LIMIT = 47 * 1024 * 1024
 
 vmem = pl.BlockSpec(memory_space=pltpu.VMEM)
 hbm = pl.BlockSpec(memory_space=pltpu.HBM)
@@ -30,13 +31,6 @@
     high = value.astype(jnp.bfloat16).astype(jnp.float32)
     middle = (value - high).astype(jnp.bfloat16).astype(jnp.float32)
     return high, middle, (value - high) - middle
-
-
-def selectors(tiles, width):
-    shape = (tiles // 2, width, 2 * width)
-    pair, row, lane = (lax.broadcasted_iota(jnp.int32, shape, n) for n in range(3))
-    wanted = 2 * pair + lane // width
-    return ((row % tiles == wanted) & (row < 3 * tiles)).astype(jnp.bfloat16)
 
 
 def copy_in(source, target, sem):
@@ -74,7 +68,7 @@
         )
 
 
-def backward(jac, weighted, picks, spots, back, square, arrived=lambda t: None):
+def backward(jac, weighted, picks, spots, back, square):
     tiles, slots, width, _ = jac.shape
     value = weighted[...]
     terms = three_terms(value)
@@ -82,7 +76,6 @@
     turned = jnp.transpose(jnp.concatenate([*terms, rest], axis=0))
     turned = turned.astype(jnp.bfloat16)
     for t in range(tiles):
-        arrived(t)
         if t % 2 == 0:
             both = jnp.dot(turned, picks[t // 2], preferred_element_type=jnp.float32)
         column = rows8(both[:, t % 2 * width : (t % 2 + 1) * width])
@@ -124,21 +117,30 @@
     out[region] = blank
 
 
+def load_kernel(jac, held, picks, sems):
+    step = jac.shape[0] // PIECES
+    pieces = [pl.ds(n * step, step) for n in range(PIECES)]
+    copies = [
+        copy_in(jac.at[piece], held.at[piece], sems.at[n])
+        for n, piece in enumerate(pieces)
+    ]
+    for copy in copies:
+        copy.start()
+    tiles, width = jac.shape[0], jac.shape[-1]
+    row = lax.broadcasted_iota(jnp.int32, picks.shape[1:], 0)
+    half = lax.broadcasted_iota(jnp.int32, picks.shape[1:], 1) // width
+    apart = jnp.where(row < 3 * tiles, row % tiles - half, -1)
+    for pair in range(picks.shape[0]):
+        picks[pair] = jnp.where(apart == 2 * pair, 1.0, 0.0).astype(jnp.bfloat16)
+    for copy in copies:
+        copy.wait()
+
+
 def diag_kernel(jac, vectors, picks, *refs):
-    ins, refs = refs[:-8], refs[-8:]
-    out, weight, spots, held, lookup, fits, back, sems = refs
+    ins, (out, weight, spots, lookup, fits, back) = refs[:-6], refs[-6:]
     tiles, slots, width, _ = jac.shape
     blocks = len(ins)
     per_dev = tiles // blocks
-    step = tiles // PIECES
-    pieces = [
-        copy_in(
-            jac.at[pl.ds(n * step, step)], held.at[pl.ds(n * step, step)], sems.at[n]
-        )
-        for n in range(PIECES)
-    ]
-    for copy in pieces:
-        copy.start()
     group = lax.axis_index("blk")
     for shift, part in enumerate(ins):
         source = lax.rem(group + (blocks - shift), blocks)
@@ -157,12 +159,7 @@
     names = names[: spots.shape[0]].astype(jnp.int32)
     column = lax.broadcasted_iota(jnp.int32, names.shape, 0)
     spots[...] = jnp.where(column == names, 1.0, 0.0).astype(jnp.bfloat16)
-
-    def arrived(t):
-        if t % step == 0:
-            pieces[t // step].wait()
-
-    squares = backward(held, weight, picks, spots, back, True, arrived)
+    squares = backward(jac, weight, picks, spots, back, True)
     publish(jnp.concatenate([squares, vectors[...]], axis=0), out)
 
 
@@ -355,22 +352,33 @@
     kept_shape = (extent + SUB, width)
     halo_shape, own_shape = (extent, width), (per_dev, width)
 
-    fits = jnp.pad(pattern, ((0, 0), (0, width - pattern.shape[1]))).astype(f32)
-    vectors = jnp.concatenate([bus_diag, right_side], axis=0)
-    mine = jnp.concatenate([branch_weight, fits], axis=0)
-    picks = selectors(tiles, width)
-    setup, weight, spots, jac, lookup = call(
+    spare = width - pattern.shape[1]
+    small = [branch_weight, jnp.pad(pattern, ((0, 0), (0, spare))), bus_diag, right_side]
+    packed = sum(
+        jnp.pad(value, ((n * per_dev, (3 - n) * per_dev), (0, 0))).astype(f32)
+        for n, value in enumerate(small)
+    )
+    packed = lax.optimization_barrier(packed)
+    mine, vectors = packed[: 2 * per_dev], packed[2 * per_dev :]
+    parts = [mine] + across_blk(mine)
+    jac, picks = call(
+        load_kernel,
+        [
+            jac.shape,
+            jax.ShapeDtypeStruct((tiles // 2, width, 2 * width), jnp.bfloat16),
+        ],
+        [pltpu.SemaphoreType.DMA((PIECES,))], [hbm], "load", flops, moved, LOAD_LIMIT,
+    )(jac)
+    setup, weight, spots, lookup = call(
         diag_kernel,
         [
             (regions, extent + 2 * per_dev, width), (tiles, width),
-            jax.ShapeDtypeStruct((extent, 4 * tiles * slots), jnp.bfloat16), jac.shape,
+            jax.ShapeDtypeStruct((extent, 4 * tiles * slots), jnp.bfloat16),
             jax.ShapeDtypeStruct((slots, tiles, width), jnp.int32),
         ],
-        [
-            pltpu.VMEM((tiles, width), f32), back, pltpu.SemaphoreType.DMA((PIECES,)),
-        ],
-        [hbm] + [vmem] * (2 + blocks), "diagonal", flops, moved, 47 * 1024 * 1024,
-    )(jac, vectors, picks, mine, *across_blk(mine))
+        [pltpu.VMEM((tiles, width), f32), back],
+        [vmem] * (3 + blocks), "diagonal", flops, moved,
+    )(jac, vectors, picks, *parts)
     setup = across_region(setup)
     out, diag, precond, resid = call(
         first_kernel, [(row_count, width), halo_shape, halo_shape, halo_shape],

time: 217 us -> 212 us (0.977)
    pallas_call x0 -> x1, Pallas kernels: none -> 2.22 us  [body(): call(load_kernel, [jac.shape, jax.ShapeDtypeStruct((tiles // 2, width, 2...]
  transfers between devices with their start and end apart: 39 -> 39, of which waited for: 34 -> 31; matrix products, arithmetic and copies ran while one was open for 1% -> 0% of each run, Pallas kernels for 0% -> 1%
where the time goes in v4:
time: 212 us
  blocking collectives  135 us (64%)
  starting transfers between devices  35.3 us (17%)
  Pallas kernels  21.5 us (10%)
  waiting for transfers between devices  18.8 us (9%)
    all_to_all x13, blocking collectives, across_region(): return lax.all_to_all(chunks, 'region', 0, 0, tiled=True)  135 us
    ppermute x39, starting transfers between devices, across_blk(): lax.ppermute(value, 'blk', [(i, (i + k) % blocks) for i in range(blocks)])  35.3 us
    ppermute x39, waiting for transfers between devices, across_blk(): lax.ppermute(value, 'blk', [(i, (i + k) % blocks) for i in range(blocks)])  18.8 us
    pallas_call x11, Pallas kernels, step(): call(step_kernel, [(row_count, width), halo_shape, halo_shape, own_shape,...  8.82 us
    pallas_call x12, Pallas kernels, image_of(): call(back_kernel, [chunk, kept_shape], [pltpu.VMEM((tiles, width), f32),...  8.21 us
  transfers between devices with their start and end apart: 39, of which 31 were waited for; matrix products, arithmetic and copies ran while one was open for 0% of the time, Pallas kernels for 1%

profile of v4, /device:TPU:0, one launch (start us, length us, event | category | flops | bytes accessed | tf_op | source)
XLA Modules:
  0.0 211.7 jit_solution(12645791552567004044)
XLA Ops:
  0.6 0.7 fusion.2
  1.9 2.6 %collective-permute-start.1 = (f32[16,128]{1,0:T(8,128)S(1)}, f32[16,128]{1,0:T(8,128)S(1)}, u32[]{:S(2)}, u32[]{:S(2)}) collective-permute-start(f32[16,128]{1,0:T(8,128)S(1)} %get-tuple-element.202.refs_0_), channel_id=1, source_target_pairs={{0,2},{1,3},{2,0},{3,1},{4,6},{5,7},{6,4},{7,5},{8,10},{9,11},{10,... | collective-permute-start | bytes 24584 | tf_op jit(solution)/shard_map/ppermute | solution.py:339
  4.5 1.4 collective-permute-start.2
  5.8 2.2 %load.1 = (f32[32,2,128,128]{3,2,1,0:T(8,128)S(1)}, bf16[16,128,256]{2,1,0:T(8,128)(2,1)S(1)}) custom-call(f32[32,2,128,128]{3,2,1,0:T(8,128)} %jac.1), custom_call_target="tpu_custom_call" | custom-call | flops 4194304 | bytes 4194304 | tf_op jit(solution)/shard_map/load/pallas_call | solution.py:364
  8.1 0.8 diagonal.1
  8.9 13.2 %all_to_all.65.received = f32[8,40,128]{2,1,0:T(8,128)S(1)} all-to-all(f32[8,40,128]{2,1,0:T(8,128)S(1)} %get-tuple-element.107), channel_id=1, replica_groups=mesh['region'=8,'blk'=4] {'region'}, dimensions={0} | all-to-all | bytes 327680 | tf_op jit(solution)/shard_map/all_to_all | solution.py:344
  22.9 1.3 collective-permute-start.4
  24.2 1.4 collective-permute-start.5
  27.7 10.2 %all_to_all.66.received = f32[8,24,128]{2,1,0:T(8,128)S(1)} all-to-all(f32[8,24,128]{2,1,0:T(8,128)S(1)} %get-tuple-element.109), channel_id=1, replica_groups=mesh['region'=8,'blk'=4] {'region'}, dimensions={0} | all-to-all | bytes 196608 | tf_op jit(solution)/shard_map/all_to_all | solution.py:344
  37.9 0.8 step.11
  38.8 1.3 collective-permute-start.7
  40.1 1.4 collective-permute-start.8
  43.7 10.2 %all_to_all.67.received = f32[8,24,128]{2,1,0:T(8,128)S(1)} all-to-all(f32[8,24,128]{2,1,0:T(8,128)S(1)} %get-tuple-element.115), channel_id=1, replica_groups=mesh['region'=8,'blk'=4] {'region'}, dimensions={0} | all-to-all | bytes 196608 | tf_op jit(solution)/shard_map/all_to_all | solution.py:344
  53.8 0.8 step.12
  54.7 0.9 collective-permute-start.10
  55.6 1.3 collective-permute-start.11
  57.0 0.9 collective-permute-done.9.refs_0_
  57.9 0.8 collective-permute-done.10.refs_1_
  59.4 10.0 %all_to_all.68.received = f32[8,24,128]{2,1,0:T(8,128)S(1)} all-to-all(f32[8,24,128]{2,1,0:T(8,128)S(1)} %get-tuple-element.123), channel_id=1, replica_groups=mesh['region'=8,'blk'=4] {'region'}, dimensions={0} | all-to-all | bytes 196608 | tf_op jit(solution)/shard_map/all_to_all | solution.py:344
  69.4 0.8 step.13
  70.4 1.2 collective-permute-start.13
  71.5 1.4 collective-permute-start.14
  75.1 10.2 %all_to_all.69.received = f32[8,24,128]{2,1,0:T(8,128)S(1)} all-to-all(f32[8,24,128]{2,1,0:T(8,128)S(1)} %get-tuple-element.131), channel_id=1, replica_groups=mesh['region'=8,'blk'=4] {'region'}, dimensions={0} | all-to-all | bytes 196608 | tf_op jit(solution)/shard_map/all_to_all | solution.py:344
  85.3 0.8 step.14
  86.2 0.9 collective-permute-start.16
  87.1 1.4 collective-permute-start.17
  88.4 1.0 collective-permute-done.15.refs_0_
  89.4 0.7 collective-permute-done.16.refs_1_
  90.8 10.0 %all_to_all.70.received = f32[8,24,128]{2,1,0:T(8,128)S(1)} all-to-all(f32[8,24,128]{2,1,0:T(8,128)S(1)} %get-tuple-element.139), channel_id=1, replica_groups=mesh['region'=8,'blk'=4] {'region'}, dimensions={0} | all-to-all | bytes 196608 | tf_op jit(solution)/shard_map/all_to_all | solution.py:344
  100.8 0.8 step.15
  101.8 1.2 collective-permute-start.19
  103.0 1.4 collective-permute-start.20
  106.6 10.2 %all_to_all.71.received = f32[8,24,128]{2,1,0:T(8,128)S(1)} all-to-all(f32[8,24,128]{2,1,0:T(8,128)S(1)} %get-tuple-element.147), channel_id=1, replica_groups=mesh['region'=8,'blk'=4] {'region'}, dimensions={0} | all-to-all | bytes 196608 | tf_op jit(solution)/shard_map/all_to_all | solution.py:344
  116.8 0.8 step.16
  117.6 0.9 collective-permute-start.22
  118.5 1.3 collective-permute-start.23
  119.8 1.0 collective-permute-done.21.refs_0_
  122.2 10.0 %all_to_all.72.received = f32[8,24,128]{2,1,0:T(8,128)S(1)} all-to-all(f32[8,24,128]{2,1,0:T(8,128)S(1)} %get-tuple-element.155), channel_id=1, replica_groups=mesh['region'=8,'blk'=4] {'region'}, dimensions={0} | all-to-all | bytes 196608 | tf_op jit(solution)/shard_map/all_to_all | solution.py:344
  132.2 0.8 step.17
  133.2 1.2 collective-permute-start.25
  134.4 1.4 collective-permute-start.26
  136.2 0.7 collective-permute-done.25.refs_1_
  138.0 10.2 %all_to_all.73.received = f32[8,24,128]{2,1,0:T(8,128)S(1)} all-to-all(f32[8,24,128]{2,1,0:T(8,128)S(1)} %get-tuple-element.163), channel_id=1, replica_groups=mesh['region'=8,'blk'=4] {'region'}, dimensions={0} | all-to-all | bytes 196608 | tf_op jit(solution)/shard_map/all_to_all | solution.py:344
  148.1 0.8 step.18
  149.0 0.9 collective-permute-start.28
  149.9 1.3 collective-permute-start.29
  151.2 1.0 collective-permute-done.27.refs_0_
  152.2 0.7 collective-permute-done.28.refs_1_
  153.6 10.0 %all_to_all.74.received = f32[8,24,128]{2,1,0:T(8,128)S(1)} all-to-all(f32[8,24,128]{2,1,0:T(8,128)S(1)} %get-tuple-element.171), channel_id=1, replica_groups=mesh['region'=8,'blk'=4] {'region'}, dimensions={0} | all-to-all | bytes 196608 | tf_op jit(solution)/shard_map/all_to_all | solution.py:344
  163.6 0.8 step.19
  164.6 1.2 collective-permute-start.31
  165.8 1.4 collective-permute-start.32
  169.3 10.2 %all_to_all.75.received = f32[8,24,128]{2,1,0:T(8,128)S(1)} all-to-all(f32[8,24,128]{2,1,0:T(8,128)S(1)} %get-tuple-element.179), channel_id=1, replica_groups=mesh['region'=8,'blk'=4] {'region'}, dimensions={0} | all-to-all | bytes 196608 | tf_op jit(solution)/shard_map/all_to_all | solution.py:344
  179.5 0.8 step.20
  180.4 0.9 collective-permute-start.34
  181.3 1.3 collective-permute-start.35
  182.7 1.0 collective-permute-done.33.refs_0_
  183.6 0.7 collective-permute-done.34.refs_1_
  185.0 10.0 %all_to_all.76.received = f32[8,24,128]{2,1,0:T(8,128)S(1)} all-to-all(f32[8,24,128]{2,1,0:T(8,128)S(1)} %get-tuple-element.187), channel_id=1, replica_groups=mesh['region'=8,'blk'=4] {'region'}, dimensions={0} | all-to-all | bytes 196608 | tf_op jit(solution)/shard_map/all_to_all | solution.py:344
  195.0 0.8 step.21
  196.0 1.2 collective-permute-start.37
  197.2 1.4 collective-permute-start.38
  200.8 10.2 %all_to_all.77.received = f32[8,24,128]{2,1,0:T(8,128)S(1)} all-to-all(f32[8,24,128]{2,1,0:T(8,128)S(1)} %get-tuple-element.195), channel_id=1, replica_groups=mesh['region'=8,'blk'=4] {'region'}, dimensions={0} | all-to-all | bytes 196608 | tf_op jit(solution)/shard_map/all_to_all | solution.py:344
  211.0 0.7 last.1
  (58 shorter events, 21.0 us)
Async XLA Ops:
  1.4 6.7 %collective-permute-start = (f32[16,128]{1,0:T(8,128)S(1)}, f32[16,128]{1,0:T(8,128)S(1)}, u32[]{:S(2)}, u32[]{:S(2)}) collective-permute-start(f32[16,128]{1,0:T(8,128)S(1)} %get-tuple-element.202.refs_0_), channel_id=1, source_target_pairs={{0,1},{1,2},{2,3},{3,0},{4,5},{5,6},{6,7},{7,4},{8,9},{9,10},{10,1... | collective-permute-start | bytes 24584 | tf_op jit(solution)/shard_map/ppermute | solution.py:339
  1.9 6.2 %collective-permute-start.1 = (f32[16,128]{1,0:T(8,128)S(1)}, f32[16,128]{1,0:T(8,128)S(1)}, u32[]{:S(2)}, u32[]{:S(2)}) collective-permute-start(f32[16,128]{1,0:T(8,128)S(1)} %get-tuple-element.202.refs_0_), channel_id=1, source_target_pairs={{0,2},{1,3},{2,0},{3,1},{4,6},{5,7},{6,4},{7,5},{8,10},{9,11},{10,... | collective-permute-start | bytes 24584 | tf_op jit(solution)/shard_map/ppermute | solution.py:339
  4.5 3.6 %collective-permute-start.2 = (f32[16,128]{1,0:T(8,128)S(1)}, f32[16,128]{1,0:T(8,128)S(1)}, u32[]{:S(2)}, u32[]{:S(2)}) collective-permute-start(f32[16,128]{1,0:T(8,128)S(1)} %get-tuple-element.202.refs_0_), channel_id=1, source_target_pairs={{0,3},{1,0},{2,1},{3,2},{4,7},{5,4},{6,5},{7,6},{8,11},{9,8},{10,9... | collective-permute-start | bytes 24584 | tf_op jit(solution)/shard_map/ppermute | solution.py:339
  22.8 3.3 %collective-permute-start.3 = (f32[40,128]{1,0:T(8,128)S(1)}, f32[40,128]{1,0:T(8,128)S(1)}, u32[]{:S(2)}, u32[]{:S(2)}) collective-permute-start(f32[40,128]{1,0:T(8,128)S(1)} %get-tuple-element.108.own), channel_id=1, source_target_pairs={{0,1},{1,2},{2,3},{3,0},{4,5},{5,6},{6,7},{7,4},{8,9},{9,10},{10,1... | collective-permute-start | bytes 61448 | tf_op jit(solution)/shard_map/ppermute | solution.py:339
  22.9 3.8 %collective-permute-start.4 = (f32[40,128]{1,0:T(8,128)S(1)}, f32[40,128]{1,0:T(8,128)S(1)}, u32[]{:S(2)}, u32[]{:S(2)}) collective-permute-start(f32[40,128]{1,0:T(8,128)S(1)} %get-tuple-element.108.own), channel_id=1, source_target_pairs={{0,2},{1,3},{2,0},{3,1},{4,6},{5,7},{6,4},{7,5},{8,10},{9,11},{10,... | collective-permute-start | bytes 61448 | tf_op jit(solution)/shard_map/ppermute | solution.py:339
  24.2 2.9 %collective-permute-start.5 = (f32[40,128]{1,0:T(8,128)S(1)}, f32[40,128]{1,0:T(8,128)S(1)}, u32[]{:S(2)}, u32[]{:S(2)}) collective-permute-start(f32[40,128]{1,0:T(8,128)S(1)} %get-tuple-element.108.own), channel_id=1, source_target_pairs={{0,3},{1,0},{2,1},{3,2},{4,7},{5,4},{6,5},{7,6},{8,11},{9,8},{10,9... | collective-permute-start | bytes 61448 | tf_op jit(solution)/shard_map/ppermute | solution.py:339
  38.7 3.3 %collective-permute-start.6 = (f32[40,128]{1,0:T(8,128)S(1)}, f32[40,128]{1,0:T(8,128)S(1)}, u32[]{:S(2)}, u32[]{:S(2)}) collective-permute-start(f32[40,128]{1,0:T(8,128)S(1)} %get-tuple-element.114.own), channel_id=1, source_target_pairs={{0,1},{1,2},{2,3},{3,0},{4,5},{5,6},{6,7},{7,4},{8,9},{9,10},{10,1... | collective-permute-start | bytes 61448 | tf_op jit(solution)/shard_map/ppermute | solution.py:339
  38.8 3.8 %collective-permute-start.7 = (f32[40,128]{1,0:T(8,128)S(1)}, f32[40,128]{1,0:T(8,128)S(1)}, u32[]{:S(2)}, u32[]{:S(2)}) collective-permute-start(f32[40,128]{1,0:T(8,128)S(1)} %get-tuple-element.114.own), channel_id=1, source_target_pairs={{0,2},{1,3},{2,0},{3,1},{4,6},{5,7},{6,4},{7,5},{8,10},{9,11},{10,... | collective-permute-start | bytes 61448 | tf_op jit(solution)/shard_map/ppermute | solution.py:339
  40.1 2.9 %collective-permute-start.8 = (f32[40,128]{1,0:T(8,128)S(1)}, f32[40,128]{1,0:T(8,128)S(1)}, u32[]{:S(2)}, u32[]{:S(2)}) collective-permute-start(f32[40,128]{1,0:T(8,128)S(1)} %get-tuple-element.114.own), channel_id=1, source_target_pairs={{0,3},{1,0},{2,1},{3,2},{4,7},{5,4},{6,5},{7,6},{8,11},{9,8},{10,9... | collective-permute-start | bytes 61448 | tf_op jit(solution)/shard_map/ppermute | solution.py:339
  54.6 3.3 %collective-permute-start.9 = (f32[40,128]{1,0:T(8,128)S(1)}, f32[40,128]{1,0:T(8,128)S(1)}, u32[]{:S(2)}, u32[]{:S(2)}) collective-permute-start(f32[40,128]{1,0:T(8,128)S(1)} %get-tuple-element.122.own), channel_id=1, source_target_pairs={{0,1},{1,2},{2,3},{3,0},{4,5},{5,6},{6,7},{7,4},{8,9},{9,10},{10,1... | collective-permute-start | bytes 61448 | tf_op jit(solution)/shard_map/ppermute | solution.py:339
  54.7 4.0 %collective-permute-start.10 = (f32[40,128]{1,0:T(8,128)S(1)}, f32[40,128]{1,0:T(8,128)S(1)}, u32[]{:S(2)}, u32[]{:S(2)}) collective-permute-start(f32[40,128]{1,0:T(8,128)S(1)} %get-tuple-element.122.own), channel_id=1, source_target_pairs={{0,2},{1,3},{2,0},{3,1},{4,6},{5,7},{6,4},{7,5},{8,10},{9,11},{10,... | collective-permute-start | bytes 61448 | tf_op jit(solution)/shard_map/ppermute | solution.py:339
  55.6 3.0 %collective-permute-start.11 = (f32[40,128]{1,0:T(8,128)S(1)}, f32[40,128]{1,0:T(8,128)S(1)}, u32[]{:S(2)}, u32[]{:S(2)}) collective-permute-start(f32[40,128]{1,0:T(8,128)S(1)} %get-tuple-element.122.own), channel_id=1, source_target_pairs={{0,3},{1,0},{2,1},{3,2},{4,7},{5,4},{6,5},{7,6},{8,11},{9,8},{10,9... | collective-permute-start | bytes 61448 | tf_op jit(solution)/shard_map/ppermute | solution.py:339
  70.2 3.3 %collective-permute-start.12 = (f32[40,128]{1,0:T(8,128)S(1)}, f32[40,128]{1,0:T(8,128)S(1)}, u32[]{:S(2)}, u32[]{:S(2)}) collective-permute-start(f32[40,128]{1,0:T(8,128)S(1)} %get-tuple-element.130.own), channel_id=1, source_target_pairs={{0,1},{1,2},{2,3},{3,0},{4,5},{5,6},{6,7},{7,4},{8,9},{9,10},{10,1... | collective-permute-start | bytes 61448 | tf_op jit(solution)/shard_map/ppermute | solution.py:339
  70.4 3.8 %collective-permute-start.13 = (f32[40,128]{1,0:T(8,128)S(1)}, f32[40,128]{1,0:T(8,128)S(1)}, u32[]{:S(2)}, u32[]{:S(2)}) collective-permute-start(f32[40,128]{1,0:T(8,128)S(1)} %get-tuple-element.130.own), channel_id=1, source_target_pairs={{0,2},{1,3},{2,0},{3,1},{4,6},{5,7},{6,4},{7,5},{8,10},{9,11},{10,... | collective-permute-start | bytes 61448 | tf_op jit(solution)/shard_map/ppermute | solution.py:339
  71.5 2.9 %collective-permute-start.14 = (f32[40,128]{1,0:T(8,128)S(1)}, f32[40,128]{1,0:T(8,128)S(1)}, u32[]{:S(2)}, u32[]{:S(2)}) collective-permute-start(f32[40,128]{1,0:T(8,128)S(1)} %get-tuple-element.130.own), channel_id=1, source_target_pairs={{0,3},{1,0},{2,1},{3,2},{4,7},{5,4},{6,5},{7,6},{8,11},{9,8},{10,9... | collective-permute-start | bytes 61448 | tf_op jit(solution)/shard_map/ppermute | solution.py:339
  86.1 3.3 %collective-permute-start.15 = (f32[40,128]{1,0:T(8,128)S(1)}, f32[40,128]{1,0:T(8,128)S(1)}, u32[]{:S(2)}, u32[]{:S(2)}) collective-permute-start(f32[40,128]{1,0:T(8,128)S(1)} %get-tuple-element.138.own), channel_id=1, source_target_pairs={{0,1},{1,2},{2,3},{3,0},{4,5},{5,6},{6,7},{7,4},{8,9},{9,10},{10,1... | collective-permute-start | bytes 61448 | tf_op jit(solution)/shard_map/ppermute | solution.py:339
  86.2 3.9 %collective-permute-start.16 = (f32[40,128]{1,0:T(8,128)S(1)}, f32[40,128]{1,0:T(8,128)S(1)}, u32[]{:S(2)}, u32[]{:S(2)}) collective-permute-start(f32[40,128]{1,0:T(8,128)S(1)} %get-tuple-element.138.own), channel_id=1, source_target_pairs={{0,2},{1,3},{2,0},{3,1},{4,6},{5,7},{6,4},{7,5},{8,10},{9,11},{10,... | collective-permute-start | bytes 61448 | tf_op jit(solution)/shard_map/ppermute | solution.py:339
  87.1 3.0 %collective-permute-start.17 = (f32[40,128]{1,0:T(8,128)S(1)}, f32[40,128]{1,0:T(8,128)S(1)}, u32[]{:S(2)}, u32[]{:S(2)}) collective-permute-start(f32[40,128]{1,0:T(8,128)S(1)} %get-tuple-element.138.own), channel_id=1, source_target_pairs={{0,3},{1,0},{2,1},{3,2},{4,7},{5,4},{6,5},{7,6},{8,11},{9,8},{10,9... | collective-permute-start | bytes 61448 | tf_op jit(solution)/shard_map/ppermute | solution.py:339
  101.6 3.3 %collective-permute-start.18 = (f32[40,128]{1,0:T(8,128)S(1)}, f32[40,128]{1,0:T(8,128)S(1)}, u32[]{:S(2)}, u32[]{:S(2)}) collective-permute-start(f32[40,128]{1,0:T(8,128)S(1)} %get-tuple-element.146.own), channel_id=1, source_target_pairs={{0,1},{1,2},{2,3},{3,0},{4,5},{5,6},{6,7},{7,4},{8,9},{9,10},{10,1... | collective-permute-start | bytes 61448 | tf_op jit(solution)/shard_map/ppermute | solution.py:339
  101.8 3.8 %collective-permute-start.19 = (f32[40,128]{1,0:T(8,128)S(1)}, f32[40,128]{1,0:T(8,128)S(1)}, u32[]{:S(2)}, u32[]{:S(2)}) collective-permute-start(f32[40,128]{1,0:T(8,128)S(1)} %get-tuple-element.146.own), channel_id=1, source_target_pairs={{0,2},{1,3},{2,0},{3,1},{4,6},{5,7},{6,4},{7,5},{8,10},{9,11},{10,... | collective-permute-start | bytes 61448 | tf_op jit(solution)/shard_map/ppermute | solution.py:339
  103.0 2.9 %collective-permute-start.20 = (f32[40,128]{1,0:T(8,128)S(1)}, f32[40,128]{1,0:T(8,128)S(1)}, u32[]{:S(2)}, u32[]{:S(2)}) collective-permute-start(f32[40,128]{1,0:T(8,128)S(1)} %get-tuple-element.146.own), channel_id=1, source_target_pairs={{0,3},{1,0},{2,1},{3,2},{4,7},{5,4},{6,5},{7,6},{8,11},{9,8},{10,9... | collective-permute-start | bytes 61448 | tf_op jit(solution)/shard_map/ppermute | solution.py:339
  117.6 3.3 %collective-permute-start.21 = (f32[40,128]{1,0:T(8,128)S(1)}, f32[40,128]{1,0:T(8,128)S(1)}, u32[]{:S(2)}, u32[]{:S(2)}) collective-permute-start(f32[40,128]{1,0:T(8,128)S(1)} %get-tuple-element.154.own), channel_id=1, source_target_pairs={{0,1},{1,2},{2,3},{3,0},{4,5},{5,6},{6,7},{7,4},{8,9},{9,10},{10,1... | collective-permute-start | bytes 61448 | tf_op jit(solution)/shard_map/ppermute | solution.py:339
  117.6 3.9 %collective-permute-start.22 = (f32[40,128]{1,0:T(8,128)S(1)}, f32[40,128]{1,0:T(8,128)S(1)}, u32[]{:S(2)}, u32[]{:S(2)}) collective-permute-start(f32[40,128]{1,0:T(8,128)S(1)} %get-tuple-element.154.own), channel_id=1, source_target_pairs={{0,2},{1,3},{2,0},{3,1},{4,6},{5,7},{6,4},{7,5},{8,10},{9,11},{10,... | collective-permute-start | bytes 61448 | tf_op jit(solution)/shard_map/ppermute | solution.py:339
  118.5 3.0 %collective-permute-start.23 = (f32[40,128]{1,0:T(8,128)S(1)}, f32[40,128]{1,0:T(8,128)S(1)}, u32[]{:S(2)}, u32[]{:S(2)}) collective-permute-start(f32[40,128]{1,0:T(8,128)S(1)} %get-tuple-element.154.own), channel_id=1, source_target_pairs={{0,3},{1,0},{2,1},{3,2},{4,7},{5,4},{6,5},{7,6},{8,11},{9,8},{10,9... | collective-permute-start | bytes 61448 | tf_op jit(solution)/shard_map/ppermute | solution.py:339
  133.0 3.3 %collective-permute-start.24 = (f32[40,128]{1,0:T(8,128)S(1)}, f32[40,128]{1,0:T(8,128)S(1)}, u32[]{:S(2)}, u32[]{:S(2)}) collective-permute-start(f32[40,128]{1,0:T(8,128)S(1)} %get-tuple-element.162.own), channel_id=1, source_target_pairs={{0,1},{1,2},{2,3},{3,0},{4,5},{5,6},{6,7},{7,4},{8,9},{9,10},{10,1... | collective-permute-start | bytes 61448 | tf_op jit(solution)/shard_map/ppermute | solution.py:339
  133.2 3.8 %collective-permute-start.25 = (f32[40,128]{1,0:T(8,128)S(1)}, f32[40,128]{1,0:T(8,128)S(1)}, u32[]{:S(2)}, u32[]{:S(2)}) collective-permute-start(f32[40,128]{1,0:T(8,128)S(1)} %get-tuple-element.162.own), channel_id=1, source_target_pairs={{0,2},{1,3},{2,0},{3,1},{4,6},{5,7},{6,4},{7,5},{8,10},{9,11},{10,... | collective-permute-start | bytes 61448 | tf_op jit(solution)/shard_map/ppermute | solution.py:339
  134.4 2.9 %collective-permute-start.26 = (f32[40,128]{1,0:T(8,128)S(1)}, f32[40,128]{1,0:T(8,128)S(1)}, u32[]{:S(2)}, u32[]{:S(2)}) collective-permute-start(f32[40,128]{1,0:T(8,128)S(1)} %get-tuple-element.162.own), channel_id=1, source_target_pairs={{0,3},{1,0},{2,1},{3,2},{4,7},{5,4},{6,5},{7,6},{8,11},{9,8},{10,9... | collective-permute-start | bytes 61448 | tf_op jit(solution)/shard_map/ppermute | solution.py:339
  148.9 3.3 %collective-permute-start.27 = (f32[40,128]{1,0:T(8,128)S(1)}, f32[40,128]{1,0:T(8,128)S(1)}, u32[]{:S(2)}, u32[]{:S(2)}) collective-permute-start(f32[40,128]{1,0:T(8,128)S(1)} %get-tuple-element.170.own), channel_id=1, source_target_pairs={{0,1},{1,2},{2,3},{3,0},{4,5},{5,6},{6,7},{7,4},{8,9},{9,10},{10,1... | collective-permute-start | bytes 61448 | tf_op jit(solution)/shard_map/ppermute | solution.py:339
  149.0 3.9 %collective-permute-start.28 = (f32[40,128]{1,0:T(8,128)S(1)}, f32[40,128]{1,0:T(8,128)S(1)}, u32[]{:S(2)}, u32[]{:S(2)}) collective-permute-start(f32[40,128]{1,0:T(8,128)S(1)} %get-tuple-element.170.own), channel_id=1, source_target_pairs={{0,2},{1,3},{2,0},{3,1},{4,6},{5,7},{6,4},{7,5},{8,10},{9,11},{10,... | collective-permute-start | bytes 61448 | tf_op jit(solution)/shard_map/ppermute | solution.py:339
  149.9 3.0 %collective-permute-start.29 = (f32[40,128]{1,0:T(8,128)S(1)}, f32[40,128]{1,0:T(8,128)S(1)}, u32[]{:S(2)}, u32[]{:S(2)}) collective-permute-start(f32[40,128]{1,0:T(8,128)S(1)} %get-tuple-element.170.own), channel_id=1, source_target_pairs={{0,3},{1,0},{2,1},{3,2},{4,7},{5,4},{6,5},{7,6},{8,11},{9,8},{10,9... | collective-permute-start | bytes 61448 | tf_op jit(solution)/shard_map/ppermute | solution.py:339
  164.4 3.3 %collective-permute-start.30 = (f32[40,128]{1,0:T(8,128)S(1)}, f32[40,128]{1,0:T(8,128)S(1)}, u32[]{:S(2)}, u32[]{:S(2)}) collective-permute-start(f32[40,128]{1,0:T(8,128)S(1)} %get-tuple-element.178.own), channel_id=1, source_target_pairs={{0,1},{1,2},{2,3},{3,0},{4,5},{5,6},{6,7},{7,4},{8,9},{9,10},{10,1... | collective-permute-start | bytes 61448 | tf_op jit(solution)/shard_map/ppermute | solution.py:339
  164.6 3.8 %collective-permute-start.31 = (f32[40,128]{1,0:T(8,128)S(1)}, f32[40,128]{1,0:T(8,128)S(1)}, u32[]{:S(2)}, u32[]{:S(2)}) collective-permute-start(f32[40,128]{1,0:T(8,128)S(1)} %get-tuple-element.178.own), channel_id=1, source_target_pairs={{0,2},{1,3},{2,0},{3,1},{4,6},{5,7},{6,4},{7,5},{8,10},{9,11},{10,... | collective-permute-start | bytes 61448 | tf_op jit(solution)/shard_map/ppermute | solution.py:339
  165.8 2.9 %collective-permute-start.32 = (f32[40,128]{1,0:T(8,128)S(1)}, f32[40,128]{1,0:T(8,128)S(1)}, u32[]{:S(2)}, u32[]{:S(2)}) collective-permute-start(f32[40,128]{1,0:T(8,128)S(1)} %get-tuple-element.178.own), channel_id=1, source_target_pairs={{0,3},{1,0},{2,1},{3,2},{4,7},{5,4},{6,5},{7,6},{8,11},{9,8},{10,9... | collective-permute-start | bytes 61448 | tf_op jit(solution)/shard_map/ppermute | solution.py:339
  180.3 3.3 %collective-permute-start.33 = (f32[40,128]{1,0:T(8,128)S(1)}, f32[40,128]{1,0:T(8,128)S(1)}, u32[]{:S(2)}, u32[]{:S(2)}) collective-permute-start(f32[40,128]{1,0:T(8,128)S(1)} %get-tuple-element.186.own), channel_id=1, source_target_pairs={{0,1},{1,2},{2,3},{3,0},{4,5},{5,6},{6,7},{7,4},{8,9},{9,10},{10,1... | collective-permute-start | bytes 61448 | tf_op jit(solution)/shard_map/ppermute | solution.py:339
  180.4 3.9 %collective-permute-start.34 = (f32[40,128]{1,0:T(8,128)S(1)}, f32[40,128]{1,0:T(8,128)S(1)}, u32[]{:S(2)}, u32[]{:S(2)}) collective-permute-start(f32[40,128]{1,0:T(8,128)S(1)} %get-tuple-element.186.own), channel_id=1, source_target_pairs={{0,2},{1,3},{2,0},{3,1},{4,6},{5,7},{6,4},{7,5},{8,10},{9,11},{10,... | collective-permute-start | bytes 61448 | tf_op jit(solution)/shard_map/ppermute | solution.py:339
  181.3 3.0 %collective-permute-start.35 = (f32[40,128]{1,0:T(8,128)S(1)}, f32[40,128]{1,0:T(8,128)S(1)}, u32[]{:S(2)}, u32[]{:S(2)}) collective-permute-start(f32[40,128]{1,0:T(8,128)S(1)} %get-tuple-element.186.own), channel_id=1, source_target_pairs={{0,3},{1,0},{2,1},{3,2},{4,7},{5,4},{6,5},{7,6},{8,11},{9,8},{10,9... | collective-permute-start | bytes 61448 | tf_op jit(solution)/shard_map/ppermute | solution.py:339
  195.8 3.3 %collective-permute-start.36 = (f32[40,128]{1,0:T(8,128)S(1)}, f32[40,128]{1,0:T(8,128)S(1)}, u32[]{:S(2)}, u32[]{:S(2)}) collective-permute-start(f32[40,128]{1,0:T(8,128)S(1)} %get-tuple-element.194.own), channel_id=1, source_target_pairs={{0,1},{1,2},{2,3},{3,0},{4,5},{5,6},{6,7},{7,4},{8,9},{9,10},{10,1... | collective-permute-start | bytes 61448 | tf_op jit(solution)/shard_map/ppermute | solution.py:339
  196.0 3.8 %collective-permute-start.37 = (f32[40,128]{1,0:T(8,128)S(1)}, f32[40,128]{1,0:T(8,128)S(1)}, u32[]{:S(2)}, u32[]{:S(2)}) collective-permute-start(f32[40,128]{1,0:T(8,128)S(1)} %get-tuple-element.194.own), channel_id=1, source_target_pairs={{0,2},{1,3},{2,0},{3,1},{4,6},{5,7},{6,4},{7,5},{8,10},{9,11},{10,... | collective-permute-start | bytes 61448 | tf_op jit(solution)/shard_map/ppermute | solution.py:339
  197.2 2.9 %collective-permute-start.38 = (f32[40,128]{1,0:T(8,128)S(1)}, f32[40,128]{1,0:T(8,128)S(1)}, u32[]{:S(2)}, u32[]{:S(2)}) collective-permute-start(f32[40,128]{1,0:T(8,128)S(1)} %get-tuple-element.194.own), channel_id=1, source_target_pairs={{0,3},{1,0},{2,1},{3,2},{4,7},{5,4},{6,5},{7,6},{8,11},{9,8},{10,9... | collective-permute-start | bytes 61448 | tf_op jit(solution)/shard_map/ppermute | solution.py:339

commit v5 on v4

--- a/solution.py
+++ b/solution.py
@@ -31,6 +31,11 @@
     high = value.astype(jnp.bfloat16).astype(jnp.float32)
     middle = (value - high).astype(jnp.bfloat16).astype(jnp.float32)
     return high, middle, (value - high) - middle
+
+
+def partners(blocks):
+    assert blocks & (blocks - 1) == 0
+    return sorted(range(1, blocks), key=lambda mask: (mask != blocks // 2, mask))
 
 
 def copy_in(source, target, sem):
@@ -93,11 +98,6 @@
     )
 
 
-def publish(chunk, out):
-    for member in range(out.shape[0]):
-        out[member] = chunk
-
-
 def place_blocks(out, keep, columns, scalars):
     regions, per_dev = out.shape[0], columns.shape[0] // 3
     region = lax.axis_index("region")
@@ -137,13 +137,14 @@
 
 
 def diag_kernel(jac, vectors, picks, *refs):
-    ins, (out, weight, spots, lookup, fits, back) = refs[:-6], refs[-6:]
+    ins, refs = refs[:-7], refs[-7:]
+    out, keep, weight, spots, lookup, fits, back = refs
     tiles, slots, width, _ = jac.shape
     blocks = len(ins)
     per_dev = tiles // blocks
     group = lax.axis_index("blk")
-    for shift, part in enumerate(ins):
-        source = lax.rem(group + (blocks - shift), blocks)
+    for mask, part in zip([0] + partners(blocks), ins):
+        source = lax.bitwise_xor(group, mask)
         spot = pl.ds(pl.multiple_of(source * per_dev, per_dev), per_dev)
         weight[spot, :] = part[:per_dev, :]
         fits[spot, :] = part[per_dev:, :]
@@ -160,20 +161,17 @@
     column = lax.broadcasted_iota(jnp.int32, names.shape, 0)
     spots[...] = jnp.where(column == names, 1.0, 0.0).astype(jnp.bfloat16)
     squares = backward(jac, weight, picks, spots, back, True)
-    publish(jnp.concatenate([squares, vectors[...]], axis=0), out)
+    place_blocks(out, keep, squares, vectors[...])
 
 
 def back_kernel(jac, weight, picks, spots, own, *refs):
     others, (out, keep, weighted, back) = refs[:-4], refs[-4:]
     tiles, slots = jac.shape[:2]
-    parts = [own] + list(others)
-    even, odd = None, None
-    for shift, part in enumerate(parts):
-        if shift % 2 == 0:
-            even = part[...] if even is None else even + part[...]
-        else:
-            odd = part[...] if odd is None else odd + part[...]
-    total = even if odd is None else even + odd
+    parts = dict(zip([0] + partners(len(others) + 1), [own, *others]))
+    total = None
+    for mask in range(0, len(parts), 2):
+        pair = parts[mask][...] + parts[mask + 1][...]
+        total = pair if total is None else total + pair
     rows, sums = total[:tiles], total[tiles:]
     weighted[...] = weight[...] * rows
     delta = jnp.sum(weighted[...] * rows, axis=0, keepdims=True) + sums[1:2]
@@ -191,42 +189,6 @@
     delta = jnp.sum(d * z * z, axis=0, keepdims=True)
     pad = jnp.zeros((SUB - 2, z.shape[1]), jnp.float32)
     out[tiles:, :] = jnp.concatenate([gamma, delta, pad], axis=0)
-
-
-def gathered(received, region, regions, per_dev):
-    blocks = []
-    for offset in (-1, 0, 1):
-        total = None
-        for e in (-1, 0, 1):
-            source = lax.rem(region + (offset + e + regions), regions)
-            start = (1 - e) * per_dev
-            term = received[source, start : start + per_dev, :]
-            total = term if total is None else total + term
-        blocks.append(total)
-    return jnp.concatenate(blocks, axis=0)
-
-
-def halo(received, region, regions, start, per_dev):
-    blocks = []
-    for offset in (-1, 0, 1):
-        source = lax.rem(region + (offset + regions), regions)
-        blocks.append(received[source, start : start + per_dev, :])
-    return jnp.concatenate(blocks, axis=0)
-
-
-def first_kernel(jac, lookup, received, out, diag, precond, resid, picked):
-    regions = received.shape[0]
-    per_dev = diag.shape[0] // 3
-    region = lax.axis_index("region")
-    extent = 3 * per_dev
-    d = halo(received, region, regions, extent, per_dev)
-    r = halo(received, region, regions, extent + per_dev, per_dev)
-    m = d + gathered(received, region, regions, per_dev)
-    diag[...] = d
-    precond[...] = m
-    resid[...] = r
-    own = slice(per_dev, 2 * per_dev)
-    send_rows(jac, lookup, r, r / m, d, picked, own, out)
 
 
 def collected(received, kept, per_dev):
@@ -249,11 +211,37 @@
     return jnp.concatenate(blocks, axis=0)
 
 
+def first_kernel(jac, lookup, received, kept, out, diag, precond, resid, picked):
+    regions = received.shape[0]
+    per_dev = diag.shape[0] // 3
+    region = lax.axis_index("region")
+
+    def halo(place):
+        blocks = []
+        for offset in (-1, 0, 1):
+            if offset == 0:
+                start = (3 + place) * per_dev
+                blocks.append(kept[start : start + per_dev, :])
+            else:
+                source = lax.rem(region + (offset + regions), regions)
+                start = (2 + place) * per_dev
+                blocks.append(received[source, start : start + per_dev, :])
+        return jnp.concatenate(blocks, axis=0)
+
+    d, r = halo(0), halo(1)
+    inverse = 1.0 / (d + collected(received, kept, per_dev))
+    diag[...] = d
+    precond[...] = inverse
+    resid[...] = r
+    own = slice(per_dev, 2 * per_dev)
+    send_rows(jac, lookup, r, r * inverse, d, picked, own, out)
+
+
 def update(received, kept, diag, precond, resid, along, direct, answer, scal):
     regions = received.shape[0]
     per_dev = direct.shape[0]
-    r, d, m = resid[...], diag[...], precond[...]
-    z = r / m
+    r, d, inverse = resid[...], diag[...], precond[...]
+    z = r * inverse
     image = d * z + collected(received, kept, per_dev)
     region = lax.axis_index("region")
     sums = None
@@ -264,10 +252,8 @@
         sums = term if sums is None else sums + term
     sums = jnp.sum(sums, axis=1, keepdims=True)
     gamma, delta = sums[:1], sums[1:2]
-    before, alpha = scal[0:1, :1], scal[1:2, :1]
-    started = alpha != 0.0
-    beta = jnp.where(started, gamma / jnp.where(started, before, 1.0), 0.0)
-    fall = jnp.where(started, beta * gamma / jnp.where(started, alpha, 1.0), 0.0)
+    beta = gamma * scal[0:1, :1]
+    fall = beta * gamma * scal[1:2, :1]
     alpha = gamma / (delta - fall)
     s = image + beta * along[...]
     p = z[per_dev : 2 * per_dev] + beta * direct[...]
@@ -287,25 +273,35 @@
     along_o[...] = s
     direct_o[...] = p
     answer_o[...] = x
-    scal_o[0:1, :] = jnp.broadcast_to(gamma, (1, scal_o.shape[1]))
-    scal_o[1:2, :] = jnp.broadcast_to(alpha, (1, scal_o.shape[1]))
+    scal_o[0:1, :] = jnp.broadcast_to(1.0 / gamma, (1, scal_o.shape[1]))
+    scal_o[1:2, :] = jnp.broadcast_to(1.0 / alpha, (1, scal_o.shape[1]))
     own = slice(per_dev, 2 * per_dev)
-    send_rows(jac, lookup, r, r / precond[...], diag, picked, own, out)
+    send_rows(jac, lookup, r, r * precond[...], diag, picked, own, out)
 
 
 def last_kernel(
     received, kept, diag, precond, resid, along, direct, answer, scal, answer_o,
-    resid_o,
+    resid_o, values, sems,
 ):
     per_dev = direct.shape[0]
     x, r, _, _, _, _ = update(
         received, kept, diag, precond, resid, along, direct, answer, scal
     )
-    answer_o[...] = x
-    resid_o[...] = r[per_dev : 2 * per_dev]
-
-
-def call(kernel, outs, scratch, specs, name, flops, moved, limit=VMEM_LIMIT):
+    values[0] = x
+    values[1] = r[per_dev : 2 * per_dev]
+    copies = [
+        copy_in(values.at[n], target, sems.at[n])
+        for n, target in enumerate((answer_o, resid_o))
+    ]
+    for copy in copies:
+        copy.start()
+    for copy in copies:
+        copy.wait()
+
+
+def call(
+    kernel, outs, scratch, specs, name, flops, moved, limit=VMEM_LIMIT, target=vmem
+):
     outs = [
         shape
         if isinstance(shape, jax.ShapeDtypeStruct)
@@ -316,7 +312,7 @@
         kernel,
         out_shape=outs,
         in_specs=specs,
-        out_specs=[vmem] * len(outs),
+        out_specs=[target] * len(outs),
         scratch_shapes=scratch,
         compiler_params=pltpu.CompilerParams(vmem_limit_bytes=limit),
         cost_estimate=pl.CostEstimate(
@@ -336,8 +332,8 @@
 
     def across_blk(value):
         return [
-            lax.ppermute(value, "blk", [(i, (i + k) % blocks) for i in range(blocks)])
-            for k in range(1, blocks)
+            lax.ppermute(value, "blk", [(i, i ^ mask) for i in range(blocks)])
+            for mask in partners(blocks)
         ]
 
     def across_region(chunks):
@@ -369,10 +365,11 @@
         ],
         [pltpu.SemaphoreType.DMA((PIECES,))], [hbm], "load", flops, moved, LOAD_LIMIT,
     )(jac)
-    setup, weight, spots, lookup = call(
+    setup, kept, weight, spots, lookup = call(
         diag_kernel,
         [
-            (regions, extent + 2 * per_dev, width), (tiles, width),
+            (regions, 4 * per_dev, width), (extent + 2 * per_dev, width),
+            (tiles, width),
             jax.ShapeDtypeStruct((extent, 4 * tiles * slots), jnp.bfloat16),
             jax.ShapeDtypeStruct((slots, tiles, width), jnp.int32),
         ],
@@ -382,8 +379,8 @@
     setup = across_region(setup)
     out, diag, precond, resid = call(
         first_kernel, [(row_count, width), halo_shape, halo_shape, halo_shape],
-        [picked], [vmem] * 3, "first", flops, moved,
-    )(jac, lookup, setup)
+        [picked], [vmem] * 4, "first", flops, moved,
+    )(jac, lookup, setup, kept)
 
     def image_of(out):
         parts = across_blk(out)
@@ -410,7 +407,9 @@
         carry = step(carry)
     received, kept, resid, along, direct, answer, scal = carry
     answer, resid = call(
-        last_kernel, [own_shape, own_shape], [], [vmem] * 9, "last", 1000, 1000
+        last_kernel, [own_shape, own_shape],
+        [pltpu.VMEM((2, *own_shape), f32), pltpu.SemaphoreType.DMA((2,))],
+        [vmem] * 9, "last", 1000, 1000, VMEM_LIMIT, hbm,
     )(received, kept, diag, precond, resid, along, direct, answer, scal)
     return answer, resid
 

time: 212 us -> 211 us (level)
  waiting for transfers between devices: 18.8 us -> 26.3 us
  starting transfers between devices: 35.3 us -> 29.7 us
  blocking collectives: 135 us -> 131 us
    ppermute x39, waiting for transfers between devices: 18.8 us -> 26.3 us  [across_blk(): lax.ppermute(value, 'blk', [(i, i ^ mask) for i in range(blocks)])]
    ppermute x39, starting transfers between devices: 35.3 us -> 29.7 us  [across_blk(): lax.ppermute(value, 'blk', [(i, i ^ mask) for i in range(blocks)])]
    all_to_all x13, blocking collectives: 135 us -> 131 us  [across_region(): return lax.all_to_all(chunks, 'region', 0, 0, tiled=True)]
  transfers between devices with their start and end apart: 39 -> 39, of which waited for: 31 -> 25; matrix products, arithmetic and copies ran while one was open for 0% -> 0% of each run, Pallas kernels for 1% -> 1%
where the time goes in v5:
time: 211 us; the launch traced here: 210 us
  blocking collectives  131 us (62%)
  starting transfers between devices  29.7 us (14%)
  waiting for transfers between devices  26.3 us (12%)
  Pallas kernels  21.5 us (10%)
    all_to_all x13, blocking collectives, across_region(): return lax.all_to_all(chunks, 'region', 0, 0, tiled=True)  131 us
    ppermute x39, starting transfers between devices, across_blk(): lax.ppermute(value, 'blk', [(i, i ^ mask) for i in range(blocks)])  29.7 us
    ppermute x39, waiting for transfers between devices, across_blk(): lax.ppermute(value, 'blk', [(i, i ^ mask) for i in range(blocks)])  26.3 us
    pallas_call x11, Pallas kernels, step(): call(step_kernel, [(row_count, width), halo_shape, halo_shape, own_shape,...  8.79 us
    pallas_call x12, Pallas kernels, image_of(): call(back_kernel, [chunk, kept_shape], [pltpu.VMEM((tiles, width), f32),...  8.22 us
  transfers between devices with their start and end apart: 39, of which 25 were waited for; matrix products, arithmetic and copies ran while one was open for 0% of the time, Pallas kernels for 1%

profile of v5, /device:TPU:0, one launch (start us, length us, event | category | flops | bytes accessed | tf_op | source)
XLA Modules:
  0.0 210.1 jit_solution(14071456584090447484)
XLA Ops:
  1.4 3.0 %collective-permute-start = (f32[16,128]{1,0:T(8,128)S(1)}, f32[16,128]{1,0:T(8,128)S(1)}, u32[]{:S(2)}, u32[]{:S(2)}) collective-permute-start(f32[16,128]{1,0:T(8,128)S(1)} %get-tuple-element.204.refs_0_), channel_id=1, source_target_pairs={{0,2},{1,3},{2,0},{3,1},{4,6},{5,7},{6,4},{7,5},{8,10},{9,11},{10,... | collective-permute-start | bytes 24584 | tf_op jit(solution)/shard_map/ppermute | solution.py:335
  4.6 2.2 %load.1 = (f32[32,2,128,128]{3,2,1,0:T(8,128)S(1)}, bf16[16,128,256]{2,1,0:T(8,128)(2,1)S(1)}) custom-call(f32[32,2,128,128]{3,2,1,0:T(8,128)} %jac.1), custom_call_target="tpu_custom_call" | custom-call | flops 4194304 | bytes 4194304 | tf_op jit(solution)/shard_map/load/pallas_call | solution.py:360
  7.5 0.8 diagonal.1
  8.3 13.3 %all_to_all.65.received = f32[8,32,128]{2,1,0:T(8,128)S(1)} all-to-all(f32[8,32,128]{2,1,0:T(8,128)S(1)} %get-tuple-element.108), channel_id=1, replica_groups=mesh['region'=8,'blk'=4] {'region'}, dimensions={0} | all-to-all | bytes 262144 | tf_op jit(solution)/shard_map/all_to_all | solution.py:340
  22.2 1.1 collective-permute-start.3
  23.3 1.1 collective-permute-start.5
  24.4 1.6 collective-permute-done.3.refs_0_
  27.2 9.8 %all_to_all.66.received = f32[8,24,128]{2,1,0:T(8,128)S(1)} all-to-all(f32[8,24,128]{2,1,0:T(8,128)S(1)} %get-tuple-element.111), channel_id=1, replica_groups=mesh['region'=8,'blk'=4] {'region'}, dimensions={0} | all-to-all | bytes 196608 | tf_op jit(solution)/shard_map/all_to_all | solution.py:340
  37.0 0.8 step.11
  37.9 1.1 collective-permute-start.6
  38.9 1.1 collective-permute-start.8
  40.1 1.6 collective-permute-done.6.refs_0_
  42.8 9.8 %all_to_all.67.received = f32[8,24,128]{2,1,0:T(8,128)S(1)} all-to-all(f32[8,24,128]{2,1,0:T(8,128)S(1)} %get-tuple-element.117), channel_id=1, replica_groups=mesh['region'=8,'blk'=4] {'region'}, dimensions={0} | all-to-all | bytes 196608 | tf_op jit(solution)/shard_map/all_to_all | solution.py:340
  52.7 0.8 step.12
  53.5 1.1 collective-permute-start.11
  54.7 1.0 collective-permute-start.9
  55.7 1.1 collective-permute-done.11.refs_2_
  56.8 1.6 collective-permute-done.9.refs_0_
  59.1 9.5 %all_to_all.68.received = f32[8,24,128]{2,1,0:T(8,128)S(1)} all-to-all(f32[8,24,128]{2,1,0:T(8,128)S(1)} %get-tuple-element.125), channel_id=1, replica_groups=mesh['region'=8,'blk'=4] {'region'}, dimensions={0} | all-to-all | bytes 196608 | tf_op jit(solution)/shard_map/all_to_all | solution.py:340
  68.7 0.8 step.13
  69.5 1.1 collective-permute-start.12
  70.5 1.1 collective-permute-start.14
  71.7 1.6 collective-permute-done.12.refs_0_
  74.4 9.8 %all_to_all.69.received = f32[8,24,128]{2,1,0:T(8,128)S(1)} all-to-all(f32[8,24,128]{2,1,0:T(8,128)S(1)} %get-tuple-element.133), channel_id=1, replica_groups=mesh['region'=8,'blk'=4] {'region'}, dimensions={0} | all-to-all | bytes 196608 | tf_op jit(solution)/shard_map/all_to_all | solution.py:340
  84.3 0.8 step.14
  85.1 1.1 collective-permute-start.15
  86.1 1.1 collective-permute-start.17
  87.3 1.6 collective-permute-done.15.refs_0_
  90.0 9.8 %all_to_all.70.received = f32[8,24,128]{2,1,0:T(8,128)S(1)} all-to-all(f32[8,24,128]{2,1,0:T(8,128)S(1)} %get-tuple-element.141), channel_id=1, replica_groups=mesh['region'=8,'blk'=4] {'region'}, dimensions={0} | all-to-all | bytes 196608 | tf_op jit(solution)/shard_map/all_to_all | solution.py:340
  99.9 0.8 step.15
  100.7 1.1 collective-permute-start.18
  101.8 1.1 collective-permute-start.20
  102.9 1.6 collective-permute-done.18.refs_0_
  105.6 9.8 %all_to_all.71.received = f32[8,24,128]{2,1,0:T(8,128)S(1)} all-to-all(f32[8,24,128]{2,1,0:T(8,128)S(1)} %get-tuple-element.149), channel_id=1, replica_groups=mesh['region'=8,'blk'=4] {'region'}, dimensions={0} | all-to-all | bytes 196608 | tf_op jit(solution)/shard_map/all_to_all | solution.py:340
  115.5 0.8 step.16
  116.3 1.1 collective-permute-start.21
  117.4 1.1 collective-permute-start.23
  118.5 1.6 collective-permute-done.21.refs_0_
  121.3 9.8 %all_to_all.72.received = f32[8,24,128]{2,1,0:T(8,128)S(1)} all-to-all(f32[8,24,128]{2,1,0:T(8,128)S(1)} %get-tuple-element.157), channel_id=1, replica_groups=mesh['region'=8,'blk'=4] {'region'}, dimensions={0} | all-to-all | bytes 196608 | tf_op jit(solution)/shard_map/all_to_all | solution.py:340
  131.1 0.8 step.17
  131.9 1.1 collective-permute-start.24
  133.0 1.1 collective-permute-start.26
  134.1 1.6 collective-permute-done.24.refs_0_
  136.9 9.8 %all_to_all.73.received = f32[8,24,128]{2,1,0:T(8,128)S(1)} all-to-all(f32[8,24,128]{2,1,0:T(8,128)S(1)} %get-tuple-element.165), channel_id=1, replica_groups=mesh['region'=8,'blk'=4] {'region'}, dimensions={0} | all-to-all | bytes 196608 | tf_op jit(solution)/shard_map/all_to_all | solution.py:340
  146.7 0.8 step.18
  147.5 1.1 collective-permute-start.27
  148.6 1.1 collective-permute-start.29
  149.7 1.6 collective-permute-done.27.refs_0_
  152.5 9.9 %all_to_all.74.received = f32[8,24,128]{2,1,0:T(8,128)S(1)} all-to-all(f32[8,24,128]{2,1,0:T(8,128)S(1)} %get-tuple-element.173), channel_id=1, replica_groups=mesh['region'=8,'blk'=4] {'region'}, dimensions={0} | all-to-all | bytes 196608 | tf_op jit(solution)/shard_map/all_to_all | solution.py:340
  162.3 0.8 step.19
  163.1 1.1 collective-permute-start.30
  164.2 1.1 collective-permute-start.32
  165.4 1.6 collective-permute-done.30.refs_0_
  168.1 9.9 %all_to_all.75.received = f32[8,24,128]{2,1,0:T(8,128)S(1)} all-to-all(f32[8,24,128]{2,1,0:T(8,128)S(1)} %get-tuple-element.181), channel_id=1, replica_groups=mesh['region'=8,'blk'=4] {'region'}, dimensions={0} | all-to-all | bytes 196608 | tf_op jit(solution)/shard_map/all_to_all | solution.py:340
  178.0 0.8 step.20
  178.8 1.1 collective-permute-start.33
  179.8 1.1 collective-permute-start.35
  181.0 1.6 collective-permute-done.33.refs_0_
  183.7 9.8 %all_to_all.76.received = f32[8,24,128]{2,1,0:T(8,128)S(1)} all-to-all(f32[8,24,128]{2,1,0:T(8,128)S(1)} %get-tuple-element.189), channel_id=1, replica_groups=mesh['region'=8,'blk'=4] {'region'}, dimensions={0} | all-to-all | bytes 196608 | tf_op jit(solution)/shard_map/all_to_all | solution.py:340
  193.6 0.8 step.21
  194.4 1.1 collective-permute-start.36
  195.5 1.1 collective-permute-start.38
  196.6 1.6 collective-permute-done.36.refs_0_
  199.4 9.8 %all_to_all.77.received = f32[8,24,128]{2,1,0:T(8,128)S(1)} all-to-all(f32[8,24,128]{2,1,0:T(8,128)S(1)} %get-tuple-element.197), channel_id=1, replica_groups=mesh['region'=8,'blk'=4] {'region'}, dimensions={0} | all-to-all | bytes 196608 | tf_op jit(solution)/shard_map/all_to_all | solution.py:340
  (58 shorter events, 16.1 us)
Async XLA Ops:
  1.4 5.4 %collective-permute-start = (f32[16,128]{1,0:T(8,128)S(1)}, f32[16,128]{1,0:T(8,128)S(1)}, u32[]{:S(2)}, u32[]{:S(2)}) collective-permute-start(f32[16,128]{1,0:T(8,128)S(1)} %get-tuple-element.204.refs_0_), channel_id=1, source_target_pairs={{0,2},{1,3},{2,0},{3,1},{4,6},{5,7},{6,4},{7,5},{8,10},{9,11},{10,... | collective-permute-start | bytes 24584 | tf_op jit(solution)/shard_map/ppermute | solution.py:335
  4.4 2.4 %collective-permute-start.1 = (f32[16,128]{1,0:T(8,128)S(1)}, f32[16,128]{1,0:T(8,128)S(1)}, u32[]{:S(2)}, u32[]{:S(2)}) collective-permute-start(f32[16,128]{1,0:T(8,128)S(1)} %get-tuple-element.204.refs_0_), channel_id=1, source_target_pairs={{0,1},{1,0},{2,3},{3,2},{4,5},{5,4},{6,7},{7,6},{8,9},{9,8},{10,11... | collective-permute-start | bytes 24584 | tf_op jit(solution)/shard_map/ppermute | solution.py:335
  4.4 3.1 %collective-permute-start.2 = (f32[16,128]{1,0:T(8,128)S(1)}, f32[16,128]{1,0:T(8,128)S(1)}, u32[]{:S(2)}, u32[]{:S(2)}) collective-permute-start(f32[16,128]{1,0:T(8,128)S(1)} %get-tuple-element.204.refs_0_), channel_id=1, source_target_pairs={{0,3},{1,2},{2,1},{3,0},{4,7},{5,6},{6,5},{7,4},{8,11},{9,10},{10,... | collective-permute-start | bytes 24584 | tf_op jit(solution)/shard_map/ppermute | solution.py:335
  22.2 3.8 %collective-permute-start.3 = (f32[40,128]{1,0:T(8,128)S(1)}, f32[40,128]{1,0:T(8,128)S(1)}, u32[]{:S(2)}, u32[]{:S(2)}) collective-permute-start(f32[40,128]{1,0:T(8,128)S(1)} %get-tuple-element.110.own), channel_id=1, source_target_pairs={{0,2},{1,3},{2,0},{3,1},{4,6},{5,7},{6,4},{7,5},{8,10},{9,11},{10,... | collective-permute-start | bytes 61448 | tf_op jit(solution)/shard_map/ppermute | solution.py:335
  23.3 2.8 %collective-permute-start.4 = (f32[40,128]{1,0:T(8,128)S(1)}, f32[40,128]{1,0:T(8,128)S(1)}, u32[]{:S(2)}, u32[]{:S(2)}) collective-permute-start(f32[40,128]{1,0:T(8,128)S(1)} %get-tuple-element.110.own), channel_id=1, source_target_pairs={{0,1},{1,0},{2,3},{3,2},{4,5},{5,4},{6,7},{7,6},{8,9},{9,8},{10,11... | collective-permute-start | bytes 61448 | tf_op jit(solution)/shard_map/ppermute | solution.py:335
  23.3 3.2 %collective-permute-start.5 = (f32[40,128]{1,0:T(8,128)S(1)}, f32[40,128]{1,0:T(8,128)S(1)}, u32[]{:S(2)}, u32[]{:S(2)}) collective-permute-start(f32[40,128]{1,0:T(8,128)S(1)} %get-tuple-element.110.own), channel_id=1, source_target_pairs={{0,3},{1,2},{2,1},{3,0},{4,7},{5,6},{6,5},{7,4},{8,11},{9,10},{10,... | collective-permute-start | bytes 61448 | tf_op jit(solution)/shard_map/ppermute | solution.py:335
  37.9 3.8 %collective-permute-start.6 = (f32[40,128]{1,0:T(8,128)S(1)}, f32[40,128]{1,0:T(8,128)S(1)}, u32[]{:S(2)}, u32[]{:S(2)}) collective-permute-start(f32[40,128]{1,0:T(8,128)S(1)} %get-tuple-element.116.own), channel_id=1, source_target_pairs={{0,2},{1,3},{2,0},{3,1},{4,6},{5,7},{6,4},{7,5},{8,10},{9,11},{10,... | collective-permute-start | bytes 61448 | tf_op jit(solution)/shard_map/ppermute | solution.py:335
  38.9 2.8 %collective-permute-start.7 = (f32[40,128]{1,0:T(8,128)S(1)}, f32[40,128]{1,0:T(8,128)S(1)}, u32[]{:S(2)}, u32[]{:S(2)}) collective-permute-start(f32[40,128]{1,0:T(8,128)S(1)} %get-tuple-element.116.own), channel_id=1, source_target_pairs={{0,1},{1,0},{2,3},{3,2},{4,5},{5,4},{6,7},{7,6},{8,9},{9,8},{10,11... | collective-permute-start | bytes 61448 | tf_op jit(solution)/shard_map/ppermute | solution.py:335
  38.9 3.2 %collective-permute-start.8 = (f32[40,128]{1,0:T(8,128)S(1)}, f32[40,128]{1,0:T(8,128)S(1)}, u32[]{:S(2)}, u32[]{:S(2)}) collective-permute-start(f32[40,128]{1,0:T(8,128)S(1)} %get-tuple-element.116.own), channel_id=1, source_target_pairs={{0,3},{1,2},{2,1},{3,0},{4,7},{5,6},{6,5},{7,4},{8,11},{9,10},{10,... | collective-permute-start | bytes 61448 | tf_op jit(solution)/shard_map/ppermute | solution.py:335
  53.5 2.2 %collective-permute-start.10 = (f32[40,128]{1,0:T(8,128)S(1)}, f32[40,128]{1,0:T(8,128)S(1)}, u32[]{:S(2)}, u32[]{:S(2)}) collective-permute-start(f32[40,128]{1,0:T(8,128)S(1)} %get-tuple-element.124.own), channel_id=1, source_target_pairs={{0,1},{1,0},{2,3},{3,2},{4,5},{5,4},{6,7},{7,6},{8,9},{9,8},{10,11... | collective-permute-start | bytes 61448 | tf_op jit(solution)/shard_map/ppermute | solution.py:335
  53.5 3.3 %collective-permute-start.11 = (f32[40,128]{1,0:T(8,128)S(1)}, f32[40,128]{1,0:T(8,128)S(1)}, u32[]{:S(2)}, u32[]{:S(2)}) collective-permute-start(f32[40,128]{1,0:T(8,128)S(1)} %get-tuple-element.124.own), channel_id=1, source_target_pairs={{0,3},{1,2},{2,1},{3,0},{4,7},{5,6},{6,5},{7,4},{8,11},{9,10},{10,... | collective-permute-start | bytes 61448 | tf_op jit(solution)/shard_map/ppermute | solution.py:335
  54.7 3.8 %collective-permute-start.9 = (f32[40,128]{1,0:T(8,128)S(1)}, f32[40,128]{1,0:T(8,128)S(1)}, u32[]{:S(2)}, u32[]{:S(2)}) collective-permute-start(f32[40,128]{1,0:T(8,128)S(1)} %get-tuple-element.124.own), channel_id=1, source_target_pairs={{0,2},{1,3},{2,0},{3,1},{4,6},{5,7},{6,4},{7,5},{8,10},{9,11},{10,... | collective-permute-start | bytes 61448 | tf_op jit(solution)/shard_map/ppermute | solution.py:335
  69.5 3.8 %collective-permute-start.12 = (f32[40,128]{1,0:T(8,128)S(1)}, f32[40,128]{1,0:T(8,128)S(1)}, u32[]{:S(2)}, u32[]{:S(2)}) collective-permute-start(f32[40,128]{1,0:T(8,128)S(1)} %get-tuple-element.132.own), channel_id=1, source_target_pairs={{0,2},{1,3},{2,0},{3,1},{4,6},{5,7},{6,4},{7,5},{8,10},{9,11},{10,... | collective-permute-start | bytes 61448 | tf_op jit(solution)/shard_map/ppermute | solution.py:335
  70.5 2.8 %collective-permute-start.13 = (f32[40,128]{1,0:T(8,128)S(1)}, f32[40,128]{1,0:T(8,128)S(1)}, u32[]{:S(2)}, u32[]{:S(2)}) collective-permute-start(f32[40,128]{1,0:T(8,128)S(1)} %get-tuple-element.132.own), channel_id=1, source_target_pairs={{0,1},{1,0},{2,3},{3,2},{4,5},{5,4},{6,7},{7,6},{8,9},{9,8},{10,11... | collective-permute-start | bytes 61448 | tf_op jit(solution)/shard_map/ppermute | solution.py:335
  70.5 3.2 %collective-permute-start.14 = (f32[40,128]{1,0:T(8,128)S(1)}, f32[40,128]{1,0:T(8,128)S(1)}, u32[]{:S(2)}, u32[]{:S(2)}) collective-permute-start(f32[40,128]{1,0:T(8,128)S(1)} %get-tuple-element.132.own), channel_id=1, source_target_pairs={{0,3},{1,2},{2,1},{3,0},{4,7},{5,6},{6,5},{7,4},{8,11},{9,10},{10,... | collective-permute-start | bytes 61448 | tf_op jit(solution)/shard_map/ppermute | solution.py:335
  85.1 3.8 %collective-permute-start.15 = (f32[40,128]{1,0:T(8,128)S(1)}, f32[40,128]{1,0:T(8,128)S(1)}, u32[]{:S(2)}, u32[]{:S(2)}) collective-permute-start(f32[40,128]{1,0:T(8,128)S(1)} %get-tuple-element.140.own), channel_id=1, source_target_pairs={{0,2},{1,3},{2,0},{3,1},{4,6},{5,7},{6,4},{7,5},{8,10},{9,11},{10,... | collective-permute-start | bytes 61448 | tf_op jit(solution)/shard_map/ppermute | solution.py:335
  86.1 2.8 %collective-permute-start.16 = (f32[40,128]{1,0:T(8,128)S(1)}, f32[40,128]{1,0:T(8,128)S(1)}, u32[]{:S(2)}, u32[]{:S(2)}) collective-permute-start(f32[40,128]{1,0:T(8,128)S(1)} %get-tuple-element.140.own), channel_id=1, source_target_pairs={{0,1},{1,0},{2,3},{3,2},{4,5},{5,4},{6,7},{7,6},{8,9},{9,8},{10,11... | collective-permute-start | bytes 61448 | tf_op jit(solution)/shard_map/ppermute | solution.py:335
  86.1 3.2 %collective-permute-start.17 = (f32[40,128]{1,0:T(8,128)S(1)}, f32[40,128]{1,0:T(8,128)S(1)}, u32[]{:S(2)}, u32[]{:S(2)}) collective-permute-start(f32[40,128]{1,0:T(8,128)S(1)} %get-tuple-element.140.own), channel_id=1, source_target_pairs={{0,3},{1,2},{2,1},{3,0},{4,7},{5,6},{6,5},{7,4},{8,11},{9,10},{10,... | collective-permute-start | bytes 61448 | tf_op jit(solution)/shard_map/ppermute | solution.py:335
  100.7 3.8 %collective-permute-start.18 = (f32[40,128]{1,0:T(8,128)S(1)}, f32[40,128]{1,0:T(8,128)S(1)}, u32[]{:S(2)}, u32[]{:S(2)}) collective-permute-start(f32[40,128]{1,0:T(8,128)S(1)} %get-tuple-element.148.own), channel_id=1, source_target_pairs={{0,2},{1,3},{2,0},{3,1},{4,6},{5,7},{6,4},{7,5},{8,10},{9,11},{10,... | collective-permute-start | bytes 61448 | tf_op jit(solution)/shard_map/ppermute | solution.py:335
  101.8 2.8 %collective-permute-start.19 = (f32[40,128]{1,0:T(8,128)S(1)}, f32[40,128]{1,0:T(8,128)S(1)}, u32[]{:S(2)}, u32[]{:S(2)}) collective-permute-start(f32[40,128]{1,0:T(8,128)S(1)} %get-tuple-element.148.own), channel_id=1, source_target_pairs={{0,1},{1,0},{2,3},{3,2},{4,5},{5,4},{6,7},{7,6},{8,9},{9,8},{10,11... | collective-permute-start | bytes 61448 | tf_op jit(solution)/shard_map/ppermute | solution.py:335
  101.8 3.2 %collective-permute-start.20 = (f32[40,128]{1,0:T(8,128)S(1)}, f32[40,128]{1,0:T(8,128)S(1)}, u32[]{:S(2)}, u32[]{:S(2)}) collective-permute-start(f32[40,128]{1,0:T(8,128)S(1)} %get-tuple-element.148.own), channel_id=1, source_target_pairs={{0,3},{1,2},{2,1},{3,0},{4,7},{5,6},{6,5},{7,4},{8,11},{9,10},{10,... | collective-permute-start | bytes 61448 | tf_op jit(solution)/shard_map/ppermute | solution.py:335
  116.3 3.8 %collective-permute-start.21 = (f32[40,128]{1,0:T(8,128)S(1)}, f32[40,128]{1,0:T(8,128)S(1)}, u32[]{:S(2)}, u32[]{:S(2)}) collective-permute-start(f32[40,128]{1,0:T(8,128)S(1)} %get-tuple-element.156.own), channel_id=1, source_target_pairs={{0,2},{1,3},{2,0},{3,1},{4,6},{5,7},{6,4},{7,5},{8,10},{9,11},{10,... | collective-permute-start | bytes 61448 | tf_op jit(solution)/shard_map/ppermute | solution.py:335
  117.4 2.8 %collective-permute-start.22 = (f32[40,128]{1,0:T(8,128)S(1)}, f32[40,128]{1,0:T(8,128)S(1)}, u32[]{:S(2)}, u32[]{:S(2)}) collective-permute-start(f32[40,128]{1,0:T(8,128)S(1)} %get-tuple-element.156.own), channel_id=1, source_target_pairs={{0,1},{1,0},{2,3},{3,2},{4,5},{5,4},{6,7},{7,6},{8,9},{9,8},{10,11... | collective-permute-start | bytes 61448 | tf_op jit(solution)/shard_map/ppermute | solution.py:335
  117.4 3.2 %collective-permute-start.23 = (f32[40,128]{1,0:T(8,128)S(1)}, f32[40,128]{1,0:T(8,128)S(1)}, u32[]{:S(2)}, u32[]{:S(2)}) collective-permute-start(f32[40,128]{1,0:T(8,128)S(1)} %get-tuple-element.156.own), channel_id=1, source_target_pairs={{0,3},{1,2},{2,1},{3,0},{4,7},{5,6},{6,5},{7,4},{8,11},{9,10},{10,... | collective-permute-start | bytes 61448 | tf_op jit(solution)/shard_map/ppermute | solution.py:335
  131.9 3.8 %collective-permute-start.24 = (f32[40,128]{1,0:T(8,128)S(1)}, f32[40,128]{1,0:T(8,128)S(1)}, u32[]{:S(2)}, u32[]{:S(2)}) collective-permute-start(f32[40,128]{1,0:T(8,128)S(1)} %get-tuple-element.164.own), channel_id=1, source_target_pairs={{0,2},{1,3},{2,0},{3,1},{4,6},{5,7},{6,4},{7,5},{8,10},{9,11},{10,... | collective-permute-start | bytes 61448 | tf_op jit(solution)/shard_map/ppermute | solution.py:335
  133.0 2.8 %collective-permute-start.25 = (f32[40,128]{1,0:T(8,128)S(1)}, f32[40,128]{1,0:T(8,128)S(1)}, u32[]{:S(2)}, u32[]{:S(2)}) collective-permute-start(f32[40,128]{1,0:T(8,128)S(1)} %get-tuple-element.164.own), channel_id=1, source_target_pairs={{0,1},{1,0},{2,3},{3,2},{4,5},{5,4},{6,7},{7,6},{8,9},{9,8},{10,11... | collective-permute-start | bytes 61448 | tf_op jit(solution)/shard_map/ppermute | solution.py:335
  133.0 3.2 %collective-permute-start.26 = (f32[40,128]{1,0:T(8,128)S(1)}, f32[40,128]{1,0:T(8,128)S(1)}, u32[]{:S(2)}, u32[]{:S(2)}) collective-permute-start(f32[40,128]{1,0:T(8,128)S(1)} %get-tuple-element.164.own), channel_id=1, source_target_pairs={{0,3},{1,2},{2,1},{3,0},{4,7},{5,6},{6,5},{7,4},{8,11},{9,10},{10,... | collective-permute-start | bytes 61448 | tf_op jit(solution)/shard_map/ppermute | solution.py:335
  147.5 3.8 %collective-permute-start.27 = (f32[40,128]{1,0:T(8,128)S(1)}, f32[40,128]{1,0:T(8,128)S(1)}, u32[]{:S(2)}, u32[]{:S(2)}) collective-permute-start(f32[40,128]{1,0:T(8,128)S(1)} %get-tuple-element.172.own), channel_id=1, source_target_pairs={{0,2},{1,3},{2,0},{3,1},{4,6},{5,7},{6,4},{7,5},{8,10},{9,11},{10,... | collective-permute-start | bytes 61448 | tf_op jit(solution)/shard_map/ppermute | solution.py:335
  148.6 2.8 %collective-permute-start.28 = (f32[40,128]{1,0:T(8,128)S(1)}, f32[40,128]{1,0:T(8,128)S(1)}, u32[]{:S(2)}, u32[]{:S(2)}) collective-permute-start(f32[40,128]{1,0:T(8,128)S(1)} %get-tuple-element.172.own), channel_id=1, source_target_pairs={{0,1},{1,0},{2,3},{3,2},{4,5},{5,4},{6,7},{7,6},{8,9},{9,8},{10,11... | collective-permute-start | bytes 61448 | tf_op jit(solution)/shard_map/ppermute | solution.py:335
  148.6 3.2 %collective-permute-start.29 = (f32[40,128]{1,0:T(8,128)S(1)}, f32[40,128]{1,0:T(8,128)S(1)}, u32[]{:S(2)}, u32[]{:S(2)}) collective-permute-start(f32[40,128]{1,0:T(8,128)S(1)} %get-tuple-element.172.own), channel_id=1, source_target_pairs={{0,3},{1,2},{2,1},{3,0},{4,7},{5,6},{6,5},{7,4},{8,11},{9,10},{10,... | collective-permute-start | bytes 61448 | tf_op jit(solution)/shard_map/ppermute | solution.py:335
  163.1 3.8 %collective-permute-start.30 = (f32[40,128]{1,0:T(8,128)S(1)}, f32[40,128]{1,0:T(8,128)S(1)}, u32[]{:S(2)}, u32[]{:S(2)}) collective-permute-start(f32[40,128]{1,0:T(8,128)S(1)} %get-tuple-element.180.own), channel_id=1, source_target_pairs={{0,2},{1,3},{2,0},{3,1},{4,6},{5,7},{6,4},{7,5},{8,10},{9,11},{10,... | collective-permute-start | bytes 61448 | tf_op jit(solution)/shard_map/ppermute | solution.py:335
  164.2 2.8 %collective-permute-start.31 = (f32[40,128]{1,0:T(8,128)S(1)}, f32[40,128]{1,0:T(8,128)S(1)}, u32[]{:S(2)}, u32[]{:S(2)}) collective-permute-start(f32[40,128]{1,0:T(8,128)S(1)} %get-tuple-element.180.own), channel_id=1, source_target_pairs={{0,1},{1,0},{2,3},{3,2},{4,5},{5,4},{6,7},{7,6},{8,9},{9,8},{10,11... | collective-permute-start | bytes 61448 | tf_op jit(solution)/shard_map/ppermute | solution.py:335
  164.2 3.2 %collective-permute-start.32 = (f32[40,128]{1,0:T(8,128)S(1)}, f32[40,128]{1,0:T(8,128)S(1)}, u32[]{:S(2)}, u32[]{:S(2)}) collective-permute-start(f32[40,128]{1,0:T(8,128)S(1)} %get-tuple-element.180.own), channel_id=1, source_target_pairs={{0,3},{1,2},{2,1},{3,0},{4,7},{5,6},{6,5},{7,4},{8,11},{9,10},{10,... | collective-permute-start | bytes 61448 | tf_op jit(solution)/shard_map/ppermute | solution.py:335
  178.8 3.8 %collective-permute-start.33 = (f32[40,128]{1,0:T(8,128)S(1)}, f32[40,128]{1,0:T(8,128)S(1)}, u32[]{:S(2)}, u32[]{:S(2)}) collective-permute-start(f32[40,128]{1,0:T(8,128)S(1)} %get-tuple-element.188.own), channel_id=1, source_target_pairs={{0,2},{1,3},{2,0},{3,1},{4,6},{5,7},{6,4},{7,5},{8,10},{9,11},{10,... | collective-permute-start | bytes 61448 | tf_op jit(solution)/shard_map/ppermute | solution.py:335
  179.8 2.8 %collective-permute-start.34 = (f32[40,128]{1,0:T(8,128)S(1)}, f32[40,128]{1,0:T(8,128)S(1)}, u32[]{:S(2)}, u32[]{:S(2)}) collective-permute-start(f32[40,128]{1,0:T(8,128)S(1)} %get-tuple-element.188.own), channel_id=1, source_target_pairs={{0,1},{1,0},{2,3},{3,2},{4,5},{5,4},{6,7},{7,6},{8,9},{9,8},{10,11... | collective-permute-start | bytes 61448 | tf_op jit(solution)/shard_map/ppermute | solution.py:335
  179.8 3.2 %collective-permute-start.35 = (f32[40,128]{1,0:T(8,128)S(1)}, f32[40,128]{1,0:T(8,128)S(1)}, u32[]{:S(2)}, u32[]{:S(2)}) collective-permute-start(f32[40,128]{1,0:T(8,128)S(1)} %get-tuple-element.188.own), channel_id=1, source_target_pairs={{0,3},{1,2},{2,1},{3,0},{4,7},{5,6},{6,5},{7,4},{8,11},{9,10},{10,... | collective-permute-start | bytes 61448 | tf_op jit(solution)/shard_map/ppermute | solution.py:335
  194.4 3.8 %collective-permute-start.36 = (f32[40,128]{1,0:T(8,128)S(1)}, f32[40,128]{1,0:T(8,128)S(1)}, u32[]{:S(2)}, u32[]{:S(2)}) collective-permute-start(f32[40,128]{1,0:T(8,128)S(1)} %get-tuple-element.196.own), channel_id=1, source_target_pairs={{0,2},{1,3},{2,0},{3,1},{4,6},{5,7},{6,4},{7,5},{8,10},{9,11},{10,... | collective-permute-start | bytes 61448 | tf_op jit(solution)/shard_map/ppermute | solution.py:335
  195.5 2.8 %collective-permute-start.37 = (f32[40,128]{1,0:T(8,128)S(1)}, f32[40,128]{1,0:T(8,128)S(1)}, u32[]{:S(2)}, u32[]{:S(2)}) collective-permute-start(f32[40,128]{1,0:T(8,128)S(1)} %get-tuple-element.196.own), channel_id=1, source_target_pairs={{0,1},{1,0},{2,3},{3,2},{4,5},{5,4},{6,7},{7,6},{8,9},{9,8},{10,11... | collective-permute-start | bytes 61448 | tf_op jit(solution)/shard_map/ppermute | solution.py:335
  195.5 3.2 %collective-permute-start.38 = (f32[40,128]{1,0:T(8,128)S(1)}, f32[40,128]{1,0:T(8,128)S(1)}, u32[]{:S(2)}, u32[]{:S(2)}) collective-permute-start(f32[40,128]{1,0:T(8,128)S(1)} %get-tuple-element.196.own), channel_id=1, source_target_pairs={{0,3},{1,2},{2,1},{3,0},{4,7},{5,6},{6,5},{7,4},{8,11},{9,10},{10,... | collective-permute-start | bytes 61448 | tf_op jit(solution)/shard_map/ppermute | solution.py:335
